TPU v7x, 32 devices: a whole 2x2x4 slice. The times are simulated.
32 devices in a mesh: gx: 8 (over z, x), gy: 4 (over y, core).
Axes of the slice: x: 2, y: 2, z: 4, core: 2. Of those that a mesh axis runs over, the one named last changes fastest.
Arguments:
- state: float32 [65536, 128], P(('gx', 'gy')), may hold values from 0 to 1
- velocity: bfloat16 [3, 3, 128, 64, 128], P(None, None, 'gx', 'gy'), may hold values from -3 to 3
- cells: int32 [3, 3, 65536], P(None, None, ('gx', 'gy')), may hold values from -1 to 126, as said below
- slots: int32 [3, 65536], P(None, ('gx', 'gy')), may hold values from 0 to 2047, as said below
- counts: int32 [3, 8, 4, 8], P(None, 'gx', 'gy'), may hold values from 0 to 64, as said below
Outputs:
- final_state: float32 [65536, 128], P(('gx', 'gy'))
Inputs may be any that keep to these rules, and one draw needn't show every extreme that they name: For every section and device the 2048 values of slots are a permutation of 0 to 2047. counts[s, i, j, r] equals counts[s, i', j', r xor 1] where (i', j') is the neighbour of (i, j) in direction r; some device sends exactly 64 in every section. cells[s, 0] lies in -1 to 15, cells[s, 1] in -1 to 15, cells[s, 2] in 0 to 126.
All inputs are finite; a program needn't handle non-finite values.
Results may differ from a plain program's by a relative error of at most 0.0003.
Values may be sent and summed in bfloat16 or wider, within the bound.
No kernel may reach another device: no remote copies, remote signals or barrier semaphores. Data moves between devices by JAX's collectives and lax.ppermute only.
A program may use at most 64 MiB of HBM per device.

v0:
```python
import functools

import jax
import jax.numpy as jnp
from jax import lax
from jax.experimental import pallas as pl
from jax.experimental.pallas import tpu as pltpu
from jax.sharding import PartitionSpec as P


CAP = 64
DIRS = 8
GAMMA = (8.0 / 15.0, 5.0 / 12.0, 3.0 / 4.0)
ZETA = (0.0, -17.0 / 60.0, -5.0 / 12.0)
SEGMENTS = (0, 4, 6, 1, 5, 7, 2, 3)
FROM_XP = (1, None, None)
FROM_XM = (0, None, None)
FROM_YP = (3, 5, 6)
FROM_YM = (2, 7, 4)
SPARE = 8
UNROLL = 16
VMEM_BYTES = 16 * 2**20
LANES = 256


def shifted(x, axis, by):
    size = lax.axis_size(axis)
    return lax.ppermute(x, axis, [(i, (i + by) % size) for i in range(size)])


def scatter_rows(state_ref, target_ref, arrivals):
    for ref, dirs in arrivals:
        for place, d in enumerate(dirs):
            if d is None:
                continue

            def body(t, carry, ref=ref, place=place, d=d):
                slot = target_ref[d * CAP + t]
                state_ref[pl.ds(slot, 1), :] = ref[pl.ds(place * CAP + t, 1), :]
                return carry

            lax.fori_loop(0, CAP, body, 0, unroll=UNROLL)


def gather_rows(slot_ref, *pairs):
    def body(t, carry):
        slot = slot_ref[t]
        for out_ref, from_ref in pairs:
            out_ref[pl.ds(t, 1), :] = from_ref[pl.ds(slot, 1), :]
        return carry

    lax.fori_loop(0, slot_ref.shape[0], body, 0, unroll=UNROLL)


def hat(base, frac, length):
    steps = lax.broadcasted_iota(jnp.int32, (length, base.shape[1]), 0) - base
    return jnp.where(steps == 0, 1.0 - frac, jnp.where(steps == 1, frac, 0.0))


def split_wide(value):
    high = value.astype(jnp.bfloat16)
    return high, value - high.astype(jnp.float32)


def split(weight):
    high = weight.astype(jnp.bfloat16)
    return high, (weight - high.astype(jnp.float32)).astype(jnp.bfloat16)


def advanced(section, turned, cell, plane, rim, widths):
    width_x, width_y, depth = widths
    lanes = cell.shape[1]
    frac, before = turned[0:3], turned[3:6]
    cx, cy, cz = cell[0:1], cell[1:2], cell[2:3]
    fx, fy, fz = frac[0:1], frac[1:2], frac[2:3]
    wx = hat(cx, fx, width_x)
    wy = hat(cy, fy, width_y)
    wz = hat(cz, fz, depth)
    x_low = jnp.where(cx == -1, 1.0 - fx, 0.0)
    x_high = jnp.where(cx == width_x - 1, fx, 0.0)
    y_low = jnp.where(cy == -1, 1.0 - fy, 0.0)
    y_high = jnp.where(cy == width_y - 1, fy, 0.0)
    inner = (wx[:, None, :] * wy[None, :, :]).reshape(width_x * width_y, lanes)
    corners = [x_low * y_low, x_high * y_low, x_low * y_high, x_high * y_high]
    pad = rim.shape[1] // 2 - 2 * (width_x + width_y) - 4
    edge = jnp.concatenate(
        [x_low * wy, x_high * wy, y_low * wx, y_high * wx, *corners, jnp.zeros((pad, lanes), jnp.float32)], axis=0
    )
    high, low = split(inner)
    columns = jnp.dot(plane, high, preferred_element_type=jnp.float32)
    columns += jnp.dot(plane, low, preferred_element_type=jnp.float32)
    columns += jnp.dot(rim, jnp.concatenate(split(edge), axis=0), preferred_element_type=jnp.float32)
    speed = jnp.concatenate(
        [jnp.sum(columns[k * depth : (k + 1) * depth] * wz, axis=0, keepdims=True) for k in range(3)], axis=0
    )
    moved = frac + GAMMA[section] * speed + ZETA[section] * before
    return jnp.concatenate([moved, speed, jnp.zeros((2, lanes), jnp.float32)], axis=0)


def turn_rim(section, halo, out_ref):
    low_x, high_x, low_y, high_y = halo
    width_x, width_y, depth = low_y.shape[2] - 2, low_x.shape[2], low_x.shape[3]
    pad = out_ref.shape[1] // 2 - 2 * (width_x + width_y)
    spot = lax.broadcasted_iota(jnp.int32, (pad, depth), 0)
    for k in range(3):
        corners = jnp.zeros((pad, depth), jnp.float32)
        for n, (ref, row) in enumerate(
            ((low_y, width_x), (low_y, width_x + 1), (high_y, width_x), (high_y, width_x + 1))
        ):
            value = ref[section, k, row : row + 1, :].astype(jnp.float32)
            corners = jnp.where(spot == n, value, corners)
        rim = jnp.concatenate(
            [
                low_x[section, k],
                high_x[section, k],
                low_y[section, k, 0:width_x, :],
                high_y[section, k, 0:width_x, :],
                corners.astype(out_ref.dtype),
            ],
            axis=0,
        )
        turned = rim.T
        out_ref[k * depth : (k + 1) * depth, :] = jnp.concatenate([turned, turned], axis=1)


def turn_plane(velocity_ref, section, out_ref):
    width_x, width_y, depth = velocity_ref.shape[2:]
    for k in range(3):
        plane = velocity_ref[section, k].reshape(width_x * width_y, depth)
        out_ref[k * depth : (k + 1) * depth, :] = plane.T


def fetch(*refs):
    sources, (state_ref, velocity_ref, cells_ref) = refs[:5], refs[5:8]
    low_ref, high_ref, plane_ref, rows_ref, leave_ref, arrive_ref, target_ref = refs[8:15]
    slots_ref, counts_ref, sems = refs[15:]
    copies = [
        pltpu.make_async_copy(src, dst, sems.at[n])
        for n, (src, dst) in enumerate(
            zip(sources, (velocity_ref, slots_ref, counts_ref, cells_ref, state_ref))
        )
    ]
    for copy in copies:
        copy.start()
    sections, parts, count = cells_ref.shape
    width_y = velocity_ref.shape[3]
    leaving = leave_ref.shape[2]

    copies[1].wait()
    copies[2].wait()
    place = lax.broadcasted_iota(jnp.int32, (DIRS, leaving), 1)
    start = lax.broadcasted_iota(jnp.int32, (DIRS, leaving), 0) * CAP
    spread = jnp.where((place >= start) & (place < start + CAP), 1.0, 0.0)
    tally = jnp.concatenate(
        [counts_ref[s, 0].astype(jnp.float32) for s in range(sections)]
        + [jnp.zeros((-sections % 8, DIRS), jnp.float32)],
        axis=0,
    )
    limit = jnp.dot(tally, spread, preferred_element_type=jnp.float32).astype(jnp.int32)
    within = lax.broadcasted_iota(jnp.int32, (1, leaving), 1) % CAP
    for s in range(sections):
        order = slots_ref[s : s + 1, 0:leaving]
        target = jnp.where(within < limit[s : s + 1], order, count)
        target_ref[s] = target
        leave_ref[s] = jnp.concatenate([order[:, d * CAP : (d + 1) * CAP] for d in SEGMENTS], axis=1)
        arrive_ref[s] = jnp.concatenate(
            [target[:, d * CAP : (d + 1) * CAP] for d in FROM_YP + FROM_YM], axis=1
        )
    copies[0].wait()
    for s in range(sections):
        for k in range(3):
            block = velocity_ref[s, k].astype(jnp.float32)
            low_ref[s, k] = block[:, 0, :].astype(low_ref.dtype)
            high_ref[s, k] = block[:, width_y - 1, :].astype(low_ref.dtype)
    turn_plane(velocity_ref, 0, plane_ref)
    copies[3].wait()
    flat = jnp.concatenate(
        [cells_ref[s].astype(jnp.float32) for s in range(sections)]
        + [jnp.zeros((-sections * parts % 8, count), jnp.float32)],
        axis=0,
    )
    rows_ref[:, 0 : flat.shape[0]] = flat.T
    copies[4].wait()


def own_cells(section, part_ref, cell_ref):
    parts = cell_ref.shape[0]
    cell_ref[...] = part_ref[...].T[section * parts : (section + 1) * parts].astype(jnp.int32)


def first(slot_ref, rows_ref, state_ref, left_ref, cell_ref, part_ref):
    gather_rows(slot_ref, (left_ref, state_ref), (part_ref, rows_ref))
    own_cells(0, part_ref, cell_ref)


def depart(section, widths, *refs):
    left_ref, cell_ref, plane_ref = refs[:3]
    leaving = left_ref.shape[0]
    if section == 0:
        halo, turned_ref, outs = refs[3:7], refs[7], refs[8:]
        turn_rim(section, halo, turned_ref)
        rows = left_ref[...]
    else:
        turned_ref, pick_ref, c_ref, d_ref = refs[3:7]
        outs = refs[7:]
        arrived = jnp.concatenate([c_ref[...], d_ref[...]], axis=0)
        high, rest = split_wide(arrived)
        middle, low = split(rest)
        rows = left_ref[...]
        for part in (high, middle, low):
            rows += jnp.dot(pick_ref[...], part, preferred_element_type=jnp.float32)
    fresh = []
    for start in range(0, leaving, LANES):
        stop = start + LANES
        cell = cell_ref[:, start:stop]
        new = advanced(section, rows[start:stop].T, cell, plane_ref[...], turned_ref[...], widths)
        fresh.append(new.T[:, 0:6])
    start = 0
    for ref in outs:
        stop = start + ref.shape[0]
        ref[...] = rows[start:stop]
        for n, part in enumerate(fresh):
            low, high = max(start, n * LANES), min(stop, (n + 1) * LANES)
            if low < high:
                ref[low - start : high - start, 0:6] = part[low - n * LANES : high - n * LANES]
        start = stop


def advance(section, widths, more, *refs):
    if section:
        target_ref, c_ref, d_ref, *refs = refs
    cells_ref, plane_ref, turned_ref, state_ref, *refs = refs
    if more:
        velocity_ref, *halo, out_ref, next_plane_ref, next_ref = refs
    else:
        (out_ref,) = refs
    if section:
        out_ref[...] = state_ref[...]
        scatter_rows(out_ref, target_ref, ((c_ref, FROM_YP), (d_ref, FROM_YM)))
        state_ref = out_ref
    count = cells_ref.shape[2]
    for start in range(0, count, LANES):
        rows = state_ref[start : start + LANES, :]
        cell = cells_ref[section, :, start : start + LANES]
        new = advanced(section, rows.T, cell, plane_ref[...], turned_ref[...], widths)
        if section == 0:
            out_ref[start : start + LANES, :] = rows
        out_ref[start : start + LANES, 0:6] = new.T[:, 0:6]
    if more:
        turn_plane(velocity_ref, section + 1, next_plane_ref)
        turn_rim(section + 1, halo, next_ref)


def settle(section, more, target_ref, *refs):
    if more:
        slot_ref, old_ref, a_ref, b_ref, rows_ref, leave_ref, arrive_ref = refs[:7]
        state_ref, left_ref, cell_ref, pick_ref, part_ref = refs[7:]
    else:
        old_ref, a_ref, b_ref, state_ref = refs
    state_ref[0 : old_ref.shape[0], :] = old_ref[...]
    scatter_rows(state_ref, target_ref, ((a_ref, FROM_XP), (b_ref, FROM_XM)))
    if more:
        leaving = left_ref.shape[0]
        gather_rows(slot_ref, (left_ref, state_ref), (part_ref, rows_ref))
        own_cells(section + 1, part_ref, cell_ref)
        leave = jnp.broadcast_to(leave_ref[section + 1].astype(jnp.float32), (8, leaving)).T[:, 0:1]
        pick = jnp.where(leave == arrive_ref[section].astype(jnp.float32), 1.0, 0.0)
        pick_ref[...] = pick.astype(pick_ref.dtype)
        left_ref[...] = jnp.where(jnp.max(pick, axis=1, keepdims=True) > 0.0, 0.0, left_ref[...])


def finish(target_ref, old_ref, c_ref, d_ref, out_ref, work_ref):
    count = out_ref.shape[0]
    work_ref[...] = old_ref[...]
    scatter_rows(work_ref, target_ref, ((c_ref, FROM_YP), (d_ref, FROM_YM)))
    out_ref[...] = work_ref[0:count, :]


def local(state, velocity, cells, slots, counts):
    sections = velocity.shape[0]
    width_x, width_y, depth = widths = velocity.shape[2:]
    count, columns = state.shape
    leaving = DIRS * CAP
    coming = CAP * (len(FROM_YP) + len(FROM_YM))
    vmem = pl.BlockSpec(memory_space=pltpu.VMEM)
    smem = pl.BlockSpec(memory_space=pltpu.SMEM)
    hbm = pl.BlockSpec(memory_space=pltpu.HBM)
    params = pltpu.CompilerParams(vmem_limit_bytes=VMEM_BYTES)

    def shape(*dims, dtype=jnp.float32):
        return jax.ShapeDtypeStruct(dims, dtype)

    def call(body, operands, scalars, outs, scratch=(), specs=None):
        single = len(outs) == 1
        return pl.pallas_call(
            body,
            out_shape=outs[0] if single else outs,
            in_specs=specs or [smem] * scalars + [vmem] * (len(operands) - scalars),
            out_specs=vmem if single else [vmem] * len(outs),
            scratch_shapes=scratch,
            compiler_params=params,
        )(*operands)

    plane_shape = shape(3 * depth, width_x * width_y, dtype=velocity.dtype)
    edge_shape = shape(sections, 3, width_x, depth, dtype=velocity.dtype)
    cell_shape = shape(3, leaving, dtype=jnp.int32)
    gathered = pltpu.VMEM((leaving, columns), jnp.float32)

    low_x = shifted(velocity[:, :, width_x - 1], "gx", 1)
    high_x = shifted(velocity[:, :, 0], "gx", -1)
    sources = (velocity, slots, counts, cells, state)
    state, velocity, cells, bottom, top, plane, rows, leave, arrive, target = call(
        fetch,
        [pltpu.with_memory_space_constraint(x, pltpu.HBM) for x in sources],
        0,
        [
            shape(*state.shape),
            shape(*velocity.shape, dtype=velocity.dtype),
            shape(*cells.shape, dtype=cells.dtype),
            edge_shape,
            edge_shape,
            plane_shape,
            shape(count, columns),
            shape(sections, 1, leaving, dtype=jnp.int32),
            shape(sections, 1, coming, dtype=jnp.int32),
            shape(sections, 1, leaving, dtype=jnp.int32),
        ],
        [
            pltpu.VMEM(slots.shape, slots.dtype),
            pltpu.VMEM(counts.shape, counts.dtype),
            pltpu.SemaphoreType.DMA((5,)),
        ],
        [hbm] * 5,
    )
    low_y = shifted(
        jnp.concatenate([top, low_x[:, :, width_y - 1 :], high_x[:, :, width_y - 1 :]], axis=2),
        "gy",
        1,
    )
    high_y = shifted(jnp.concatenate([bottom, low_x[:, :, :1], high_x[:, :, :1]], axis=2), "gy", -1)
    halo = [low_x, high_x, low_y, high_y]
    used = 2 * (width_x + width_y) + 4
    turned_shape = shape(3 * depth, 2 * (used + -used % 16), dtype=velocity.dtype)
    targets = [target[section].reshape(leaving) for section in range(sections)]
    slot = [leave[section].reshape(leaving) for section in range(sections)]

    left, cell = call(
        first, [slot[0], rows, state], 1, [shape(leaving, columns), cell_shape], [gathered]
    )
    messages = [shape(3 * CAP, columns)] * 2 + [shape(CAP, columns)] * 2
    for section in range(sections):
        more = section + 1 < sections
        body = functools.partial(depart, section, widths)
        if section == 0:
            turned, *sent = call(body, [left, cell, plane, *halo], 0, [turned_shape, *messages])
        else:
            sent = call(
                body, [left, cell, plane, turned, pick, from_low_y, from_high_y], 0, messages
            )
        xp, xm, yp, ym = sent
        from_low_x = shifted(xp, "gx", 1)
        from_high_x = shifted(xm, "gx", -1)
        out = call(
            functools.partial(advance, section, widths, more),
            ([targets[section - 1], from_low_y, from_high_y] if section else [])
            + [cells, plane, turned, state]
            + ([velocity, *halo] if more else []),
            1 if section else 0,
            [shape(count + SPARE if section else count, columns)]
            + ([plane_shape, turned_shape] if more else []),
        )
        state, plane, turned = out if more else (out, None, None)
        from_low_y = shifted(
            jnp.concatenate([yp, from_low_x[CAP : 2 * CAP], from_high_x[2 * CAP :]], axis=0),
            "gy",
            1,
        )
        from_high_y = shifted(
            jnp.concatenate([ym, from_low_x[2 * CAP :], from_high_x[CAP : 2 * CAP]], axis=0),
            "gy",
            -1,
        )
        out = call(
            functools.partial(settle, section, more),
            [targets[section]]
            + ([slot[section + 1]] if more else [])
            + [state, from_low_x, from_high_x]
            + ([rows, leave, arrive] if more else []),
            2 if more else 1,
            [shape(count + SPARE, columns)]
            + (
                [shape(leaving, columns), cell_shape, shape(leaving, coming, dtype=jnp.bfloat16)]
                if more
                else []
            ),
            [gathered] if more else [],
        )
        state, left, cell, pick = out if more else (out, None, None, None)
    return call(
        finish,
        [targets[sections - 1], state, from_low_y, from_high_y],
        1,
        [shape(count, columns)],
        [pltpu.VMEM((count + SPARE, columns), jnp.float32)],
    )


def solution(mesh):
    return jax.shard_map(
        local,
        mesh=mesh,
        in_specs=(
            P(("gx", "gy"), None),
            P(None, None, "gx", "gy", None),
            P(None, None, ("gx", "gy")),
            P(None, ("gx", "gy")),
            P(None, "gx", "gy", None),
        ),
        out_specs=P(("gx", "gy"), None),
        check_vma=False,
    )
```

profile of v0, /device:TPU:1, one launch (start us, length us, event | category | flops | bytes accessed | tf_op | source)
XLA Modules:
  0.0 63.1 jit_solution(5528260691601234055)
XLA Ops:
  0.0 0.8 %slice_bitcast_fusion = (bf16[3,3,16,128]{3,2,1,0:T(8,128)(2,1)S(1)}, bf16[3,3,16,128]{3,2,1,0:T(8,128)(2,1)S(1)}) fusion(bf16[3,3,16,16,128]{4,3,2,1,0:T(8,128)(2,1)} %refs_0_.1), kind=kLoop, calls=%fused_computation.8 | loop fusion | bytes 147456 | tf_op jit(solution)/shard_map/squeeze | solution.py:310
  0.8 5.1 %collective-permute-start.1 = (bf16[3,3,16,128]{3,2,1,0:T(8,128)(2,1)S(1)}, bf16[3,3,16,128]{3,2,1,0:T(8,128)(2,1)S(1)}, u32[]{:S(2)}, u32[]{:S(2)}) collective-permute-start(bf16[3,3,16,128]{3,2,1,0:T(8,128)(2,1)S(1)} %get-tuple-element.83), channel_id=1, source_target_pairs={{0,28},{4,0},{8,4},{12,8},{16,12},{20,16},{24,20},{28,24},{1,29},{... | collective-permute-start | bytes 110600 | tf_op jit(solution)/shard_map/ppermute | solution.py:28
  5.9 1.7 %shard_map.55 = (f32[2048,128]{1,0:T(8,128)S(1)}, bf16[3,3,16,16,128]{4,3,2,1,0:T(8,128)(2,1)S(1)}, s32[3,3,2048]{2,1,0:T(4,128)S(1)}, bf16[3,3,16,128]{3,2,1,0:...) custom-call(bf16[3,3,16,16,128]{4,3,2,1,0:T(8,128)(2,1)} %refs_0_.1,, ...), custom_call_target="tpu_custom_call" | custom-call | tf_op jit(solution)/shard_map/pallas_call | solution.py:295
  7.6 3.7 %collective-permute-done.refs_3_.refs_5_.refs_8_ = bf16[3,3,16,128]{3,2,1,0:T(8,128)(2,1)S(1)} collective-permute-done((bf16[3,3,16,128]{3,2,1,0:T(8,128)(2,1)S(1)}, bf16[3,3,16,128]{3,2,1,0:T(8,128)(2,1)S(1)}, u32[]{:S(2)}, u32[]{:S(2)}) %collective-permute-start) | collective-permute-done | bytes 36896 | tf_op jit(solution)/shard_map/ppermute | solution.py:28
  11.4 3.3 %collective-permute-start.2 = (bf16[3,3,18,128]{3,2,1,0:T(8,128)(2,1)S(1)}, bf16[3,3,18,128]{3,2,1,0:T(8,128)(2,1)S(1)}, u32[]{:S(2)}, u32[]{:S(2)}) collective-permute-start(bf16[3,3,18,128]{3,2,1,0:T(8,128)(2,1)S(1)} %pad_maximum_fusion.6), channel_id=1, source_target_pairs={{0,1},{1,2},{2,3},{3,0},{4,5},{5,6},{6,7},{7,4},{8,9},{9,10},{10,1... | collective-permute-start | bytes 124424 | tf_op jit(solution)/shard_map/ppermute | solution.py:28
  14.8 1.4 %shard_map.56 = (f32[512,128]{1,0:T(8,128)S(1)}, s32[3,512]{1,0:T(4,128)S(1)}) custom-call(s32[512]{0:T(512)S(1)} %bitcast.20, f32[2048,128]{1,0:T(8,128)S(1)} %get-tuple-element.48.rows_ref.refs_4_, f32[2048,128]{1,0:T(8,128)S(1)} %get-tuple-element.49.state_ref.refs_3_), custom_call_target="tpu_custom_call" | custom-call | tf_op jit(solution)/shard_map/pallas_call | solution.py:295
  16.2 2.2 %collective-permute-done.3.refs_6_.refs_8_.refs_11_ = bf16[3,3,18,128]{3,2,1,0:T(8,128)(2,1)S(1)} collective-permute-done((bf16[3,3,18,128]{3,2,1,0:T(8,128)(2,1)S(1)}, bf16[3,3,18,128]{3,2,1,0:T(8,128)(2,1)S(1)}, u32[]{:S(2)}, u32[]{:S(2)}) %collective-permute-start.3) | collective-permute-done | bytes 41504 | tf_op jit(solution)/shard_map/ppermute | solution.py:28
  18.3 0.7 %shard_map.57 = (bf16[384,160]{1,0:T(8,128)(2,1)S(1)}, f32[192,128]{1,0:T(8,128)S(1)}, f32[192,128]{1,0:T(8,128)S(1)}, f32[64,128]{1,0:T(8,128)S(1)}, f32[64,128]{1,0:T(8,128)S(1)}) custom-call(f32[512,128]{1,0:T(8,128)S(1)} %get-tuple-element.50.refs_0_, s32[3,512]{1,0:T(4,128)S(1)} %get-tuple-element.51.refs_1_, ...), custom_call_target="tpu_custom_call" | custom-call | tf_op jit(solution)/shard_map/pallas_call | solution.py:295
  19.1 1.5 %collective-permute-start.4 = (f32[192,128]{1,0:T(8,128)S(1)}, f32[192,128]{1,0:T(8,128)S(1)}, u32[]{:S(2)}, u32[]{:S(2)}) collective-permute-start(f32[192,128]{1,0:T(8,128)S(1)} %get-tuple-element.57), channel_id=1, source_target_pairs={{0,4},{4,8},{8,12},{12,16},{16,20},{20,24},{24,28},{28,0},{1,5},{5... | collective-permute-start | bytes 294920 | tf_op jit(solution)/shard_map/ppermute | solution.py:28
  20.6 2.4 %collective-permute-done.5.refs_3_ = f32[192,128]{1,0:T(8,128)S(1)} collective-permute-done((f32[192,128]{1,0:T(8,128)S(1)}, f32[192,128]{1,0:T(8,128)S(1)}, u32[]{:S(2)}, u32[]{:S(2)}) %collective-permute-start.5) | collective-permute-done | bytes 98336 | tf_op jit(solution)/shard_map/ppermute | solution.py:28
  22.9 2.8 %collective-permute-done.4.refs_2_ = f32[192,128]{1,0:T(8,128)S(1)} collective-permute-done((f32[192,128]{1,0:T(8,128)S(1)}, f32[192,128]{1,0:T(8,128)S(1)}, u32[]{:S(2)}, u32[]{:S(2)}) %collective-permute-start.4) | collective-permute-done | bytes 98336 | tf_op jit(solution)/shard_map/ppermute | solution.py:28
  25.7 1.5 %collective-permute-start.6 = (f32[192,128]{1,0:T(8,128)S(1)}, f32[192,128]{1,0:T(8,128)S(1)}, u32[]{:S(2)}, u32[]{:S(2)}) collective-permute-start(f32[192,128]{1,0:T(8,128)S(1)} %pad_maximum_fusion), channel_id=1, source_target_pairs={{0,1},{1,2},{2,3},{3,0},{4,5},{5,6},{6,7},{7,4},{8,9},{9,10},{10,1... | collective-permute-start | bytes 294920 | tf_op jit(solution)/shard_map/ppermute | solution.py:28
  27.3 1.7 %shard_map.58 = (f32[2048,128]{1,0:T(8,128)S(1)}, bf16[384,256]{1,0:T(8,128)(2,1)S(1)}, bf16[384,160]{1,0:T(8,128)(2,1)S(1)}) custom-call(s32[3,3,2048]{2,1,0:T(4,128)S(1)} %get-tuple-element.46.refs_0_.refs_3_, bf16[384,256]{1,0:T(8,128)(2,1)S(1)} %get-tuple-element.47.refs_2_.refs_1_, bf16[384,160]{1,0:T(8,128)(2,1)S(1)} %get-tuple-element.54.refs_2_, ...), custom_call_target="tpu_custom_call" | custom-call | tf_op jit(solution)/shard_map/pallas_call | solution.py:295
  29.0 1.9 %shard_map.59 = (f32[2056,128]{1,0:T(8,128)S(1)}, f32[512,128]{1,0:T(8,128)S(1)}, s32[3,512]{1,0:T(4,128)S(1)}, bf16[512,384]{1,0:T(8,128)(2,1)S(1)}) custom-call(s32[512]{0:T(512)S(1)} %bitcast.18, s32[512]{0:T(512)S(1)} %bitcast.22, f32[2048,128]{1,0:T(8,128)S(1)} %get-tuple-element.56.refs_1_, f32[192,128]{1,0:T(8,128)S(1)} %collective-permute-done.4.refs_2_, ...), custom_call_target="tpu_custom_call" | custom-call | tf_op jit(solution)/shard_map/pallas_call | solution.py:295
  31.0 0.4 collective-permute-done.7.refs_6_.refs_2_
  31.4 1.1 %shard_map.60 = (f32[192,128]{1,0:T(8,128)S(1)}, f32[192,128]{1,0:T(8,128)S(1)}, f32[64,128]{1,0:T(8,128)S(1)}, f32[64,128]{1,0:T(8,128)S(1)}) custom-call(f32[512,128]{1,0:T(8,128)S(1)} %get-tuple-element.60.refs_0_, s32[3,512]{1,0:T(4,128)S(1)} %get-tuple-element.61.refs_1_, bf16[384,256]{1,0:T(8,128)(2,1)S(1)} %get-tuple-element.62.refs_2_.refs_4_, ...), custom_call_target="tpu_custom_call" | custom-call | tf_op jit(solution)/shard_map/pallas_call | solution.py:295
  32.6 1.5 %collective-permute-start.8 = (f32[192,128]{1,0:T(8,128)S(1)}, f32[192,128]{1,0:T(8,128)S(1)}, u32[]{:S(2)}, u32[]{:S(2)}) collective-permute-start(f32[192,128]{1,0:T(8,128)S(1)} %get-tuple-element.68), channel_id=1, source_target_pairs={{0,4},{4,8},{8,12},{12,16},{16,20},{20,24},{24,28},{28,0},{1,5},{5... | collective-permute-start | bytes 294920 | tf_op jit(solution)/shard_map/ppermute | solution.py:28
  34.0 3.0 %collective-permute-done.9.refs_3_ = f32[192,128]{1,0:T(8,128)S(1)} collective-permute-done((f32[192,128]{1,0:T(8,128)S(1)}, f32[192,128]{1,0:T(8,128)S(1)}, u32[]{:S(2)}, u32[]{:S(2)}) %collective-permute-start.9) | collective-permute-done | bytes 98336 | tf_op jit(solution)/shard_map/ppermute | solution.py:28
  37.0 2.8 %collective-permute-done.8.refs_2_ = f32[192,128]{1,0:T(8,128)S(1)} collective-permute-done((f32[192,128]{1,0:T(8,128)S(1)}, f32[192,128]{1,0:T(8,128)S(1)}, u32[]{:S(2)}, u32[]{:S(2)}) %collective-permute-start.8) | collective-permute-done | bytes 98336 | tf_op jit(solution)/shard_map/ppermute | solution.py:28
  39.8 1.7 %collective-permute-start.10 = (f32[192,128]{1,0:T(8,128)S(1)}, f32[192,128]{1,0:T(8,128)S(1)}, u32[]{:S(2)}, u32[]{:S(2)}) collective-permute-start(f32[192,128]{1,0:T(8,128)S(1)} %pad_maximum_fusion.2), channel_id=1, source_target_pairs={{0,1},{1,2},{2,3},{3,0},{4,5},{5,6},{6,7},{7,4},{8,9},{9,10},{10,1... | collective-permute-start | bytes 294920 | tf_op jit(solution)/shard_map/ppermute | solution.py:28
  41.6 2.9 %shard_map.61 = (f32[2056,128]{1,0:T(8,128)S(1)}, bf16[384,256]{1,0:T(8,128)(2,1)S(1)}, bf16[384,160]{1,0:T(8,128)(2,1)S(1)}) custom-call(s32[512]{0:T(512)S(1)} %bitcast.19, f32[192,128]{1,0:T(8,128)S(1)} %collective-permute-done.6.refs_5_.refs_1_, f32[192,128]{1,0:T(8,128)S(1)} %collective-permute-done.7.refs_6_.refs_2_, ...), custom_call_target="tpu_custom_call" | custom-call | tf_op jit(solution)/shard_map/pallas_call | solution.py:295
  44.5 1.9 %shard_map.62 = (f32[2056,128]{1,0:T(8,128)S(1)}, f32[512,128]{1,0:T(8,128)S(1)}, s32[3,512]{1,0:T(4,128)S(1)}, bf16[512,384]{1,0:T(8,128)(2,1)S(1)}) custom-call(s32[512]{0:T(512)S(1)} %bitcast.14, s32[512]{0:T(512)S(1)} %bitcast.21, f32[2056,128]{1,0:T(8,128)S(1)} %get-tuple-element.74.refs_1_, f32[192,128]{1,0:T(8,128)S(1)} %collective-permute-done.8.refs_2_, ...), custom_call_target="tpu_custom_call" | custom-call | tf_op jit(solution)/shard_map/pallas_call | solution.py:295
  46.5 1.1 %shard_map.64 = (f32[192,128]{1,0:T(8,128)S(1)}, f32[192,128]{1,0:T(8,128)S(1)}, f32[64,128]{1,0:T(8,128)S(1)}, f32[64,128]{1,0:T(8,128)S(1)}) custom-call(f32[512,128]{1,0:T(8,128)S(1)} %get-tuple-element.76.refs_0_, s32[3,512]{1,0:T(4,128)S(1)} %get-tuple-element.77.refs_1_, bf16[384,256]{1,0:T(8,128)(2,1)S(1)} %get-tuple-element.72.refs_4_.refs_2_, ...), custom_call_target="tpu_custom_call" | custom-call | tf_op jit(solution)/shard_map/pallas_call | solution.py:295
  47.6 0.1 collective-permute-start.13
  47.7 1.5 %collective-permute-start.12 = (f32[192,128]{1,0:T(8,128)S(1)}, f32[192,128]{1,0:T(8,128)S(1)}, u32[]{:S(2)}, u32[]{:S(2)}) collective-permute-start(f32[192,128]{1,0:T(8,128)S(1)} %get-tuple-element.79), channel_id=1, source_target_pairs={{0,4},{4,8},{8,12},{12,16},{16,20},{20,24},{24,28},{28,0},{1,5},{5... | collective-permute-start | bytes 294920 | tf_op jit(solution)/shard_map/ppermute | solution.py:28
  49.1 2.0 %collective-permute-done.13.refs_2_ = f32[192,128]{1,0:T(8,128)S(1)} collective-permute-done((f32[192,128]{1,0:T(8,128)S(1)}, f32[192,128]{1,0:T(8,128)S(1)}, u32[]{:S(2)}, u32[]{:S(2)}) %collective-permute-start.13) | collective-permute-done | bytes 98336 | tf_op jit(solution)/shard_map/ppermute | solution.py:28
  51.1 2.8 %collective-permute-done.12.refs_1_ = f32[192,128]{1,0:T(8,128)S(1)} collective-permute-done((f32[192,128]{1,0:T(8,128)S(1)}, f32[192,128]{1,0:T(8,128)S(1)}, u32[]{:S(2)}, u32[]{:S(2)}) %collective-permute-start.12) | collective-permute-done | bytes 98336 | tf_op jit(solution)/shard_map/ppermute | solution.py:28
  53.9 2.9 %collective-permute-start.14 = (f32[192,128]{1,0:T(8,128)S(1)}, f32[192,128]{1,0:T(8,128)S(1)}, u32[]{:S(2)}, u32[]{:S(2)}) collective-permute-start(f32[192,128]{1,0:T(8,128)S(1)} %pad_maximum_fusion.4), channel_id=1, source_target_pairs={{0,1},{1,2},{2,3},{3,0},{4,5},{5,6},{6,7},{7,4},{8,9},{9,10},{10,1... | collective-permute-start | bytes 294920 | tf_op jit(solution)/shard_map/ppermute | solution.py:28
  56.9 2.9 %shard_map.63.refs_0_ = f32[2056,128]{1,0:T(8,128)S(1)} custom-call(s32[512]{0:T(512)S(1)} %bitcast.15, f32[192,128]{1,0:T(8,128)S(1)} %collective-permute-done.10.refs_1_.refs_5_, f32[192,128]{1,0:T(8,128)S(1)} %collective-permute-done.11.refs_2_.refs_6_, s32[3,3,2048]{2,1,0:T(4,128)S(1)} %get-tuple-element.46.refs_0_.refs_3_, ...), custom_call_target="tpu_custom_call" | custom-call | tf_op jit(solution)/shard_map/pallas_call | solution.py:295
  59.8 0.8 %shard_map.65.old_ref = f32[2056,128]{1,0:T(8,128)S(1)} custom-call(s32[512]{0:T(512)S(1)} %bitcast.16, f32[2056,128]{1,0:T(8,128)S(1)} %shard_map.63.refs_0_, f32[192,128]{1,0:T(8,128)S(1)} %collective-permute-done.12.refs_1_, f32[192,128]{1,0:T(8,128)S(1)} %collective-permute-done.13.refs_2_), custom_call_target="tpu_custom_call" | custom-call | tf_op jit(solution)/shard_map/pallas_call | solution.py:295
  60.6 0.3 collective-permute-done.15.d_ref
  60.9 2.2 %shard_map.66 = f32[2048,128]{1,0:T(8,128)} custom-call(s32[512]{0:T(512)S(1)} %bitcast.17, f32[2056,128]{1,0:T(8,128)S(1)} %shard_map.65.old_ref, f32[192,128]{1,0:T(8,128)S(1)} %collective-permute-done.14.c_ref, f32[192,128]{1,0:T(8,128)S(1)} %collective-permute-done.15.d_ref), custom_call_target="tpu_custom_call" | custom-call | tf_op jit(solution)/shard_map/pallas_call | solution.py:295
  (31 shorter events, 0.5 us)
Async XLA Ops:
  0.8 6.8 %collective-permute-start.1 = (bf16[3,3,16,128]{3,2,1,0:T(8,128)(2,1)S(1)}, bf16[3,3,16,128]{3,2,1,0:T(8,128)(2,1)S(1)}, u32[]{:S(2)}, u32[]{:S(2)}) collective-permute-start(bf16[3,3,16,128]{3,2,1,0:T(8,128)(2,1)S(1)} %get-tuple-element.83), channel_id=1, source_target_pairs={{0,28},{4,0},{8,4},{12,8},{16,12},{20,16},{24,20},{28,24},{1,29},{... | collective-permute-start | bytes 110600 | tf_op jit(solution)/shard_map/ppermute | solution.py:28
  5.9 5.5 %collective-permute-start = (bf16[3,3,16,128]{3,2,1,0:T(8,128)(2,1)S(1)}, bf16[3,3,16,128]{3,2,1,0:T(8,128)(2,1)S(1)}, u32[]{:S(2)}, u32[]{:S(2)}) collective-permute-start(bf16[3,3,16,128]{3,2,1,0:T(8,128)(2,1)S(1)} %get-tuple-element.84), channel_id=1, source_target_pairs={{0,4},{4,8},{8,12},{12,16},{16,20},{20,24},{24,28},{28,0},{1,5},{5... | collective-permute-start | bytes 110600 | tf_op jit(solution)/shard_map/ppermute | solution.py:28
  11.4 4.8 %collective-permute-start.2 = (bf16[3,3,18,128]{3,2,1,0:T(8,128)(2,1)S(1)}, bf16[3,3,18,128]{3,2,1,0:T(8,128)(2,1)S(1)}, u32[]{:S(2)}, u32[]{:S(2)}) collective-permute-start(bf16[3,3,18,128]{3,2,1,0:T(8,128)(2,1)S(1)} %pad_maximum_fusion.6), channel_id=1, source_target_pairs={{0,1},{1,2},{2,3},{3,0},{4,5},{5,6},{6,7},{7,4},{8,9},{9,10},{10,1... | collective-permute-start | bytes 124424 | tf_op jit(solution)/shard_map/ppermute | solution.py:28
  14.7 3.6 %collective-permute-start.3 = (bf16[3,3,18,128]{3,2,1,0:T(8,128)(2,1)S(1)}, bf16[3,3,18,128]{3,2,1,0:T(8,128)(2,1)S(1)}, u32[]{:S(2)}, u32[]{:S(2)}) collective-permute-start(bf16[3,3,18,128]{3,2,1,0:T(8,128)(2,1)S(1)} %pad_maximum_fusion.7), channel_id=1, source_target_pairs={{0,3},{1,0},{2,1},{3,2},{4,7},{5,4},{6,5},{7,6},{8,11},{9,8},{10,9... | collective-permute-start | bytes 124424 | tf_op jit(solution)/shard_map/ppermute | solution.py:28
  19.1 3.9 %collective-permute-start.5 = (f32[192,128]{1,0:T(8,128)S(1)}, f32[192,128]{1,0:T(8,128)S(1)}, u32[]{:S(2)}, u32[]{:S(2)}) collective-permute-start(f32[192,128]{1,0:T(8,128)S(1)} %get-tuple-element.58), channel_id=1, source_target_pairs={{0,28},{4,0},{8,4},{12,8},{16,12},{20,16},{24,20},{28,24},{1,29},{... | collective-permute-start | bytes 294920 | tf_op jit(solution)/shard_map/ppermute | solution.py:28
  19.1 6.6 %collective-permute-start.4 = (f32[192,128]{1,0:T(8,128)S(1)}, f32[192,128]{1,0:T(8,128)S(1)}, u32[]{:S(2)}, u32[]{:S(2)}) collective-permute-start(f32[192,128]{1,0:T(8,128)S(1)} %get-tuple-element.57), channel_id=1, source_target_pairs={{0,4},{4,8},{8,12},{12,16},{16,20},{20,24},{24,28},{28,0},{1,5},{5... | collective-permute-start | bytes 294920 | tf_op jit(solution)/shard_map/ppermute | solution.py:28
  25.7 5.3 %collective-permute-start.6 = (f32[192,128]{1,0:T(8,128)S(1)}, f32[192,128]{1,0:T(8,128)S(1)}, u32[]{:S(2)}, u32[]{:S(2)}) collective-permute-start(f32[192,128]{1,0:T(8,128)S(1)} %pad_maximum_fusion), channel_id=1, source_target_pairs={{0,1},{1,2},{2,3},{3,0},{4,5},{5,6},{6,7},{7,4},{8,9},{9,10},{10,1... | collective-permute-start | bytes 294920 | tf_op jit(solution)/shard_map/ppermute | solution.py:28
  27.3 4.1 %collective-permute-start.7 = (f32[192,128]{1,0:T(8,128)S(1)}, f32[192,128]{1,0:T(8,128)S(1)}, u32[]{:S(2)}, u32[]{:S(2)}) collective-permute-start(f32[192,128]{1,0:T(8,128)S(1)} %pad_maximum_fusion.1), channel_id=1, source_target_pairs={{0,3},{1,0},{2,1},{3,2},{4,7},{5,4},{6,5},{7,6},{8,11},{9,8},{10,9... | collective-permute-start | bytes 294920 | tf_op jit(solution)/shard_map/ppermute | solution.py:28
  32.5 4.5 %collective-permute-start.9 = (f32[192,128]{1,0:T(8,128)S(1)}, f32[192,128]{1,0:T(8,128)S(1)}, u32[]{:S(2)}, u32[]{:S(2)}) collective-permute-start(f32[192,128]{1,0:T(8,128)S(1)} %get-tuple-element.69), channel_id=1, source_target_pairs={{0,28},{4,0},{8,4},{12,8},{16,12},{20,16},{24,20},{28,24},{1,29},{... | collective-permute-start | bytes 294920 | tf_op jit(solution)/shard_map/ppermute | solution.py:28
  32.6 7.2 %collective-permute-start.8 = (f32[192,128]{1,0:T(8,128)S(1)}, f32[192,128]{1,0:T(8,128)S(1)}, u32[]{:S(2)}, u32[]{:S(2)}) collective-permute-start(f32[192,128]{1,0:T(8,128)S(1)} %get-tuple-element.68), channel_id=1, source_target_pairs={{0,4},{4,8},{8,12},{12,16},{16,20},{20,24},{24,28},{28,0},{1,5},{5... | collective-permute-start | bytes 294920 | tf_op jit(solution)/shard_map/ppermute | solution.py:28
  39.8 6.6 %collective-permute-start.10 = (f32[192,128]{1,0:T(8,128)S(1)}, f32[192,128]{1,0:T(8,128)S(1)}, u32[]{:S(2)}, u32[]{:S(2)}) collective-permute-start(f32[192,128]{1,0:T(8,128)S(1)} %pad_maximum_fusion.2), channel_id=1, source_target_pairs={{0,1},{1,2},{2,3},{3,0},{4,5},{5,6},{6,7},{7,4},{8,9},{9,10},{10,1... | collective-permute-start | bytes 294920 | tf_op jit(solution)/shard_map/ppermute | solution.py:28
  41.6 4.9 %collective-permute-start.11 = (f32[192,128]{1,0:T(8,128)S(1)}, f32[192,128]{1,0:T(8,128)S(1)}, u32[]{:S(2)}, u32[]{:S(2)}) collective-permute-start(f32[192,128]{1,0:T(8,128)S(1)} %pad_maximum_fusion.3), channel_id=1, source_target_pairs={{0,3},{1,0},{2,1},{3,2},{4,7},{5,4},{6,5},{7,6},{8,11},{9,8},{10,9... | collective-permute-start | bytes 294920 | tf_op jit(solution)/shard_map/ppermute | solution.py:28
  47.6 3.5 %collective-permute-start.13 = (f32[192,128]{1,0:T(8,128)S(1)}, f32[192,128]{1,0:T(8,128)S(1)}, u32[]{:S(2)}, u32[]{:S(2)}) collective-permute-start(f32[192,128]{1,0:T(8,128)S(1)} %get-tuple-element.80), channel_id=1, source_target_pairs={{0,28},{4,0},{8,4},{12,8},{16,12},{20,16},{24,20},{28,24},{1,29},{... | collective-permute-start | bytes 294920 | tf_op jit(solution)/shard_map/ppermute | solution.py:28
  47.7 6.2 %collective-permute-start.12 = (f32[192,128]{1,0:T(8,128)S(1)}, f32[192,128]{1,0:T(8,128)S(1)}, u32[]{:S(2)}, u32[]{:S(2)}) collective-permute-start(f32[192,128]{1,0:T(8,128)S(1)} %get-tuple-element.79), channel_id=1, source_target_pairs={{0,4},{4,8},{8,12},{12,16},{16,20},{20,24},{24,28},{28,0},{1,5},{5... | collective-permute-start | bytes 294920 | tf_op jit(solution)/shard_map/ppermute | solution.py:28
  53.9 6.7 %collective-permute-start.14 = (f32[192,128]{1,0:T(8,128)S(1)}, f32[192,128]{1,0:T(8,128)S(1)}, u32[]{:S(2)}, u32[]{:S(2)}) collective-permute-start(f32[192,128]{1,0:T(8,128)S(1)} %pad_maximum_fusion.4), channel_id=1, source_target_pairs={{0,1},{1,2},{2,3},{3,0},{4,5},{5,6},{6,7},{7,4},{8,9},{9,10},{10,1... | collective-permute-start | bytes 294920 | tf_op jit(solution)/shard_map/ppermute | solution.py:28
  56.8 4.1 %collective-permute-start.15 = (f32[192,128]{1,0:T(8,128)S(1)}, f32[192,128]{1,0:T(8,128)S(1)}, u32[]{:S(2)}, u32[]{:S(2)}) collective-permute-start(f32[192,128]{1,0:T(8,128)S(1)} %pad_maximum_fusion.5), channel_id=1, source_target_pairs={{0,3},{1,0},{2,1},{3,2},{4,7},{5,4},{6,5},{7,6},{8,11},{9,8},{10,9... | collective-permute-start | bytes 294920 | tf_op jit(solution)/shard_map/ppermute | solution.py:28
where the time goes:
time: 63.9 us; the launch traced here: 63.1 us
  waiting for transfers between devices  22.3 us (35%)
  Pallas kernels  20.4 us (32%)
  starting transfers between devices  19.3 us (30%)
  local copies, waits for them, and re-layouts  0.86 us (1%)
    ppermute x16, waiting for transfers between devices, shifted(): return lax.ppermute(x, axis, [(i, (i + by) % size) for i in range(size)])  22.3 us
    pallas_call x12, Pallas kernels, call(): pl.pallas_call(body, out_shape=outs[0] if single else outs, in_specs=spec...  20.4 us
    ppermute x16, starting transfers between devices, shifted(): return lax.ppermute(x, axis, [(i, (i + by) % size) for i in range(size)])  19.3 us
  transfers between devices with their start and end apart: 16, of which 10 were waited for; matrix products, arithmetic and copies ran while one was open for 0% of the time, Pallas kernels for 24%

commit v1 on v0

--- a/solution.py
+++ b/solution.py
@@ -17,10 +17,18 @@
 FROM_XM = (0, None, None)
 FROM_YP = (3, 5, 6)
 FROM_YM = (2, 7, 4)
+TAIL = 8
+SEGMENT = CAP + TAIL
+RANGE = 2.0**15
+SHRINK = 2.0**-10
+SECOND = 2.0**11
+TINY = 2.0**-14
+NUDGE = 0.75 * 2.0**-12
 SPARE = 8
 UNROLL = 16
 VMEM_BYTES = 16 * 2**20
 LANES = 256
+PIECES = 1
 
 
 def shifted(x, axis, by):
@@ -55,6 +63,32 @@
 def hat(base, frac, length):
     steps = lax.broadcasted_iota(jnp.int32, (length, base.shape[1]), 0) - base
     return jnp.where(steps == 0, 1.0 - frac, jnp.where(steps == 1, frac, 0.0))
+
+
+def eleven_bits(value):
+    wide = value * 8193.0
+    return wide - (wide - value)
+
+
+def encoded(rows):
+    value = rows * RANGE
+    code = eleven_bits(value)
+    return jnp.where(value >= code, code, -code)
+
+
+def encoded_first(columns):
+    value = columns * SHRINK
+    high = jnp.where(jnp.abs(value) < TINY, (value + 0.75) - 0.75, eleven_bits(value))
+    return high, (value - high) * SECOND
+
+
+def decode(message_ref, place, out_ref, out_place):
+    start, stop = place * SEGMENT, place * SEGMENT + CAP
+    code = message_ref[start:stop, :]
+    second = message_ref[stop : stop + TAIL, :].T[0:CAP, 0:6]
+    rows = pl.ds(out_place * CAP, CAP)
+    out_ref[rows, :] = jnp.abs(code) * jnp.where(code < 0.0, (1.0 - NUDGE) / RANGE, (1.0 + NUDGE) / RANGE)
+    out_ref[rows, 0:6] = (code[:, 0:6] + second * (1.0 / SECOND)) * (1.0 / SHRINK)
 
 
 def split_wide(value):
@@ -202,33 +236,44 @@
         rows = left_ref[...]
     else:
         turned_ref, pick_ref, c_ref, d_ref = refs[3:7]
-        outs = refs[7:]
-        arrived = jnp.concatenate([c_ref[...], d_ref[...]], axis=0)
+        landed_ref, *outs = refs[7:]
+        for n, ref in enumerate((c_ref, d_ref)):
+            for place in range(3):
+                decode(ref, place, landed_ref, 3 * n + place)
+        arrived = landed_ref[...]
         high, rest = split_wide(arrived)
         middle, low = split(rest)
+        columns = arrived.shape[1]
+        put = jnp.dot(
+            pick_ref[...],
+            jnp.concatenate([high, middle, low], axis=1),
+            preferred_element_type=jnp.float32,
+        )
         rows = left_ref[...]
-        for part in (high, middle, low):
-            rows += jnp.dot(pick_ref[...], part, preferred_element_type=jnp.float32)
-    fresh = []
+        for n in range(3):
+            rows += put[:, n * columns : (n + 1) * columns]
+    outs = [(ref, place) for ref in outs for place in range(ref.shape[0] // SEGMENT)]
     for start in range(0, leaving, LANES):
-        stop = start + LANES
-        cell = cell_ref[:, start:stop]
-        new = advanced(section, rows[start:stop].T, cell, plane_ref[...], turned_ref[...], widths)
-        fresh.append(new.T[:, 0:6])
-    start = 0
-    for ref in outs:
-        stop = start + ref.shape[0]
-        ref[...] = rows[start:stop]
-        for n, part in enumerate(fresh):
-            low, high = max(start, n * LANES), min(stop, (n + 1) * LANES)
-            if low < high:
-                ref[low - start : high - start, 0:6] = part[low - n * LANES : high - n * LANES]
-        start = stop
+        cell = cell_ref[:, start : start + LANES]
+        part = rows[start : start + LANES]
+        new = advanced(section, part.T, cell, plane_ref[...], turned_ref[...], widths)
+        high, low = encoded_first(new)
+        code = encoded(part)
+        turned = high.T
+        for n in range(LANES // CAP):
+            ref, place = outs[start // CAP + n]
+            own = slice(n * CAP, (n + 1) * CAP)
+            base = place * SEGMENT
+            ref[base : base + CAP, :] = code[own]
+            ref[base : base + CAP, 0:6] = turned[own, 0:6]
+            ref[base + CAP : base + SEGMENT, :] = jnp.concatenate(
+                [low[:, own], jnp.zeros((TAIL, ref.shape[1] - CAP), jnp.float32)], axis=1
+            )
 
 
 def advance(section, widths, more, *refs):
     if section:
-        target_ref, c_ref, d_ref, *refs = refs
+        target_ref, landed_ref, *refs = refs
     cells_ref, plane_ref, turned_ref, state_ref, *refs = refs
     if more:
         velocity_ref, *halo, out_ref, next_plane_ref, next_ref = refs
@@ -236,7 +281,7 @@
         (out_ref,) = refs
     if section:
         out_ref[...] = state_ref[...]
-        scatter_rows(out_ref, target_ref, ((c_ref, FROM_YP), (d_ref, FROM_YM)))
+        scatter_rows(out_ref, target_ref, ((landed_ref, FROM_YP + FROM_YM),))
         state_ref = out_ref
     count = cells_ref.shape[2]
     for start in range(0, count, LANES):
@@ -254,11 +299,13 @@
 def settle(section, more, target_ref, *refs):
     if more:
         slot_ref, old_ref, a_ref, b_ref, rows_ref, leave_ref, arrive_ref = refs[:7]
-        state_ref, left_ref, cell_ref, pick_ref, part_ref = refs[7:]
+        state_ref, left_ref, cell_ref, pick_ref, landed_ref, part_ref = refs[7:]
     else:
-        old_ref, a_ref, b_ref, state_ref = refs
+        old_ref, a_ref, b_ref, state_ref, landed_ref = refs
+    decode(a_ref, 0, landed_ref, 0)
+    decode(b_ref, 0, landed_ref, 1)
     state_ref[0 : old_ref.shape[0], :] = old_ref[...]
-    scatter_rows(state_ref, target_ref, ((a_ref, FROM_XP), (b_ref, FROM_XM)))
+    scatter_rows(state_ref, target_ref, ((landed_ref, (FROM_XP[0], FROM_XM[0])),))
     if more:
         leaving = left_ref.shape[0]
         gather_rows(slot_ref, (left_ref, state_ref), (part_ref, rows_ref))
@@ -269,11 +316,30 @@
         left_ref[...] = jnp.where(jnp.max(pick, axis=1, keepdims=True) > 0.0, 0.0, left_ref[...])
 
 
-def finish(target_ref, old_ref, c_ref, d_ref, out_ref, work_ref):
-    count = out_ref.shape[0]
+def land(target_ref, old_ref, c_ref, state_ref, landed_ref):
+    state_ref[...] = old_ref[...]
+    for place in range(3):
+        decode(c_ref, place, landed_ref, place)
+    scatter_rows(state_ref, target_ref, ((landed_ref, FROM_YP),))
+
+
+def finish(target_ref, old_ref, d_ref, out_hbm, work_ref, landed_ref, sems):
+    count = out_hbm.shape[0]
     work_ref[...] = old_ref[...]
-    scatter_rows(work_ref, target_ref, ((c_ref, FROM_YP), (d_ref, FROM_YM)))
-    out_ref[...] = work_ref[0:count, :]
+    for place in range(3):
+        decode(d_ref, place, landed_ref, place)
+    scatter_rows(work_ref, target_ref, ((landed_ref, FROM_YM),))
+    step = count // PIECES
+    copies = [
+        pltpu.make_async_copy(
+            work_ref.at[pl.ds(n * step, step), :], out_hbm.at[pl.ds(n * step, step), :], sems.at[n]
+        )
+        for n in range(PIECES)
+    ]
+    for copy in copies:
+        copy.start()
+    for copy in copies:
+        copy.wait()
 
 
 def local(state, velocity, cells, slots, counts):
@@ -332,11 +398,7 @@
         ],
         [hbm] * 5,
     )
-    low_y = shifted(
-        jnp.concatenate([top, low_x[:, :, width_y - 1 :], high_x[:, :, width_y - 1 :]], axis=2),
-        "gy",
-        1,
-    )
+    low_y = shifted(jnp.concatenate([top, low_x[:, :, width_y - 1 :], high_x[:, :, width_y - 1 :]], axis=2), "gy", 1)
     high_y = shifted(jnp.concatenate([bottom, low_x[:, :, :1], high_x[:, :, :1]], axis=2), "gy", -1)
     halo = [low_x, high_x, low_y, high_y]
     used = 2 * (width_x + width_y) + 4
@@ -344,25 +406,23 @@
     targets = [target[section].reshape(leaving) for section in range(sections)]
     slot = [leave[section].reshape(leaving) for section in range(sections)]
 
-    left, cell = call(
-        first, [slot[0], rows, state], 1, [shape(leaving, columns), cell_shape], [gathered]
-    )
-    messages = [shape(3 * CAP, columns)] * 2 + [shape(CAP, columns)] * 2
+    left, cell = call(first, [slot[0], rows, state], 1, [shape(leaving, columns), cell_shape], [gathered])
+    messages = [shape(3 * SEGMENT, columns)] * 2 + [shape(SEGMENT, columns)] * 2
     for section in range(sections):
         more = section + 1 < sections
         body = functools.partial(depart, section, widths)
         if section == 0:
             turned, *sent = call(body, [left, cell, plane, *halo], 0, [turned_shape, *messages])
         else:
-            sent = call(
-                body, [left, cell, plane, turned, pick, from_low_y, from_high_y], 0, messages
+            landed, *sent = call(
+                body, [left, cell, plane, turned, pick, from_low_y, from_high_y], 0, [shape(coming, columns), *messages]
             )
-        xp, xm, yp, ym = sent
+        xp, xm, yp, ym = (x.astype(jnp.float16) for x in sent)
         from_low_x = shifted(xp, "gx", 1)
         from_high_x = shifted(xm, "gx", -1)
         out = call(
             functools.partial(advance, section, widths, more),
-            ([targets[section - 1], from_low_y, from_high_y] if section else [])
+            ([targets[section - 1], landed] if section else [])
             + [cells, plane, turned, state]
             + ([velocity, *halo] if more else []),
             1 if section else 0,
@@ -371,20 +431,17 @@
         )
         state, plane, turned = out if more else (out, None, None)
         from_low_y = shifted(
-            jnp.concatenate([yp, from_low_x[CAP : 2 * CAP], from_high_x[2 * CAP :]], axis=0),
-            "gy",
-            1,
+            jnp.concatenate([yp, from_low_x[SEGMENT : 2 * SEGMENT], from_high_x[2 * SEGMENT :]], axis=0), "gy", 1
         )
         from_high_y = shifted(
-            jnp.concatenate([ym, from_low_x[2 * CAP :], from_high_x[CAP : 2 * CAP]], axis=0),
-            "gy",
-            -1,
-        )
+            jnp.concatenate([ym, from_low_x[2 * SEGMENT :], from_high_x[SEGMENT : 2 * SEGMENT]], axis=0), "gy", -1
+        )
+        from_low_y, from_high_y = from_low_y.astype(jnp.float32), from_high_y.astype(jnp.float32)
         out = call(
             functools.partial(settle, section, more),
             [targets[section]]
             + ([slot[section + 1]] if more else [])
-            + [state, from_low_x, from_high_x]
+            + [state, from_low_x[:SEGMENT].astype(jnp.float32), from_high_x[:SEGMENT].astype(jnp.float32)]
             + ([rows, leave, arrive] if more else []),
             2 if more else 1,
             [shape(count + SPARE, columns)]
@@ -393,16 +450,29 @@
                 if more
                 else []
             ),
-            [gathered] if more else [],
+            [pltpu.VMEM((2 * CAP, columns), jnp.float32)] + ([gathered] if more else []),
         )
         state, left, cell, pick = out if more else (out, None, None, None)
-    return call(
+    state = call(
+        land,
+        [targets[sections - 1], state, from_low_y],
+        1,
+        [shape(count + SPARE, columns)],
+        [pltpu.VMEM((3 * CAP, columns), jnp.float32)],
+    )
+    return pl.pallas_call(
         finish,
-        [targets[sections - 1], state, from_low_y, from_high_y],
-        1,
-        [shape(count, columns)],
-        [pltpu.VMEM((count + SPARE, columns), jnp.float32)],
-    )
+        out_shape=shape(count, columns),
+        in_specs=[smem, vmem, vmem],
+        out_specs=hbm,
+        scratch_shapes=[
+            pltpu.VMEM((count + SPARE, columns), jnp.float32),
+            pltpu.VMEM((3 * CAP, columns), jnp.float32),
+            pltpu.SemaphoreType.DMA((PIECES,)),
+        ],
+        compiler_params=params,
+        name="finish",
+    )(targets[sections - 1], state, from_high_y)
 
 
 def solution(mesh):

time: 63.9 us -> 62.7 us (0.981)
  waiting for transfers between devices: 22.3 us -> 10.3 us
  starting transfers between devices: 19.3 us -> 28.7 us
  Pallas kernels: 20.4 us -> 21.3 us
    ppermute x16, waiting for transfers between devices: 22.3 us -> 10.3 us  [shifted(): return lax.ppermute(x, axis, [(i, (i + by) % size) for i in range(size)])]
    ppermute x16, starting transfers between devices: 19.3 us -> 28.7 us  [shifted(): return lax.ppermute(x, axis, [(i, (i + by) % size) for i in range(size)])]
    pallas_call x0 -> x1, Pallas kernels: none -> 1.9 us  [local(): pl.pallas_call(finish, out_shape=shape(count, columns), in_specs=[smem, v...]
    pallas_call x12, Pallas kernels: 20.4 us -> 19.4 us  [call(): pl.pallas_call(body, out_shape=outs[0] if single else outs, in_specs=spec...]
  transfers between devices with their start and end apart: 16 -> 16, of which waited for: 10 -> 5; matrix products, arithmetic and copies ran while one was open for 0% -> 0% of each run, Pallas kernels for 24% -> 26%
where the time goes in v1:
time: 62.7 us; the launch traced here: 61.9 us
  starting transfers between devices  28.7 us (46%)
  Pallas kernels  21.3 us (34%)
  waiting for transfers between devices  10.3 us (16%)
  local copies, waits for them, and re-layouts  0.82 us (1%)
    ppermute x16, starting transfers between devices, shifted(): return lax.ppermute(x, axis, [(i, (i + by) % size) for i in range(size)])  28.7 us
    pallas_call x12, Pallas kernels, call(): pl.pallas_call(body, out_shape=outs[0] if single else outs, in_specs=spec...  19.4 us
    ppermute x16, waiting for transfers between devices, shifted(): return lax.ppermute(x, axis, [(i, (i + by) % size) for i in range(size)])  10.3 us
    pallas_call x1, Pallas kernels, local(): pl.pallas_call(finish, out_shape=shape(count, columns), in_specs=[smem, v...  1.9 us
  transfers between devices with their start and end apart: 16, of which 5 were waited for; matrix products, arithmetic and copies ran while one was open for 0% of the time, Pallas kernels for 26%

profile of v1, /device:TPU:1, one launch (start us, length us, event | category | flops | bytes accessed | tf_op | source)
XLA Modules:
  0.0 61.9 jit_solution(16567805548002954687)
XLA Ops:
  0.0 0.8 %slice_bitcast_fusion = (bf16[3,3,16,128]{3,2,1,0:T(8,128)(2,1)S(1)}, bf16[3,3,16,128]{3,2,1,0:T(8,128)(2,1)S(1)}) fusion(bf16[3,3,16,16,128]{4,3,2,1,0:T(8,128)(2,1)} %refs_0_.1), kind=kLoop, calls=%fused_computation.8 | loop fusion | bytes 147456 | tf_op jit(solution)/shard_map/squeeze | solution.py:376
  0.8 5.1 %collective-permute-start.1 = (bf16[3,3,16,128]{3,2,1,0:T(8,128)(2,1)S(1)}, bf16[3,3,16,128]{3,2,1,0:T(8,128)(2,1)S(1)}, u32[]{:S(2)}, u32[]{:S(2)}) collective-permute-start(bf16[3,3,16,128]{3,2,1,0:T(8,128)(2,1)S(1)} %get-tuple-element.87), channel_id=1, source_target_pairs={{0,28},{4,0},{8,4},{12,8},{16,12},{20,16},{24,20},{28,24},{1,29},{... | collective-permute-start | bytes 110600 | tf_op jit(solution)/shard_map/ppermute | solution.py:36
  5.9 1.7 %shard_map.55 = (f32[2048,128]{1,0:T(8,128)S(1)}, bf16[3,3,16,16,128]{4,3,2,1,0:T(8,128)(2,1)S(1)}, s32[3,3,2048]{2,1,0:T(4,128)S(1)}, bf16[3,3,16,128]{3,2,1,0:...) custom-call(bf16[3,3,16,16,128]{4,3,2,1,0:T(8,128)(2,1)} %refs_0_.1,, ...), custom_call_target="tpu_custom_call" | custom-call | tf_op jit(solution)/shard_map/pallas_call | solution.py:361
  7.6 3.7 %collective-permute-done.refs_3_.refs_5_.refs_7_ = bf16[3,3,16,128]{3,2,1,0:T(8,128)(2,1)S(1)} collective-permute-done((bf16[3,3,16,128]{3,2,1,0:T(8,128)(2,1)S(1)}, bf16[3,3,16,128]{3,2,1,0:T(8,128)(2,1)S(1)}, u32[]{:S(2)}, u32[]{:S(2)}) %collective-permute-start) | collective-permute-done | bytes 36896 | tf_op jit(solution)/shard_map/ppermute | solution.py:36
  11.4 3.3 %collective-permute-start.2 = (bf16[3,3,18,128]{3,2,1,0:T(8,128)(2,1)S(1)}, bf16[3,3,18,128]{3,2,1,0:T(8,128)(2,1)S(1)}, u32[]{:S(2)}, u32[]{:S(2)}) collective-permute-start(bf16[3,3,18,128]{3,2,1,0:T(8,128)(2,1)S(1)} %pad_maximum_fusion), channel_id=1, source_target_pairs={{0,1},{1,2},{2,3},{3,0},{4,5},{5,6},{6,7},{7,4},{8,9},{9,10},{10,1... | collective-permute-start | bytes 124424 | tf_op jit(solution)/shard_map/ppermute | solution.py:36
  14.7 0.1 collective-permute-start.3
  14.8 1.4 %shard_map.56 = (f32[512,128]{1,0:T(8,128)S(1)}, s32[3,512]{1,0:T(4,128)S(1)}) custom-call(s32[512]{0:T(512)S(1)} %bitcast.21, f32[2048,128]{1,0:T(8,128)S(1)} %get-tuple-element.50.rows_ref.refs_4_, f32[2048,128]{1,0:T(8,128)S(1)} %get-tuple-element.51.state_ref.refs_3_), custom_call_target="tpu_custom_call" | custom-call | tf_op jit(solution)/shard_map/pallas_call | solution.py:361
  16.2 2.2 %collective-permute-done.3.refs_6_.refs_8_.refs_10_ = bf16[3,3,18,128]{3,2,1,0:T(8,128)(2,1)S(1)} collective-permute-done((bf16[3,3,18,128]{3,2,1,0:T(8,128)(2,1)S(1)}, bf16[3,3,18,128]{3,2,1,0:T(8,128)(2,1)S(1)}, u32[]{:S(2)}, u32[]{:S(2)}) %collective-permute-start.3) | collective-permute-done | bytes 41504 | tf_op jit(solution)/shard_map/ppermute | solution.py:36
  18.3 0.7 %shard_map.57 = (bf16[384,160]{1,0:T(8,128)(2,1)S(1)}, f32[216,128]{1,0:T(8,128)S(1)}, f32[216,128]{1,0:T(8,128)S(1)}, f32[72,128]{1,0:T(8,128)S(1)}, f32[72,128]{1,0:T(8,128)S(1)}) custom-call(f32[512,128]{1,0:T(8,128)S(1)} %get-tuple-element.52.refs_0_, s32[3,512]{1,0:T(4,128)S(1)} %get-tuple-element.53.refs_1_, ...), custom_call_target="tpu_custom_call" | custom-call | tf_op jit(solution)/shard_map/pallas_call | solution.py:361
  19.1 0.1 collective-permute-start.4
  19.2 4.2 %collective-permute-start.5 = (f16[216,128]{1,0:T(8,128)(2,1)S(1)}, f16[216,128]{1,0:T(8,128)(2,1)S(1)}, u32[]{:S(2)}, u32[]{:S(2)}) collective-permute-start(f16[216,128]{1,0:T(8,128)(2,1)S(1)} %convert_element_type.74), channel_id=1, source_target_pairs={{0,28},{4,0},{8,4},{12,8},{16,12},{20,16},{24,20},{28,24},{1,29},{... | collective-permute-start | bytes 165896 | tf_op jit(solution)/shard_map/ppermute | solution.py:36
  23.4 1.5 %collective-permute-done.4 = f16[216,128]{1,0:T(8,128)(2,1)S(1)} collective-permute-done((f16[216,128]{1,0:T(8,128)(2,1)S(1)}, f16[216,128]{1,0:T(8,128)(2,1)S(1)}, u32[]{:S(2)}, u32[]{:S(2)}) %collective-permute-start.4) | collective-permute-done | bytes 55328 | tf_op jit(solution)/shard_map/ppermute | solution.py:36
  24.9 1.4 %collective-permute-start.6 = (f16[216,128]{1,0:T(8,128)(2,1)S(1)}, f16[216,128]{1,0:T(8,128)(2,1)S(1)}, u32[]{:S(2)}, u32[]{:S(2)}) collective-permute-start(f16[216,128]{1,0:T(8,128)(2,1)S(1)} %pad_maximum_fusion.2), channel_id=1, source_target_pairs={{0,1},{1,2},{2,3},{3,0},{4,5},{5,6},{6,7},{7,4},{8,9},{9,10},{10,1... | collective-permute-start | bytes 165896 | tf_op jit(solution)/shard_map/ppermute | solution.py:36
  26.4 0.1 collective-permute-start.7
  26.5 1.7 %shard_map.58 = (f32[2048,128]{1,0:T(8,128)S(1)}, bf16[384,256]{1,0:T(8,128)(2,1)S(1)}, bf16[384,160]{1,0:T(8,128)(2,1)S(1)}) custom-call(s32[3,3,2048]{2,1,0:T(4,128)S(1)} %get-tuple-element.48.refs_0_.refs_2_, bf16[384,256]{1,0:T(8,128)(2,1)S(1)} %get-tuple-element.49.refs_2_.refs_1_, bf16[384,160]{1,0:T(8,128)(2,1)S(1)} %get-tuple-element.56.refs_2_, ...), custom_call_target="tpu_custom_call" | custom-call | tf_op jit(solution)/shard_map/pallas_call | solution.py:361
  28.2 2.0 %shard_map.59 = (f32[2056,128]{1,0:T(8,128)S(1)}, f32[512,128]{1,0:T(8,128)S(1)}, s32[3,512]{1,0:T(4,128)S(1)}, bf16[512,384]{1,0:T(8,128)(2,1)S(1)}) custom-call(s32[512]{0:T(512)S(1)} %bitcast.19, s32[512]{0:T(512)S(1)} %bitcast.23, f32[2048,128]{1,0:T(8,128)S(1)} %get-tuple-element.58.refs_1_, f32[72,128]{1,0:T(8,128)S(1)} %get-tuple-element.103.refs_2_, ...), custom_call_target="tpu_custom_call" | custom-call | tf_op jit(solution)/shard_map/pallas_call | solution.py:361
  30.2 1.3 %shard_map.60 = (f32[384,128]{1,0:T(8,128)S(1)}, f32[216,128]{1,0:T(8,128)S(1)}, f32[216,128]{1,0:T(8,128)S(1)}, f32[72,128]{1,0:T(8,128)S(1)}, f32[72,128]{1,0:T(8,128)S(1)}) custom-call(f32[512,128]{1,0:T(8,128)S(1)} %get-tuple-element.62.refs_0_, s32[3,512]{1,0:T(4,128)S(1)} %get-tuple-element.63.refs_1_, ...), custom_call_target="tpu_custom_call" | custom-call | tf_op jit(solution)/shard_map/pallas_call | solution.py:361
  31.5 0.1 collective-permute-start.8
  31.6 4.3 %collective-permute-start.9 = (f16[216,128]{1,0:T(8,128)(2,1)S(1)}, f16[216,128]{1,0:T(8,128)(2,1)S(1)}, u32[]{:S(2)}, u32[]{:S(2)}) collective-permute-start(f16[216,128]{1,0:T(8,128)(2,1)S(1)} %convert_element_type.82), channel_id=1, source_target_pairs={{0,28},{4,0},{8,4},{12,8},{16,12},{20,16},{24,20},{28,24},{1,29},{... | collective-permute-start | bytes 165896 | tf_op jit(solution)/shard_map/ppermute | solution.py:36
  35.8 1.4 %collective-permute-done.8 = f16[216,128]{1,0:T(8,128)(2,1)S(1)} collective-permute-done((f16[216,128]{1,0:T(8,128)(2,1)S(1)}, f16[216,128]{1,0:T(8,128)(2,1)S(1)}, u32[]{:S(2)}, u32[]{:S(2)}) %collective-permute-start.8) | collective-permute-done | bytes 55328 | tf_op jit(solution)/shard_map/ppermute | solution.py:36
  37.4 2.9 %collective-permute-start.10 = (f16[216,128]{1,0:T(8,128)(2,1)S(1)}, f16[216,128]{1,0:T(8,128)(2,1)S(1)}, u32[]{:S(2)}, u32[]{:S(2)}) collective-permute-start(f16[216,128]{1,0:T(8,128)(2,1)S(1)} %pad_maximum_fusion.4), channel_id=1, source_target_pairs={{0,1},{1,2},{2,3},{3,0},{4,5},{5,6},{6,7},{7,4},{8,9},{9,10},{10,1... | collective-permute-start | bytes 165896 | tf_op jit(solution)/shard_map/ppermute | solution.py:36
  40.3 2.8 %shard_map.61 = (f32[2056,128]{1,0:T(8,128)S(1)}, bf16[384,256]{1,0:T(8,128)(2,1)S(1)}, bf16[384,160]{1,0:T(8,128)(2,1)S(1)}) custom-call(s32[512]{0:T(512)S(1)} %bitcast.20, f32[384,128]{1,0:T(8,128)S(1)} %get-tuple-element.69.refs_1_, s32[3,3,2048]{2,1,0:T(4,128)S(1)} %get-tuple-element.48.refs_0_.refs_2_, ...), custom_call_target="tpu_custom_call" | custom-call | tf_op jit(solution)/shard_map/pallas_call | solution.py:361
  43.2 2.0 %shard_map.62 = (f32[2056,128]{1,0:T(8,128)S(1)}, f32[512,128]{1,0:T(8,128)S(1)}, s32[3,512]{1,0:T(4,128)S(1)}, bf16[512,384]{1,0:T(8,128)(2,1)S(1)}) custom-call(s32[512]{0:T(512)S(1)} %bitcast.17, s32[512]{0:T(512)S(1)} %bitcast.22, f32[2056,128]{1,0:T(8,128)S(1)} %get-tuple-element.71.refs_1_, f32[72,128]{1,0:T(8,128)S(1)} %get-tuple-element.97.refs_2_, ...), custom_call_target="tpu_custom_call" | custom-call | tf_op jit(solution)/shard_map/pallas_call | solution.py:361
  45.2 1.3 %shard_map.63 = (f32[384,128]{1,0:T(8,128)S(1)}, f32[216,128]{1,0:T(8,128)S(1)}, f32[216,128]{1,0:T(8,128)S(1)}, f32[72,128]{1,0:T(8,128)S(1)}, f32[72,128]{1,0:T(8,128)S(1)}) custom-call(f32[512,128]{1,0:T(8,128)S(1)} %get-tuple-element.74.refs_0_, s32[3,512]{1,0:T(4,128)S(1)} %get-tuple-element.75.refs_1_, ...), custom_call_target="tpu_custom_call" | custom-call | tf_op jit(solution)/shard_map/pallas_call | solution.py:361
  46.5 0.1 collective-permute-start.12
  46.6 4.5 %collective-permute-start.13 = (f16[216,128]{1,0:T(8,128)(2,1)S(1)}, f16[216,128]{1,0:T(8,128)(2,1)S(1)}, u32[]{:S(2)}, u32[]{:S(2)}) collective-permute-start(f16[216,128]{1,0:T(8,128)(2,1)S(1)} %convert_element_type.90), channel_id=1, source_target_pairs={{0,28},{4,0},{8,4},{12,8},{16,12},{20,16},{24,20},{28,24},{1,29},{... | collective-permute-start | bytes 165896 | tf_op jit(solution)/shard_map/ppermute | solution.py:36
  51.1 1.4 %collective-permute-done.12 = f16[216,128]{1,0:T(8,128)(2,1)S(1)} collective-permute-done((f16[216,128]{1,0:T(8,128)(2,1)S(1)}, f16[216,128]{1,0:T(8,128)(2,1)S(1)}, u32[]{:S(2)}, u32[]{:S(2)}) %collective-permute-start.12) | collective-permute-done | bytes 55328 | tf_op jit(solution)/shard_map/ppermute | solution.py:36
  52.6 2.7 %collective-permute-start.14 = (f16[216,128]{1,0:T(8,128)(2,1)S(1)}, f16[216,128]{1,0:T(8,128)(2,1)S(1)}, u32[]{:S(2)}, u32[]{:S(2)}) collective-permute-start(f16[216,128]{1,0:T(8,128)(2,1)S(1)} %pad_maximum_fusion.6), channel_id=1, source_target_pairs={{0,1},{1,2},{2,3},{3,0},{4,5},{5,6},{6,7},{7,4},{8,9},{9,10},{10,1... | collective-permute-start | bytes 165896 | tf_op jit(solution)/shard_map/ppermute | solution.py:36
  55.4 2.8 %shard_map.64.refs_0_ = f32[2056,128]{1,0:T(8,128)S(1)} custom-call(s32[512]{0:T(512)S(1)} %bitcast.18, f32[384,128]{1,0:T(8,128)S(1)} %get-tuple-element.81.refs_1_, s32[3,3,2048]{2,1,0:T(4,128)S(1)} %get-tuple-element.48.refs_0_.refs_2_, bf16[384,256]{1,0:T(8,128)(2,1)S(1)} %get-tuple-element.76.refs_2_.refs_3_, ...), custom_call_target="tpu_custom_call" | custom-call | tf_op jit(solution)/shard_map/pallas_call | solution.py:361
  58.2 0.8 %shard_map.65.old_ref = f32[2056,128]{1,0:T(8,128)S(1)} custom-call(s32[512]{0:T(512)S(1)} %bitcast.14, f32[2056,128]{1,0:T(8,128)S(1)} %shard_map.64.refs_0_, f32[72,128]{1,0:T(8,128)S(1)} %get-tuple-element.91.refs_1_, f32[72,128]{1,0:T(8,128)S(1)} %get-tuple-element.94.refs_2_), custom_call_target="tpu_custom_call" | custom-call | tf_op jit(solution)/shard_map/pallas_call | solution.py:361
  59.1 0.9 %shard_map.66.old_ref = f32[2056,128]{1,0:T(8,128)S(1)} custom-call(s32[512]{0:T(512)S(1)} %bitcast.15, f32[2056,128]{1,0:T(8,128)S(1)} %shard_map.65.old_ref, f32[216,128]{1,0:T(8,128)S(1)} %convert_element_type.93.c_ref), custom_call_target="tpu_custom_call" | custom-call | tf_op jit(solution)/shard_map/pallas_call | solution.py:361
  60.0 1.9 %finish.1 = f32[2048,128]{1,0:T(8,128)} custom-call(s32[512]{0:T(512)S(1)} %bitcast.16, f32[2056,128]{1,0:T(8,128)S(1)} %shard_map.66.old_ref, f32[216,128]{1,0:T(8,128)S(1)} %convert_element_type.95.d_ref), custom_call_target="tpu_custom_call" | custom-call | tf_op jit(solution)/shard_map/finish/pallas_call | solution.py:463
  (49 shorter events, 0.6 us)
Async XLA Ops:
  0.8 6.8 %collective-permute-start.1 = (bf16[3,3,16,128]{3,2,1,0:T(8,128)(2,1)S(1)}, bf16[3,3,16,128]{3,2,1,0:T(8,128)(2,1)S(1)}, u32[]{:S(2)}, u32[]{:S(2)}) collective-permute-start(bf16[3,3,16,128]{3,2,1,0:T(8,128)(2,1)S(1)} %get-tuple-element.87), channel_id=1, source_target_pairs={{0,28},{4,0},{8,4},{12,8},{16,12},{20,16},{24,20},{28,24},{1,29},{... | collective-permute-start | bytes 110600 | tf_op jit(solution)/shard_map/ppermute | solution.py:36
  5.9 5.5 %collective-permute-start = (bf16[3,3,16,128]{3,2,1,0:T(8,128)(2,1)S(1)}, bf16[3,3,16,128]{3,2,1,0:T(8,128)(2,1)S(1)}, u32[]{:S(2)}, u32[]{:S(2)}) collective-permute-start(bf16[3,3,16,128]{3,2,1,0:T(8,128)(2,1)S(1)} %get-tuple-element.88), channel_id=1, source_target_pairs={{0,4},{4,8},{8,12},{12,16},{16,20},{20,24},{24,28},{28,0},{1,5},{5... | collective-permute-start | bytes 110600 | tf_op jit(solution)/shard_map/ppermute | solution.py:36
  11.4 4.8 %collective-permute-start.2 = (bf16[3,3,18,128]{3,2,1,0:T(8,128)(2,1)S(1)}, bf16[3,3,18,128]{3,2,1,0:T(8,128)(2,1)S(1)}, u32[]{:S(2)}, u32[]{:S(2)}) collective-permute-start(bf16[3,3,18,128]{3,2,1,0:T(8,128)(2,1)S(1)} %pad_maximum_fusion), channel_id=1, source_target_pairs={{0,1},{1,2},{2,3},{3,0},{4,5},{5,6},{6,7},{7,4},{8,9},{9,10},{10,1... | collective-permute-start | bytes 124424 | tf_op jit(solution)/shard_map/ppermute | solution.py:36
  14.7 3.6 %collective-permute-start.3 = (bf16[3,3,18,128]{3,2,1,0:T(8,128)(2,1)S(1)}, bf16[3,3,18,128]{3,2,1,0:T(8,128)(2,1)S(1)}, u32[]{:S(2)}, u32[]{:S(2)}) collective-permute-start(bf16[3,3,18,128]{3,2,1,0:T(8,128)(2,1)S(1)} %pad_maximum_fusion.1), channel_id=1, source_target_pairs={{0,3},{1,0},{2,1},{3,2},{4,7},{5,4},{6,5},{7,6},{8,11},{9,8},{10,9... | collective-permute-start | bytes 124424 | tf_op jit(solution)/shard_map/ppermute | solution.py:36
  19.1 5.8 %collective-permute-start.4 = (f16[216,128]{1,0:T(8,128)(2,1)S(1)}, f16[216,128]{1,0:T(8,128)(2,1)S(1)}, u32[]{:S(2)}, u32[]{:S(2)}) collective-permute-start(f16[216,128]{1,0:T(8,128)(2,1)S(1)} %convert_element_type.72), channel_id=1, source_target_pairs={{0,4},{4,8},{8,12},{12,16},{16,20},{20,24},{24,28},{28,0},{1,5},{5... | collective-permute-start | bytes 165896 | tf_op jit(solution)/shard_map/ppermute | solution.py:36
  19.2 5.7 %collective-permute-start.5 = (f16[216,128]{1,0:T(8,128)(2,1)S(1)}, f16[216,128]{1,0:T(8,128)(2,1)S(1)}, u32[]{:S(2)}, u32[]{:S(2)}) collective-permute-start(f16[216,128]{1,0:T(8,128)(2,1)S(1)} %convert_element_type.74), channel_id=1, source_target_pairs={{0,28},{4,0},{8,4},{12,8},{16,12},{20,16},{24,20},{28,24},{1,29},{... | collective-permute-start | bytes 165896 | tf_op jit(solution)/shard_map/ppermute | solution.py:36
  24.9 5.2 %collective-permute-start.6 = (f16[216,128]{1,0:T(8,128)(2,1)S(1)}, f16[216,128]{1,0:T(8,128)(2,1)S(1)}, u32[]{:S(2)}, u32[]{:S(2)}) collective-permute-start(f16[216,128]{1,0:T(8,128)(2,1)S(1)} %pad_maximum_fusion.2), channel_id=1, source_target_pairs={{0,1},{1,2},{2,3},{3,0},{4,5},{5,6},{6,7},{7,4},{8,9},{9,10},{10,1... | collective-permute-start | bytes 165896 | tf_op jit(solution)/shard_map/ppermute | solution.py:36
  26.4 3.8 %collective-permute-start.7 = (f16[216,128]{1,0:T(8,128)(2,1)S(1)}, f16[216,128]{1,0:T(8,128)(2,1)S(1)}, u32[]{:S(2)}, u32[]{:S(2)}) collective-permute-start(f16[216,128]{1,0:T(8,128)(2,1)S(1)} %pad_maximum_fusion.3), channel_id=1, source_target_pairs={{0,3},{1,0},{2,1},{3,2},{4,7},{5,4},{6,5},{7,6},{8,11},{9,8},{10,9... | collective-permute-start | bytes 165896 | tf_op jit(solution)/shard_map/ppermute | solution.py:36
  31.5 5.8 %collective-permute-start.8 = (f16[216,128]{1,0:T(8,128)(2,1)S(1)}, f16[216,128]{1,0:T(8,128)(2,1)S(1)}, u32[]{:S(2)}, u32[]{:S(2)}) collective-permute-start(f16[216,128]{1,0:T(8,128)(2,1)S(1)} %convert_element_type.80), channel_id=1, source_target_pairs={{0,4},{4,8},{8,12},{12,16},{16,20},{20,24},{24,28},{28,0},{1,5},{5... | collective-permute-start | bytes 165896 | tf_op jit(solution)/shard_map/ppermute | solution.py:36
  31.6 5.7 %collective-permute-start.9 = (f16[216,128]{1,0:T(8,128)(2,1)S(1)}, f16[216,128]{1,0:T(8,128)(2,1)S(1)}, u32[]{:S(2)}, u32[]{:S(2)}) collective-permute-start(f16[216,128]{1,0:T(8,128)(2,1)S(1)} %convert_element_type.82), channel_id=1, source_target_pairs={{0,28},{4,0},{8,4},{12,8},{16,12},{20,16},{24,20},{28,24},{1,29},{... | collective-permute-start | bytes 165896 | tf_op jit(solution)/shard_map/ppermute | solution.py:36
  37.4 7.8 %collective-permute-start.10 = (f16[216,128]{1,0:T(8,128)(2,1)S(1)}, f16[216,128]{1,0:T(8,128)(2,1)S(1)}, u32[]{:S(2)}, u32[]{:S(2)}) collective-permute-start(f16[216,128]{1,0:T(8,128)(2,1)S(1)} %pad_maximum_fusion.4), channel_id=1, source_target_pairs={{0,1},{1,2},{2,3},{3,0},{4,5},{5,6},{6,7},{7,4},{8,9},{9,10},{10,1... | collective-permute-start | bytes 165896 | tf_op jit(solution)/shard_map/ppermute | solution.py:36
  40.3 4.9 %collective-permute-start.11 = (f16[216,128]{1,0:T(8,128)(2,1)S(1)}, f16[216,128]{1,0:T(8,128)(2,1)S(1)}, u32[]{:S(2)}, u32[]{:S(2)}) collective-permute-start(f16[216,128]{1,0:T(8,128)(2,1)S(1)} %pad_maximum_fusion.5), channel_id=1, source_target_pairs={{0,3},{1,0},{2,1},{3,2},{4,7},{5,4},{6,5},{7,6},{8,11},{9,8},{10,9... | collective-permute-start | bytes 165896 | tf_op jit(solution)/shard_map/ppermute | solution.py:36
  46.5 6.1 %collective-permute-start.12 = (f16[216,128]{1,0:T(8,128)(2,1)S(1)}, f16[216,128]{1,0:T(8,128)(2,1)S(1)}, u32[]{:S(2)}, u32[]{:S(2)}) collective-permute-start(f16[216,128]{1,0:T(8,128)(2,1)S(1)} %convert_element_type.88), channel_id=1, source_target_pairs={{0,4},{4,8},{8,12},{12,16},{16,20},{20,24},{24,28},{28,0},{1,5},{5... | collective-permute-start | bytes 165896 | tf_op jit(solution)/shard_map/ppermute | solution.py:36
  46.6 6.0 %collective-permute-start.13 = (f16[216,128]{1,0:T(8,128)(2,1)S(1)}, f16[216,128]{1,0:T(8,128)(2,1)S(1)}, u32[]{:S(2)}, u32[]{:S(2)}) collective-permute-start(f16[216,128]{1,0:T(8,128)(2,1)S(1)} %convert_element_type.90), channel_id=1, source_target_pairs={{0,28},{4,0},{8,4},{12,8},{16,12},{20,16},{24,20},{28,24},{1,29},{... | collective-permute-start | bytes 165896 | tf_op jit(solution)/shard_map/ppermute | solution.py:36
  52.6 6.4 %collective-permute-start.14 = (f16[216,128]{1,0:T(8,128)(2,1)S(1)}, f16[216,128]{1,0:T(8,128)(2,1)S(1)}, u32[]{:S(2)}, u32[]{:S(2)}) collective-permute-start(f16[216,128]{1,0:T(8,128)(2,1)S(1)} %pad_maximum_fusion.6), channel_id=1, source_target_pairs={{0,1},{1,2},{2,3},{3,0},{4,5},{5,6},{6,7},{7,4},{8,9},{9,10},{10,1... | collective-permute-start | bytes 165896 | tf_op jit(solution)/shard_map/ppermute | solution.py:36
  55.3 4.7 %collective-permute-start.15 = (f16[216,128]{1,0:T(8,128)(2,1)S(1)}, f16[216,128]{1,0:T(8,128)(2,1)S(1)}, u32[]{:S(2)}, u32[]{:S(2)}) collective-permute-start(f16[216,128]{1,0:T(8,128)(2,1)S(1)} %pad_maximum_fusion.7), channel_id=1, source_target_pairs={{0,3},{1,0},{2,1},{3,2},{4,7},{5,4},{6,5},{7,6},{8,11},{9,8},{10,9... | collective-permute-start | bytes 165896 | tf_op jit(solution)/shard_map/ppermute | solution.py:36

commit v2 on v1

v2 whole, which is shorter than its diff:
```python
import functools

import jax
import jax.numpy as jnp
from jax import lax
from jax.experimental import pallas as pl
from jax.experimental.pallas import tpu as pltpu
from jax.sharding import PartitionSpec as P


CAP = 64
DIRS = 8
GAMMA = (8.0 / 15.0, 5.0 / 12.0, 3.0 / 4.0)
ZETA = (0.0, -17.0 / 60.0, -5.0 / 12.0)
SEGMENTS = (0, 4, 6, 1, 5, 7, 2, 3)
FROM_XP = (1, None, None)
FROM_XM = (0, None, None)
FROM_YP = (3, 5, 6)
FROM_YM = (2, 7, 4)
TAIL = 8
FIRST = 6
SEGMENT = CAP + TAIL
RANGE = 2.0**15
SHRINK = 2.0**-10
SECOND = 2.0**11
TINY = 2.0**-14
NUDGE = 0.75 * 2.0**-12
SPARE = 8
UNROLL = 16
VMEM_BYTES = 16 * 2**20
LANES = 256
PIECES = 1


def shifted(x, axis, by):
    size = lax.axis_size(axis)
    return lax.ppermute(x, axis, [(i, (i + by) % size) for i in range(size)])


def scatter_rows(state_ref, target, arrivals):
    target_ref = target.wait()
    for ref, dirs in arrivals:
        for place, d in enumerate(dirs):
            if d is None:
                continue

            def body(t, carry, ref=ref, place=place, d=d):
                slot = target_ref[d * CAP + t]
                state_ref[pl.ds(slot, 1), :] = ref[pl.ds(place * CAP + t, 1), :]
                return carry

            lax.fori_loop(0, CAP, body, 0, unroll=UNROLL)


class Table:
    def __init__(self, source_ref, ref, sem):
        self.ref, self.copy = ref, pltpu.make_async_copy(source_ref, ref, sem)
        self.copy.start()

    def wait(self):
        self.copy.wait()
        return self.ref


def with_tables(body, count, *refs):
    sems = refs[-1]
    tables = [Table(refs[n], refs[n - count - 1], sems.at[n]) for n in range(count)]
    body(*tables, *refs[count : len(refs) - count - 1])


def gather_rows(slot, *pairs):
    slot_ref = slot.wait()

    def body(t, carry):
        slot = slot_ref[t]
        for out_ref, from_ref in pairs:
            out_ref[pl.ds(t, 1), :] = from_ref[pl.ds(slot, 1), :]
        return carry

    lax.fori_loop(0, slot_ref.shape[0], body, 0, unroll=UNROLL)


def hat(base, frac, length):
    steps = lax.broadcasted_iota(jnp.int32, (length, base.shape[1]), 0) - base
    return jnp.where(steps == 0, 1.0 - frac, jnp.where(steps == 1, frac, 0.0))


def eleven_bits(value):
    wide = value * 8193.0
    return wide - (wide - value)


def encoded(rows):
    value = rows * RANGE
    code = eleven_bits(value)
    lane = lax.broadcasted_iota(jnp.int32, rows.shape, 1)
    return jnp.where(lane < FIRST, 0.0, jnp.where(value >= code, code, -code))


def encoded_first(columns):
    value = columns * SHRINK
    high = jnp.where(jnp.abs(value) < TINY, (value + 0.75) - 0.75, eleven_bits(value))
    return high, (value - high) * SECOND


def first_columns(message_ref, place):
    stop = place * SEGMENT + CAP
    tail = message_ref[stop : stop + TAIL, :]
    return (tail[:, 0:CAP] + tail[:, CAP:] * (1.0 / SECOND)) * (1.0 / SHRINK)


def decode(segments, out_ref):
    columns = jnp.concatenate([first_columns(ref, place) for ref, place in segments], axis=1)
    for n, (ref, place) in enumerate(segments):
        code = ref[place * SEGMENT : place * SEGMENT + CAP, :]
        scale = jnp.where(code < 0.0, (1.0 - NUDGE) / RANGE, (1.0 + NUDGE) / RANGE)
        out_ref[n * CAP : (n + 1) * CAP, :] = jnp.abs(code) * scale
    out_ref[0 : len(segments) * CAP, 0:FIRST] = columns.T[:, 0:FIRST]


def split_wide(value):
    high = value.astype(jnp.bfloat16)
    return high, value - high.astype(jnp.float32)


def split(weight):
    high = weight.astype(jnp.bfloat16)
    return high, (weight - high.astype(jnp.float32)).astype(jnp.bfloat16)


def advanced(section, turned, cell, plane, rim, widths):
    width_x, width_y, depth = widths
    lanes = cell.shape[1]
    frac, before = turned[0:3], turned[3:6]
    cx, cy, cz = cell[0:1], cell[1:2], cell[2:3]
    fx, fy, fz = frac[0:1], frac[1:2], frac[2:3]
    wx = hat(cx, fx, width_x)
    wy = hat(cy, fy, width_y)
    wz = hat(cz, fz, depth)
    x_low = jnp.where(cx == -1, 1.0 - fx, 0.0)
    x_high = jnp.where(cx == width_x - 1, fx, 0.0)
    y_low = jnp.where(cy == -1, 1.0 - fy, 0.0)
    y_high = jnp.where(cy == width_y - 1, fy, 0.0)
    inner = (wx[:, None, :] * wy[None, :, :]).reshape(width_x * width_y, lanes)
    corners = [x_low * y_low, x_high * y_low, x_low * y_high, x_high * y_high]
    pad = rim.shape[1] // 2 - 2 * (width_x + width_y) - 4
    edge = jnp.concatenate(
        [x_low * wy, x_high * wy, y_low * wx, y_high * wx, *corners, jnp.zeros((pad, lanes), jnp.float32)], axis=0
    )
    high, low = split(inner)
    columns = jnp.dot(plane, high, preferred_element_type=jnp.float32)
    columns += jnp.dot(plane, low, preferred_element_type=jnp.float32)
    columns += jnp.dot(rim, jnp.concatenate(split(edge), axis=0), preferred_element_type=jnp.float32)
    speed = jnp.concatenate(
        [jnp.sum(columns[k * depth : (k + 1) * depth] * wz, axis=0, keepdims=True) for k in range(3)], axis=0
    )
    moved = frac + GAMMA[section] * speed + ZETA[section] * before
    return jnp.concatenate([moved, speed, jnp.zeros((2, lanes), jnp.float32)], axis=0)


def turn_rim(section, halo, out_ref):
    low_x, high_x, low_y, high_y = halo
    width_x, width_y, depth = low_y.shape[2] - 2, low_x.shape[2], low_x.shape[3]
    pad = out_ref.shape[1] // 2 - 2 * (width_x + width_y)
    spot = lax.broadcasted_iota(jnp.int32, (pad, depth), 0)
    for k in range(3):
        corners = jnp.zeros((pad, depth), jnp.float32)
        for n, (ref, row) in enumerate(
            ((low_y, width_x), (low_y, width_x + 1), (high_y, width_x), (high_y, width_x + 1))
        ):
            value = ref[section, k, row : row + 1, :].astype(jnp.float32)
            corners = jnp.where(spot == n, value, corners)
        rim = jnp.concatenate(
            [
                low_x[section, k],
                high_x[section, k],
                low_y[section, k, 0:width_x, :],
                high_y[section, k, 0:width_x, :],
                corners.astype(out_ref.dtype),
            ],
            axis=0,
        )
        turned = rim.T
        out_ref[k * depth : (k + 1) * depth, :] = jnp.concatenate([turned, turned], axis=1)


def turn_plane(velocity_ref, section, out_ref):
    width_x, width_y, depth = velocity_ref.shape[2:]
    for k in range(3):
        plane = velocity_ref[section, k].reshape(width_x * width_y, depth)
        out_ref[k * depth : (k + 1) * depth, :] = plane.T


def turned_row(row):
    return jnp.broadcast_to(row, (8, row.shape[1])).T[:, 0:1]


def fetch(*refs):
    sources, (state_ref, cells_ref) = refs[:5], refs[5:7]
    low_ref, high_ref, rows_ref, leave_ref, target_ref = refs[7:12]
    sections = cells_ref.shape[0]
    plane_refs, refs = refs[12 : 12 + sections], refs[12 + sections :]
    pick_refs, (velocity_ref, slots_ref, counts_ref, sems) = refs[:-4], refs[-4:]
    copies = [
        pltpu.make_async_copy(src, dst, sems.at[n])
        for n, (src, dst) in enumerate(
            zip(sources, (velocity_ref, slots_ref, counts_ref, cells_ref, state_ref))
        )
    ]
    for copy in copies:
        copy.start()
    _, parts, count = cells_ref.shape
    width_y = velocity_ref.shape[3]
    leaving = leave_ref.shape[2]

    copies[1].wait()
    copies[2].wait()
    place = lax.broadcasted_iota(jnp.int32, (DIRS, leaving), 1)
    start = lax.broadcasted_iota(jnp.int32, (DIRS, leaving), 0) * CAP
    spread = jnp.where((place >= start) & (place < start + CAP), 1.0, 0.0)
    tally = jnp.concatenate(
        [counts_ref[s, 0].astype(jnp.float32) for s in range(sections)]
        + [jnp.zeros((-sections % 8, DIRS), jnp.float32)],
        axis=0,
    )
    limit = jnp.dot(tally, spread, preferred_element_type=jnp.float32).astype(jnp.int32)
    within = lax.broadcasted_iota(jnp.int32, (1, leaving), 1) % CAP
    arrives = []
    for s in range(sections):
        order = slots_ref[s : s + 1, 0:leaving]
        target = jnp.where(within < limit[s : s + 1], order, count)
        target_ref[s] = target
        leave_ref[s] = jnp.concatenate([order[:, d * CAP : (d + 1) * CAP] for d in SEGMENTS], axis=1)
        arrive = jnp.concatenate([target[:, d * CAP : (d + 1) * CAP] for d in FROM_YP + FROM_YM], axis=1)
        arrives.append(arrive.astype(jnp.float32))
    copies[0].wait()
    for s in range(sections):
        for k in range(3):
            block = velocity_ref[s, k].astype(jnp.float32)
            low_ref[s, k] = block[:, 0, :].astype(low_ref.dtype)
            high_ref[s, k] = block[:, width_y - 1, :].astype(low_ref.dtype)
    for s, plane_ref in enumerate(plane_refs):
        turn_plane(velocity_ref, s, plane_ref)
    copies[3].wait()
    flat = jnp.concatenate(
        [cells_ref[s].astype(jnp.float32) for s in range(sections)]
        + [jnp.zeros((-sections * parts % 8, count), jnp.float32)],
        axis=0,
    )
    rows_ref[:, 0 : flat.shape[0]] = flat.T
    for s in range(1, sections):
        pick_ref, turned_pick_ref, keep_ref = pick_refs[3 * (s - 1) : 3 * s]
        leave, arrive = leave_ref[s].astype(jnp.float32), arrives[s - 1]
        pick = jnp.where(turned_row(leave) == arrive, 1.0, 0.0)
        pick_ref[...] = pick.astype(pick_ref.dtype)
        turned_pick_ref[...] = jnp.where(turned_row(arrive) == leave, 1.0, 0.0).astype(pick_ref.dtype)
        keep_ref[...] = jnp.broadcast_to(1.0 - jnp.max(pick, axis=1, keepdims=True), keep_ref.shape)
    copies[4].wait()


def own_cells(section, part_ref, cell_ref):
    parts = cell_ref.shape[0]
    cell_ref[...] = part_ref[...].T[section * parts : (section + 1) * parts].astype(jnp.int32)


def first(slot, rows_ref, state_ref, code_ref, columns_ref, cell_ref, left_ref, part_ref):
    gather_rows(slot, (left_ref, state_ref), (part_ref, rows_ref))
    own_cells(0, part_ref, cell_ref)
    rows = left_ref[...]
    code_ref[...] = encoded(rows)
    columns_ref[...] = rows.T[0:TAIL]


def depart(section, widths, *refs):
    code_ref, columns_ref, cell_ref, plane_ref = refs[:4]
    leaving = code_ref.shape[0]
    codes, columns = code_ref[...], columns_ref[...]
    if section == 0:
        halo, turned_ref, outs = refs[4:8], refs[8], refs[9:]
        turn_rim(section, halo, turned_ref)
    else:
        turned_ref, pick_ref, turned_pick_ref, c_ref, d_ref = refs[4:9]
        outs = refs[9:]
        came = [(ref, place) for ref in (c_ref, d_ref) for place in range(3)]
        arrived = jnp.concatenate([first_columns(ref, place) for ref, place in came], axis=1)
        high, rest = split_wide(arrived)
        middle, low = split(rest)
        parts = [part.astype(jnp.float32) for part in (high, middle, low)]
        put = jnp.dot(
            jnp.concatenate(parts, axis=0).astype(jnp.bfloat16),
            turned_pick_ref[...],
            preferred_element_type=jnp.float32,
        )
        for n in range(len(parts)):
            columns += put[n * TAIL : (n + 1) * TAIL]
        arrived = jnp.concatenate(
            [ref[place * SEGMENT : place * SEGMENT + CAP, :] for ref, place in came], axis=0
        )
        put = jnp.dot(
            pick_ref[...], jnp.concatenate(split(arrived), axis=1), preferred_element_type=jnp.float32
        )
        width = arrived.shape[1]
        codes += put[:, 0:width] + put[:, width:]
    outs = [(ref, place) for ref in outs for place in range(ref.shape[0] // SEGMENT)]
    for n, (ref, place) in enumerate(outs):
        ref[place * SEGMENT : place * SEGMENT + CAP, :] = codes[n * CAP : (n + 1) * CAP]
    for start in range(0, leaving, LANES):
        new = advanced(
            section,
            columns[:, start : start + LANES],
            cell_ref[:, start : start + LANES],
            plane_ref[...],
            turned_ref[...],
            widths,
        )
        high, low = encoded_first(new)
        for n in range(LANES // CAP):
            ref, place = outs[start // CAP + n]
            own = slice(n * CAP, (n + 1) * CAP)
            stop = place * SEGMENT + CAP
            ref[stop : stop + TAIL, :] = jnp.concatenate([high[:, own], low[:, own]], axis=1)


def advance(section, widths, halos, *refs):
    if section:
        target, c_ref, d_ref, *refs, work_ref, landed_ref = refs
    cells_ref, plane_ref, turned_ref, state_ref, *refs = refs
    halo, (out_ref, *turned_refs) = refs[:halos], refs[halos:]
    if section:
        work_ref[...] = state_ref[...]
        decode([(ref, place) for ref in (c_ref, d_ref) for place in range(3)], landed_ref)
        scatter_rows(work_ref, target, ((landed_ref, FROM_YP + FROM_YM),))
        state_ref = work_ref
    count = cells_ref.shape[2]
    for start in range(0, count, LANES):
        rows = state_ref[start : start + LANES, :]
        cell = cells_ref[section, :, start : start + LANES]
        new = advanced(section, rows.T, cell, plane_ref[...], turned_ref[...], widths)
        out_ref[start : start + LANES, :] = rows
        out_ref[start : start + LANES, 0:6] = new.T[:, 0:6]
    for n, next_ref in enumerate(turned_refs):
        turn_rim(section + 1 + n, halo, next_ref)


def settle(section, more, target, *refs):
    if more:
        slot, old_ref, a_ref, b_ref, rows_ref, keep_ref = refs[:6]
        state_ref, code_ref, columns_ref, cell_ref = refs[6:10]
        landed_ref, left_ref, part_ref = refs[10:]
    else:
        old_ref, a_ref, b_ref, state_ref, landed_ref = refs
    decode([(a_ref, 0), (b_ref, 0)], landed_ref)
    state_ref[0 : old_ref.shape[0], :] = old_ref[...]
    scatter_rows(state_ref, target, ((landed_ref, (FROM_XP[0], FROM_XM[0])),))
    if more:
        gather_rows(slot, (left_ref, state_ref), (part_ref, rows_ref))
        own_cells(section + 1, part_ref, cell_ref)
        rows = left_ref[...] * keep_ref[...]
        code_ref[...] = encoded(rows)
        columns_ref[...] = rows.T[0:TAIL]


def land(target, old_ref, c_ref, state_ref, landed_ref):
    state_ref[...] = old_ref[...]
    decode([(c_ref, place) for place in range(3)], landed_ref)
    scatter_rows(state_ref, target, ((landed_ref, FROM_YP),))


def finish(target, old_ref, d_ref, out_hbm, work_ref, landed_ref, sems):
    count = out_hbm.shape[0]
    work_ref[...] = old_ref[...]
    decode([(d_ref, place) for place in range(3)], landed_ref)
    scatter_rows(work_ref, target, ((landed_ref, FROM_YM),))
    step = count // PIECES
    copies = [
        pltpu.make_async_copy(
            work_ref.at[pl.ds(n * step, step), :], out_hbm.at[pl.ds(n * step, step), :], sems.at[n]
        )
        for n in range(PIECES)
    ]
    for copy in copies:
        copy.start()
    for copy in copies:
        copy.wait()


def local(state, velocity, cells, slots, counts):
    sections = velocity.shape[0]
    width_x, width_y, depth = widths = velocity.shape[2:]
    count, columns = state.shape
    leaving = DIRS * CAP
    coming = CAP * (len(FROM_YP) + len(FROM_YM))
    vmem = pl.BlockSpec(memory_space=pltpu.VMEM)
    hbm = pl.BlockSpec(memory_space=pltpu.HBM)
    params = pltpu.CompilerParams(vmem_limit_bytes=VMEM_BYTES)

    def shape(*dims, dtype=jnp.float32):
        return jax.ShapeDtypeStruct(dims, dtype)

    def call(body, operands, tables, outs, scratch=(), spec=vmem, out_spec=vmem):
        single = len(outs) == 1
        wanted = [pltpu.SMEM(x.shape, x.dtype) for x in operands[:tables]]
        if tables:
            scratch = [*scratch, *wanted, pltpu.SemaphoreType.DMA((tables,))]
            body = functools.partial(with_tables, body, tables)
        return pl.pallas_call(
            body,
            out_shape=outs[0] if single else outs,
            in_specs=[spec] * len(operands),
            out_specs=out_spec if single else [out_spec] * len(outs),
            scratch_shapes=scratch,
            compiler_params=params,
        )(*operands)

    plane_shape = shape(3 * depth, width_x * width_y, dtype=velocity.dtype)
    edge_shape = shape(sections, 3, width_x, depth, dtype=velocity.dtype)
    cell_shape = shape(3, leaving, dtype=jnp.int32)
    pick_shapes = [
        shape(leaving, coming, dtype=jnp.bfloat16),
        shape(coming, leaving, dtype=jnp.bfloat16),
        shape(leaving, columns),
    ]
    gathered = pltpu.VMEM((leaving, columns), jnp.float32)

    low_x = shifted(velocity[:, :, width_x - 1], "gx", 1)
    high_x = shifted(velocity[:, :, 0], "gx", -1)
    sources = (velocity, slots, counts, cells, state)
    state, cells, bottom, top, rows, leave, target, *rest = call(
        fetch,
        [pltpu.with_memory_space_constraint(x, pltpu.HBM) for x in sources],
        0,
        [
            shape(*state.shape),
            shape(*cells.shape, dtype=cells.dtype),
            edge_shape,
            edge_shape,
            shape(count, columns),
            shape(sections, 1, leaving, dtype=jnp.int32),
            shape(sections, 1, leaving, dtype=jnp.int32),
            *[plane_shape] * sections,
            *pick_shapes * (sections - 1),
        ],
        [
            pltpu.VMEM(velocity.shape, velocity.dtype),
            pltpu.VMEM(slots.shape, slots.dtype),
            pltpu.VMEM(counts.shape, counts.dtype),
            pltpu.SemaphoreType.DMA((5,)),
        ],
        hbm,
    )
    planes, picks = rest[:sections], rest[sections:]
    low_y = shifted(jnp.concatenate([top, low_x[:, :, width_y - 1 :], high_x[:, :, width_y - 1 :]], axis=2), "gy", 1)
    high_y = shifted(jnp.concatenate([bottom, low_x[:, :, :1], high_x[:, :, :1]], axis=2), "gy", -1)
    halo = [low_x, high_x, low_y, high_y]
    used = 2 * (width_x + width_y) + 4
    turned_shape = shape(3 * depth, 2 * (used + -used % 16), dtype=velocity.dtype)
    targets = [target[section].reshape(leaving) for section in range(sections)]
    slot = [leave[section].reshape(leaving) for section in range(sections)]

    ahead = [shape(leaving, columns), shape(TAIL, leaving), cell_shape]
    left = call(first, [slot[0], rows, state], 1, ahead, [gathered] * 2)
    messages = [shape(3 * SEGMENT, columns)] * 2 + [shape(SEGMENT, columns)] * 2
    for section in range(sections):
        more = section + 1 < sections
        body = functools.partial(depart, section, widths)
        if section == 0:
            first_turned, *sent = call(body, [*left, planes[0], *halo], 0, [turned_shape, *messages])
        else:
            sent = call(
                body, [*left, planes[section], turned[section], *pick[:2], from_low_y, from_high_y], 0, messages
            )
        xp, xm, yp, ym = (x.astype(jnp.float16) for x in sent)
        from_low_x = shifted(xp, "gx", 1)
        from_high_x = shifted(xm, "gx", -1)
        extra = halo if section == 0 else []
        if section == 0:
            turned = [first_turned]
        out = call(
            functools.partial(advance, section, widths, len(extra)),
            ([targets[section - 1], from_low_y, from_high_y] if section else [])
            + [cells, planes[section], turned[section], state, *extra],
            1 if section else 0,
            [shape(count, columns)]
            + ([turned_shape] * (sections - 1) if extra else []),
            [pltpu.VMEM((n, columns), jnp.float32) for n in (count + SPARE, coming)] if section else [],
        )
        if extra and sections > 1:
            state, *more_turned = out
            turned += more_turned
        else:
            state = out
        from_low_y = shifted(
            jnp.concatenate([yp, from_low_x[SEGMENT : 2 * SEGMENT], from_high_x[2 * SEGMENT :]], axis=0), "gy", 1
        )
        from_high_y = shifted(
            jnp.concatenate([ym, from_low_x[2 * SEGMENT :], from_high_x[SEGMENT : 2 * SEGMENT]], axis=0), "gy", -1
        )
        from_low_y, from_high_y = from_low_y.astype(jnp.float32), from_high_y.astype(jnp.float32)
        pick = picks[3 * section : 3 * section + 3]
        out = call(
            functools.partial(settle, section, more),
            [targets[section]]
            + ([slot[section + 1]] if more else [])
            + [state, from_low_x[:SEGMENT].astype(jnp.float32), from_high_x[:SEGMENT].astype(jnp.float32)]
            + ([rows, pick[2]] if more else []),
            2 if more else 1,
            [shape(count + SPARE, columns)]
            + (ahead if more else []),
            [pltpu.VMEM((2 * CAP, columns), jnp.float32)] + ([gathered] * 2 if more else []),
        )
        if more:
            state, *left = out
        else:
            state = out
    state = call(
        land,
        [targets[sections - 1], state, from_low_y],
        1,
        [shape(count + SPARE, columns)],
        [pltpu.VMEM((3 * CAP, columns), jnp.float32)],
    )
    return call(
        finish,
        [targets[sections - 1], state, from_high_y],
        1,
        [shape(count, columns)],
        [
            pltpu.VMEM((count + SPARE, columns), jnp.float32),
            pltpu.VMEM((3 * CAP, columns), jnp.float32),
            pltpu.SemaphoreType.DMA((PIECES,)),
        ],
        out_spec=hbm,
    )


def solution(mesh):
    return jax.shard_map(
        local,
        mesh=mesh,
        in_specs=(
            P(("gx", "gy"), None),
            P(None, None, "gx", "gy", None),
            P(None, None, ("gx", "gy")),
            P(None, ("gx", "gy")),
            P(None, "gx", "gy", None),
        ),
        out_specs=P(("gx", "gy"), None),
        check_vma=False,
    )
```

time: 62.7 us -> 62.6 us (level)
  the two profiles are of different devices: /device:TPU:1 before, /device:TPU:0 now
where the time goes in v2:
time: 62.6 us; the launch traced here: 62.4 us
  waiting for transfers between devices  21.4 us (34%)
  Pallas kernels  20.9 us (33%)
  starting transfers between devices  18.5 us (30%)
  local copies, waits for them, and re-layouts  0.82 us (1%)
    ppermute x16, waiting for transfers between devices, shifted(): return lax.ppermute(x, axis, [(i, (i + by) % size) for i in range(size)])  21.4 us
    pallas_call x13, Pallas kernels, call(): pl.pallas_call(body, out_shape=outs[0] if single else outs, in_specs=[spe...  20.9 us
    ppermute x16, starting transfers between devices, shifted(): return lax.ppermute(x, axis, [(i, (i + by) % size) for i in range(size)])  18.5 us
  transfers between devices with their start and end apart: 16, of which 8 were waited for; matrix products, arithmetic and copies ran while one was open for 0% of the time, Pallas kernels for 26%

profile of v2, /device:TPU:0, one launch (start us, length us, event | category | flops | bytes accessed | tf_op | source)
XLA Modules:
  0.0 62.4 jit_solution(3840992536959998261)
XLA Ops:
  0.0 0.8 %slice_bitcast_fusion = (bf16[3,3,16,128]{3,2,1,0:T(8,128)(2,1)S(1)}, bf16[3,3,16,128]{3,2,1,0:T(8,128)(2,1)S(1)}) fusion(bf16[3,3,16,16,128]{4,3,2,1,0:T(8,128)(2,1)} %refs_0_.1), kind=kLoop, calls=%fused_computation.8 | loop fusion | bytes 147456 | tf_op jit(solution)/shard_map/squeeze | solution.py:426
  0.8 6.0 %collective-permute-start.1 = (bf16[3,3,16,128]{3,2,1,0:T(8,128)(2,1)S(1)}, bf16[3,3,16,128]{3,2,1,0:T(8,128)(2,1)S(1)}, u32[]{:S(2)}, u32[]{:S(2)}) collective-permute-start(bf16[3,3,16,128]{3,2,1,0:T(8,128)(2,1)S(1)} %get-tuple-element.91), channel_id=1, source_target_pairs={{0,28},{4,0},{8,4},{12,8},{16,12},{20,16},{24,20},{28,24},{1,29},{... | collective-permute-start | bytes 110600 | tf_op jit(solution)/shard_map/ppermute | solution.py:37
  6.8 2.6 %shard_map.55 = (f32[2048,128]{1,0:T(8,128)S(1)}, s32[3,3,2048]{2,1,0:T(4,128)S(1)}, bf16[3,3,16,128]{3,2,1,0:T(8,128)(2,1)S(1)}, bf16[3,3,16,128]{3,2,1,0:T(8,1...) custom-call(bf16[3,3,16,16,128]{4,3,2,1,0:T(8,128)(2,1)} %refs_0_.1,, ...), custom_call_target="tpu_custom_call" | custom-call | tf_op jit(solution)/shard_map/pallas_call | solution.py:406
  9.4 4.0 %collective-permute-done.refs_4_ = bf16[3,3,16,128]{3,2,1,0:T(8,128)(2,1)S(1)} collective-permute-done((bf16[3,3,16,128]{3,2,1,0:T(8,128)(2,1)S(1)}, bf16[3,3,16,128]{3,2,1,0:T(8,128)(2,1)S(1)}, u32[]{:S(2)}, u32[]{:S(2)}) %collective-permute-start) | collective-permute-done | bytes 36896 | tf_op jit(solution)/shard_map/ppermute | solution.py:37
  13.6 0.5 collective-permute-start.2
  14.1 1.5 %shard_map.56 = (f32[512,128]{1,0:T(8,128)S(1)}, f32[8,512]{1,0:T(8,128)S(1)}, s32[3,512]{1,0:T(4,128)S(1)}) custom-call(s32[512]{0:T(512)S(1)} %bitcast.23, f32[2048,128]{1,0:T(8,128)S(1)} %get-tuple-element.52.refs_1_.refs_5_, f32[2048,128]{1,0:T(8,128)S(1)} %get-tuple-element.53.refs_2_.refs_3_), custom_call_target="tpu_custom_call" | custom-call | tf_op jit(solution)/shard_map/pallas_call | solution.py:406
  15.6 2.2 %collective-permute-done.2.refs_6_ = bf16[3,3,18,128]{3,2,1,0:T(8,128)(2,1)S(1)} collective-permute-done((bf16[3,3,18,128]{3,2,1,0:T(8,128)(2,1)S(1)}, bf16[3,3,18,128]{3,2,1,0:T(8,128)(2,1)S(1)}, u32[]{:S(2)}, u32[]{:S(2)}) %collective-permute-start.2) | collective-permute-done | bytes 41504 | tf_op jit(solution)/shard_map/ppermute | solution.py:37
  17.8 0.7 %shard_map.57 = (bf16[384,160]{1,0:T(8,128)(2,1)S(1)}, f32[216,128]{1,0:T(8,128)S(1)}, f32[216,128]{1,0:T(8,128)S(1)}, f32[72,128]{1,0:T(8,128)S(1)}, f32[72,128]{1,0:T(8,128)S(1)}) custom-call(f32[512,128]{1,0:T(8,128)S(1)} %get-tuple-element.54.refs_0_, f32[8,512]{1,0:T(8,128)S(1)} %get-tuple-element.55.refs_1_, s32[3,512]{1,0:T(4,128)S(1)} %get-tuple-element.56.refs_2_, ...), custom_call_target="tpu_custom_call" | custom-call | tf_op jit(solution)/shard_map/pallas_call | solution.py:406
  18.5 0.8 %collective-permute-start.5 = (f16[216,128]{1,0:T(8,128)(2,1)S(1)}, f16[216,128]{1,0:T(8,128)(2,1)S(1)}, u32[]{:S(2)}, u32[]{:S(2)}) collective-permute-start(f16[216,128]{1,0:T(8,128)(2,1)S(1)} %convert_element_type.74), channel_id=1, source_target_pairs={{0,28},{4,0},{8,4},{12,8},{16,12},{20,16},{24,20},{28,24},{1,29},{... | collective-permute-start | bytes 165896 | tf_op jit(solution)/shard_map/ppermute | solution.py:37
  19.3 1.3 %collective-permute-start.4 = (f16[216,128]{1,0:T(8,128)(2,1)S(1)}, f16[216,128]{1,0:T(8,128)(2,1)S(1)}, u32[]{:S(2)}, u32[]{:S(2)}) collective-permute-start(f16[216,128]{1,0:T(8,128)(2,1)S(1)} %convert_element_type.72), channel_id=1, source_target_pairs={{0,4},{4,8},{8,12},{12,16},{16,20},{20,24},{24,28},{28,0},{1,5},{5... | collective-permute-start | bytes 165896 | tf_op jit(solution)/shard_map/ppermute | solution.py:37
  20.6 2.0 %collective-permute-done.5 = f16[216,128]{1,0:T(8,128)(2,1)S(1)} collective-permute-done((f16[216,128]{1,0:T(8,128)(2,1)S(1)}, f16[216,128]{1,0:T(8,128)(2,1)S(1)}, u32[]{:S(2)}, u32[]{:S(2)}) %collective-permute-start.5) | collective-permute-done | bytes 55328 | tf_op jit(solution)/shard_map/ppermute | solution.py:37
  22.7 3.5 %collective-permute-done.4 = f16[216,128]{1,0:T(8,128)(2,1)S(1)} collective-permute-done((f16[216,128]{1,0:T(8,128)(2,1)S(1)}, f16[216,128]{1,0:T(8,128)(2,1)S(1)}, u32[]{:S(2)}, u32[]{:S(2)}) %collective-permute-start.4) | collective-permute-done | bytes 55328 | tf_op jit(solution)/shard_map/ppermute | solution.py:37
  26.3 1.8 %collective-permute-start.7 = (f16[216,128]{1,0:T(8,128)(2,1)S(1)}, f16[216,128]{1,0:T(8,128)(2,1)S(1)}, u32[]{:S(2)}, u32[]{:S(2)}) collective-permute-start(f16[216,128]{1,0:T(8,128)(2,1)S(1)} %pad_maximum_fusion.3), channel_id=1, source_target_pairs={{0,3},{1,0},{2,1},{3,2},{4,7},{5,4},{6,5},{7,6},{8,11},{9,8},{10,9... | collective-permute-start | bytes 165896 | tf_op jit(solution)/shard_map/ppermute | solution.py:37
  28.1 1.7 %shard_map.58 = (f32[2048,128]{1,0:T(8,128)S(1)}, bf16[384,160]{1,0:T(8,128)(2,1)S(1)}, bf16[384,160]{1,0:T(8,128)(2,1)S(1)}) custom-call(s32[3,3,2048]{2,1,0:T(4,128)S(1)} %get-tuple-element.50.refs_0_.refs_3_, bf16[384,256]{1,0:T(8,128)(2,1)S(1)} %get-tuple-element.51.refs_3_.refs_1_, bf16[384,160]{1,0:T(8,128)(2,1)S(1)} %get-tuple-element.59.refs_2_, ...), custom_call_target="tpu_custom_call" | custom-call | tf_op jit(solution)/shard_map/pallas_call | solution.py:406
  29.9 1.6 %shard_map.59 = (f32[2056,128]{1,0:T(8,128)S(1)}, f32[512,128]{1,0:T(8,128)S(1)}, f32[8,512]{1,0:T(8,128)S(1)}, s32[3,512]{1,0:T(4,128)S(1)}) custom-call(s32[512]{0:T(512)S(1)} %bitcast.19, s32[512]{0:T(512)S(1)} %bitcast.22, f32[2048,128]{1,0:T(8,128)S(1)} %get-tuple-element.60.refs_2_, f32[72,128]{1,0:T(8,128)S(1)} %get-tuple-element.107.refs_3_, ...), custom_call_target="tpu_custom_call" | custom-call | tf_op jit(solution)/shard_map/pallas_call | solution.py:406
  31.6 0.9 %shard_map.60 = (f32[216,128]{1,0:T(8,128)S(1)}, f32[216,128]{1,0:T(8,128)S(1)}, f32[72,128]{1,0:T(8,128)S(1)}, f32[72,128]{1,0:T(8,128)S(1)}) custom-call(f32[512,128]{1,0:T(8,128)S(1)} %get-tuple-element.64.refs_0_, f32[8,512]{1,0:T(8,128)S(1)} %get-tuple-element.65.refs_1_, s32[3,512]{1,0:T(4,128)S(1)} %get-tuple-element.66.refs_2_, ...), custom_call_target="tpu_custom_call" | custom-call | tf_op jit(solution)/shard_map/pallas_call | solution.py:406
  32.5 0.1 collective-permute-start.9
  32.7 2.1 %collective-permute-start.8 = (f16[216,128]{1,0:T(8,128)(2,1)S(1)}, f16[216,128]{1,0:T(8,128)(2,1)S(1)}, u32[]{:S(2)}, u32[]{:S(2)}) collective-permute-start(f16[216,128]{1,0:T(8,128)(2,1)S(1)} %convert_element_type.81), channel_id=1, source_target_pairs={{0,4},{4,8},{8,12},{12,16},{16,20},{20,24},{24,28},{28,0},{1,5},{5... | collective-permute-start | bytes 165896 | tf_op jit(solution)/shard_map/ppermute | solution.py:37
  34.7 2.0 %collective-permute-done.9 = f16[216,128]{1,0:T(8,128)(2,1)S(1)} collective-permute-done((f16[216,128]{1,0:T(8,128)(2,1)S(1)}, f16[216,128]{1,0:T(8,128)(2,1)S(1)}, u32[]{:S(2)}, u32[]{:S(2)}) %collective-permute-start.9) | collective-permute-done | bytes 55328 | tf_op jit(solution)/shard_map/ppermute | solution.py:37
  36.8 2.8 %collective-permute-done.8 = f16[216,128]{1,0:T(8,128)(2,1)S(1)} collective-permute-done((f16[216,128]{1,0:T(8,128)(2,1)S(1)}, f16[216,128]{1,0:T(8,128)(2,1)S(1)}, u32[]{:S(2)}, u32[]{:S(2)}) %collective-permute-start.8) | collective-permute-done | bytes 55328 | tf_op jit(solution)/shard_map/ppermute | solution.py:37
  39.7 1.8 %collective-permute-start.11 = (f16[216,128]{1,0:T(8,128)(2,1)S(1)}, f16[216,128]{1,0:T(8,128)(2,1)S(1)}, u32[]{:S(2)}, u32[]{:S(2)}) collective-permute-start(f16[216,128]{1,0:T(8,128)(2,1)S(1)} %pad_maximum_fusion.5), channel_id=1, source_target_pairs={{0,3},{1,0},{2,1},{3,2},{4,7},{5,4},{6,5},{7,6},{8,11},{9,8},{10,9... | collective-permute-start | bytes 165896 | tf_op jit(solution)/shard_map/ppermute | solution.py:37
  41.5 2.9 %shard_map.61.refs_2_ = f32[2048,128]{1,0:T(8,128)S(1)} custom-call(s32[512]{0:T(512)S(1)} %bitcast.20, f32[216,128]{1,0:T(8,128)S(1)} %convert_element_type.77.refs_7_.refs_1_, f32[216,128]{1,0:T(8,128)S(1)} %convert_element_type.79.refs_8_.refs_2_, s32[3,3,2048]{2,1,0:T(4,128)S(1)} %get-tuple-element.50.refs_0_.refs_3_, ...), custom_call_target="tpu_custom_call" | custom-call | tf_op jit(solution)/shard_map/pallas_call | solution.py:406
  44.4 1.6 %shard_map.62 = (f32[2056,128]{1,0:T(8,128)S(1)}, f32[512,128]{1,0:T(8,128)S(1)}, f32[8,512]{1,0:T(8,128)S(1)}, s32[3,512]{1,0:T(4,128)S(1)}) custom-call(s32[512]{0:T(512)S(1)} %bitcast.17, s32[512]{0:T(512)S(1)} %bitcast.21, f32[2048,128]{1,0:T(8,128)S(1)} %shard_map.61.refs_2_, f32[72,128]{1,0:T(8,128)S(1)} %get-tuple-element.102.refs_3_, ...), custom_call_target="tpu_custom_call" | custom-call | tf_op jit(solution)/shard_map/pallas_call | solution.py:406
  46.1 0.9 %shard_map.64 = (f32[216,128]{1,0:T(8,128)S(1)}, f32[216,128]{1,0:T(8,128)S(1)}, f32[72,128]{1,0:T(8,128)S(1)}, f32[72,128]{1,0:T(8,128)S(1)}) custom-call(f32[512,128]{1,0:T(8,128)S(1)} %get-tuple-element.82.refs_0_, f32[8,512]{1,0:T(8,128)S(1)} %get-tuple-element.83.refs_1_, s32[3,512]{1,0:T(4,128)S(1)} %get-tuple-element.84.refs_2_, ...), custom_call_target="tpu_custom_call" | custom-call | tf_op jit(solution)/shard_map/pallas_call | solution.py:406
  47.2 2.1 %collective-permute-start.12 = (f16[216,128]{1,0:T(8,128)(2,1)S(1)}, f16[216,128]{1,0:T(8,128)(2,1)S(1)}, u32[]{:S(2)}, u32[]{:S(2)}) collective-permute-start(f16[216,128]{1,0:T(8,128)(2,1)S(1)} %convert_element_type.88), channel_id=1, source_target_pairs={{0,4},{4,8},{8,12},{12,16},{16,20},{20,24},{24,28},{28,0},{1,5},{5... | collective-permute-start | bytes 165896 | tf_op jit(solution)/shard_map/ppermute | solution.py:37
  49.3 2.0 %collective-permute-done.13 = f16[216,128]{1,0:T(8,128)(2,1)S(1)} collective-permute-done((f16[216,128]{1,0:T(8,128)(2,1)S(1)}, f16[216,128]{1,0:T(8,128)(2,1)S(1)}, u32[]{:S(2)}, u32[]{:S(2)}) %collective-permute-start.13) | collective-permute-done | bytes 55328 | tf_op jit(solution)/shard_map/ppermute | solution.py:37
  51.3 2.8 %collective-permute-done.12 = f16[216,128]{1,0:T(8,128)(2,1)S(1)} collective-permute-done((f16[216,128]{1,0:T(8,128)(2,1)S(1)}, f16[216,128]{1,0:T(8,128)(2,1)S(1)}, u32[]{:S(2)}, u32[]{:S(2)}) %collective-permute-start.12) | collective-permute-done | bytes 55328 | tf_op jit(solution)/shard_map/ppermute | solution.py:37
  54.2 1.8 %collective-permute-start.15 = (f16[216,128]{1,0:T(8,128)(2,1)S(1)}, f16[216,128]{1,0:T(8,128)(2,1)S(1)}, u32[]{:S(2)}, u32[]{:S(2)}) collective-permute-start(f16[216,128]{1,0:T(8,128)(2,1)S(1)} %pad_maximum_fusion.7), channel_id=1, source_target_pairs={{0,3},{1,0},{2,1},{3,2},{4,7},{5,4},{6,5},{7,6},{8,11},{9,8},{10,9... | collective-permute-start | bytes 165896 | tf_op jit(solution)/shard_map/ppermute | solution.py:37
  56.0 2.9 %shard_map.63.refs_1_ = f32[2048,128]{1,0:T(8,128)S(1)} custom-call(s32[512]{0:T(512)S(1)} %bitcast.18, f32[216,128]{1,0:T(8,128)S(1)} %convert_element_type.83.refs_1_.refs_7_, f32[216,128]{1,0:T(8,128)S(1)} %convert_element_type.85.refs_2_.refs_8_, s32[3,3,2048]{2,1,0:T(4,128)S(1)} %get-tuple-element.50.refs_0_.refs_3_, ...), custom_call_target="tpu_custom_call" | custom-call | tf_op jit(solution)/shard_map/pallas_call | solution.py:406
  59.0 0.7 %shard_map.65.refs_1_ = f32[2056,128]{1,0:T(8,128)S(1)} custom-call(s32[512]{0:T(512)S(1)} %bitcast.14, f32[2048,128]{1,0:T(8,128)S(1)} %shard_map.63.refs_1_, f32[72,128]{1,0:T(8,128)S(1)} %get-tuple-element.95.refs_2_, f32[72,128]{1,0:T(8,128)S(1)} %get-tuple-element.98.refs_3_), custom_call_target="tpu_custom_call" | custom-call | tf_op jit(solution)/shard_map/pallas_call | solution.py:406
  59.7 0.8 %shard_map.66.refs_1_ = f32[2056,128]{1,0:T(8,128)S(1)} custom-call(s32[512]{0:T(512)S(1)} %bitcast.15, f32[2056,128]{1,0:T(8,128)S(1)} %shard_map.65.refs_1_, f32[216,128]{1,0:T(8,128)S(1)} %convert_element_type.93.refs_2_), custom_call_target="tpu_custom_call" | custom-call | tf_op jit(solution)/shard_map/pallas_call | solution.py:406
  60.6 1.8 %shard_map.67 = f32[2048,128]{1,0:T(8,128)} custom-call(s32[512]{0:T(512)S(1)} %bitcast.16, f32[2056,128]{1,0:T(8,128)S(1)} %shard_map.66.refs_1_, f32[216,128]{1,0:T(8,128)S(1)} %convert_element_type.95.refs_2_), custom_call_target="tpu_custom_call" | custom-call | tf_op jit(solution)/shard_map/pallas_call | solution.py:406
  (49 shorter events, 0.8 us)
Async XLA Ops:
  0.8 8.6 %collective-permute-start.1 = (bf16[3,3,16,128]{3,2,1,0:T(8,128)(2,1)S(1)}, bf16[3,3,16,128]{3,2,1,0:T(8,128)(2,1)S(1)}, u32[]{:S(2)}, u32[]{:S(2)}) collective-permute-start(bf16[3,3,16,128]{3,2,1,0:T(8,128)(2,1)S(1)} %get-tuple-element.91), channel_id=1, source_target_pairs={{0,28},{4,0},{8,4},{12,8},{16,12},{20,16},{24,20},{28,24},{1,29},{... | collective-permute-start | bytes 110600 | tf_op jit(solution)/shard_map/ppermute | solution.py:37
  6.8 6.7 %collective-permute-start = (bf16[3,3,16,128]{3,2,1,0:T(8,128)(2,1)S(1)}, bf16[3,3,16,128]{3,2,1,0:T(8,128)(2,1)S(1)}, u32[]{:S(2)}, u32[]{:S(2)}) collective-permute-start(bf16[3,3,16,128]{3,2,1,0:T(8,128)(2,1)S(1)} %get-tuple-element.92), channel_id=1, source_target_pairs={{0,4},{4,8},{8,12},{12,16},{16,20},{20,24},{24,28},{28,0},{1,5},{5... | collective-permute-start | bytes 110600 | tf_op jit(solution)/shard_map/ppermute | solution.py:37
  13.5 2.1 %collective-permute-start.3 = (bf16[3,3,18,128]{3,2,1,0:T(8,128)(2,1)S(1)}, bf16[3,3,18,128]{3,2,1,0:T(8,128)(2,1)S(1)}, u32[]{:S(2)}, u32[]{:S(2)}) collective-permute-start(bf16[3,3,18,128]{3,2,1,0:T(8,128)(2,1)S(1)} %pad_maximum_fusion.1), channel_id=1, source_target_pairs={{0,3},{1,0},{2,1},{3,2},{4,7},{5,4},{6,5},{7,6},{8,11},{9,8},{10,9... | collective-permute-start | bytes 124424 | tf_op jit(solution)/shard_map/ppermute | solution.py:37
  13.6 4.2 %collective-permute-start.2 = (bf16[3,3,18,128]{3,2,1,0:T(8,128)(2,1)S(1)}, bf16[3,3,18,128]{3,2,1,0:T(8,128)(2,1)S(1)}, u32[]{:S(2)}, u32[]{:S(2)}) collective-permute-start(bf16[3,3,18,128]{3,2,1,0:T(8,128)(2,1)S(1)} %pad_maximum_fusion), channel_id=1, source_target_pairs={{0,1},{1,2},{2,3},{3,0},{4,5},{5,6},{6,7},{7,4},{8,9},{9,10},{10,1... | collective-permute-start | bytes 124424 | tf_op jit(solution)/shard_map/ppermute | solution.py:37
  18.5 4.2 %collective-permute-start.5 = (f16[216,128]{1,0:T(8,128)(2,1)S(1)}, f16[216,128]{1,0:T(8,128)(2,1)S(1)}, u32[]{:S(2)}, u32[]{:S(2)}) collective-permute-start(f16[216,128]{1,0:T(8,128)(2,1)S(1)} %convert_element_type.74), channel_id=1, source_target_pairs={{0,28},{4,0},{8,4},{12,8},{16,12},{20,16},{24,20},{28,24},{1,29},{... | collective-permute-start | bytes 165896 | tf_op jit(solution)/shard_map/ppermute | solution.py:37
  19.3 6.9 %collective-permute-start.4 = (f16[216,128]{1,0:T(8,128)(2,1)S(1)}, f16[216,128]{1,0:T(8,128)(2,1)S(1)}, u32[]{:S(2)}, u32[]{:S(2)}) collective-permute-start(f16[216,128]{1,0:T(8,128)(2,1)S(1)} %convert_element_type.72), channel_id=1, source_target_pairs={{0,4},{4,8},{8,12},{12,16},{16,20},{20,24},{24,28},{28,0},{1,5},{5... | collective-permute-start | bytes 165896 | tf_op jit(solution)/shard_map/ppermute | solution.py:37
  26.2 5.3 %collective-permute-start.6 = (f16[216,128]{1,0:T(8,128)(2,1)S(1)}, f16[216,128]{1,0:T(8,128)(2,1)S(1)}, u32[]{:S(2)}, u32[]{:S(2)}) collective-permute-start(f16[216,128]{1,0:T(8,128)(2,1)S(1)} %pad_maximum_fusion.2), channel_id=1, source_target_pairs={{0,1},{1,2},{2,3},{3,0},{4,5},{5,6},{6,7},{7,4},{8,9},{9,10},{10,1... | collective-permute-start | bytes 165896 | tf_op jit(solution)/shard_map/ppermute | solution.py:37
  26.3 5.2 %collective-permute-start.7 = (f16[216,128]{1,0:T(8,128)(2,1)S(1)}, f16[216,128]{1,0:T(8,128)(2,1)S(1)}, u32[]{:S(2)}, u32[]{:S(2)}) collective-permute-start(f16[216,128]{1,0:T(8,128)(2,1)S(1)} %pad_maximum_fusion.3), channel_id=1, source_target_pairs={{0,3},{1,0},{2,1},{3,2},{4,7},{5,4},{6,5},{7,6},{8,11},{9,8},{10,9... | collective-permute-start | bytes 165896 | tf_op jit(solution)/shard_map/ppermute | solution.py:37
  32.5 4.2 %collective-permute-start.9 = (f16[216,128]{1,0:T(8,128)(2,1)S(1)}, f16[216,128]{1,0:T(8,128)(2,1)S(1)}, u32[]{:S(2)}, u32[]{:S(2)}) collective-permute-start(f16[216,128]{1,0:T(8,128)(2,1)S(1)} %convert_element_type.82), channel_id=1, source_target_pairs={{0,28},{4,0},{8,4},{12,8},{16,12},{20,16},{24,20},{28,24},{1,29},{... | collective-permute-start | bytes 165896 | tf_op jit(solution)/shard_map/ppermute | solution.py:37
  32.7 6.9 %collective-permute-start.8 = (f16[216,128]{1,0:T(8,128)(2,1)S(1)}, f16[216,128]{1,0:T(8,128)(2,1)S(1)}, u32[]{:S(2)}, u32[]{:S(2)}) collective-permute-start(f16[216,128]{1,0:T(8,128)(2,1)S(1)} %convert_element_type.81), channel_id=1, source_target_pairs={{0,4},{4,8},{8,12},{12,16},{16,20},{20,24},{24,28},{28,0},{1,5},{5... | collective-permute-start | bytes 165896 | tf_op jit(solution)/shard_map/ppermute | solution.py:37
  39.6 6.4 %collective-permute-start.10 = (f16[216,128]{1,0:T(8,128)(2,1)S(1)}, f16[216,128]{1,0:T(8,128)(2,1)S(1)}, u32[]{:S(2)}, u32[]{:S(2)}) collective-permute-start(f16[216,128]{1,0:T(8,128)(2,1)S(1)} %pad_maximum_fusion.4), channel_id=1, source_target_pairs={{0,1},{1,2},{2,3},{3,0},{4,5},{5,6},{6,7},{7,4},{8,9},{9,10},{10,1... | collective-permute-start | bytes 165896 | tf_op jit(solution)/shard_map/ppermute | solution.py:37
  39.7 6.4 %collective-permute-start.11 = (f16[216,128]{1,0:T(8,128)(2,1)S(1)}, f16[216,128]{1,0:T(8,128)(2,1)S(1)}, u32[]{:S(2)}, u32[]{:S(2)}) collective-permute-start(f16[216,128]{1,0:T(8,128)(2,1)S(1)} %pad_maximum_fusion.5), channel_id=1, source_target_pairs={{0,3},{1,0},{2,1},{3,2},{4,7},{5,4},{6,5},{7,6},{8,11},{9,8},{10,9... | collective-permute-start | bytes 165896 | tf_op jit(solution)/shard_map/ppermute | solution.py:37
  47.1 4.2 %collective-permute-start.13 = (f16[216,128]{1,0:T(8,128)(2,1)S(1)}, f16[216,128]{1,0:T(8,128)(2,1)S(1)}, u32[]{:S(2)}, u32[]{:S(2)}) collective-permute-start(f16[216,128]{1,0:T(8,128)(2,1)S(1)} %convert_element_type.90), channel_id=1, source_target_pairs={{0,28},{4,0},{8,4},{12,8},{16,12},{20,16},{24,20},{28,24},{1,29},{... | collective-permute-start | bytes 165896 | tf_op jit(solution)/shard_map/ppermute | solution.py:37
  47.2 6.9 %collective-permute-start.12 = (f16[216,128]{1,0:T(8,128)(2,1)S(1)}, f16[216,128]{1,0:T(8,128)(2,1)S(1)}, u32[]{:S(2)}, u32[]{:S(2)}) collective-permute-start(f16[216,128]{1,0:T(8,128)(2,1)S(1)} %convert_element_type.88), channel_id=1, source_target_pairs={{0,4},{4,8},{8,12},{12,16},{16,20},{20,24},{24,28},{28,0},{1,5},{5... | collective-permute-start | bytes 165896 | tf_op jit(solution)/shard_map/ppermute | solution.py:37
  54.2 5.5 %collective-permute-start.14 = (f16[216,128]{1,0:T(8,128)(2,1)S(1)}, f16[216,128]{1,0:T(8,128)(2,1)S(1)}, u32[]{:S(2)}, u32[]{:S(2)}) collective-permute-start(f16[216,128]{1,0:T(8,128)(2,1)S(1)} %pad_maximum_fusion.6), channel_id=1, source_target_pairs={{0,1},{1,2},{2,3},{3,0},{4,5},{5,6},{6,7},{7,4},{8,9},{9,10},{10,1... | collective-permute-start | bytes 165896 | tf_op jit(solution)/shard_map/ppermute | solution.py:37
  54.2 6.3 %collective-permute-start.15 = (f16[216,128]{1,0:T(8,128)(2,1)S(1)}, f16[216,128]{1,0:T(8,128)(2,1)S(1)}, u32[]{:S(2)}, u32[]{:S(2)}) collective-permute-start(f16[216,128]{1,0:T(8,128)(2,1)S(1)} %pad_maximum_fusion.7), channel_id=1, source_target_pairs={{0,3},{1,0},{2,1},{3,2},{4,7},{5,4},{6,5},{7,6},{8,11},{9,8},{10,9... | collective-permute-start | bytes 165896 | tf_op jit(solution)/shard_map/ppermute | solution.py:37

commit v3 on v2

--- a/solution.py
+++ b/solution.py
@@ -26,7 +26,8 @@
 TINY = 2.0**-14
 NUDGE = 0.75 * 2.0**-12
 SPARE = 8
-UNROLL = 16
+UNROLL = 64
+SHORT = 32
 VMEM_BYTES = 16 * 2**20
 LANES = 256
 PIECES = 1
@@ -37,7 +38,7 @@
     return lax.ppermute(x, axis, [(i, (i + by) % size) for i in range(size)])
 
 
-def scatter_rows(state_ref, target, arrivals):
+def scatter_rows(state_ref, target, arrivals, unroll=CAP):
     target_ref = target.wait()
     for ref, dirs in arrivals:
         for place, d in enumerate(dirs):
@@ -49,7 +50,7 @@
                 state_ref[pl.ds(slot, 1), :] = ref[pl.ds(place * CAP + t, 1), :]
                 return carry
 
-            lax.fori_loop(0, CAP, body, 0, unroll=UNROLL)
+            lax.fori_loop(0, CAP, body, 0, unroll=unroll)
 
 
 class Table:
@@ -329,7 +330,7 @@
     if section:
         work_ref[...] = state_ref[...]
         decode([(ref, place) for ref in (c_ref, d_ref) for place in range(3)], landed_ref)
-        scatter_rows(work_ref, target, ((landed_ref, FROM_YP + FROM_YM),))
+        scatter_rows(work_ref, target, ((landed_ref, FROM_YP + FROM_YM),), SHORT)
         state_ref = work_ref
     count = cells_ref.shape[2]
     for start in range(0, count, LANES):

time: 62.6 us -> 62 us (level)
  Pallas kernels: 20.9 us -> 19.8 us
    pallas_call x13, Pallas kernels: 20.9 us -> 19.8 us  [call(): pl.pallas_call(body, out_shape=outs[0] if single else outs, in_specs=[spe...]
  transfers between devices with their start and end apart: 16 -> 16, of which waited for: 8 -> 8; matrix products, arithmetic and copies ran while one was open for 0% -> 0% of each run, Pallas kernels for 26% -> 25%
where the time goes in v3:
time: 62 us; the launch traced here: 61.9 us
  waiting for transfers between devices  21.5 us (35%)
  Pallas kernels  19.8 us (32%)
  starting transfers between devices  18.7 us (30%)
  local copies, waits for them, and re-layouts  0.82 us (1%)
    ppermute x16, waiting for transfers between devices, shifted(): return lax.ppermute(x, axis, [(i, (i + by) % size) for i in range(size)])  21.5 us
    pallas_call x13, Pallas kernels, call(): pl.pallas_call(body, out_shape=outs[0] if single else outs, in_specs=[spe...  19.8 us
    ppermute x16, starting transfers between devices, shifted(): return lax.ppermute(x, axis, [(i, (i + by) % size) for i in range(size)])  18.7 us
  transfers between devices with their start and end apart: 16, of which 8 were waited for; matrix products, arithmetic and copies ran while one was open for 0% of the time, Pallas kernels for 25%

profile of v3, /device:TPU:0, one launch (start us, length us, event | category | flops | bytes accessed | tf_op | source)
XLA Modules:
  0.0 61.9 jit_solution(8740189860797024995)
XLA Ops:
  0.0 0.8 %slice_bitcast_fusion = (bf16[3,3,16,128]{3,2,1,0:T(8,128)(2,1)S(1)}, bf16[3,3,16,128]{3,2,1,0:T(8,128)(2,1)S(1)}) fusion(bf16[3,3,16,16,128]{4,3,2,1,0:T(8,128)(2,1)} %refs_0_.1), kind=kLoop, calls=%fused_computation.8 | loop fusion | bytes 147456 | tf_op jit(solution)/shard_map/squeeze | solution.py:427
  0.8 6.0 %collective-permute-start.1 = (bf16[3,3,16,128]{3,2,1,0:T(8,128)(2,1)S(1)}, bf16[3,3,16,128]{3,2,1,0:T(8,128)(2,1)S(1)}, u32[]{:S(2)}, u32[]{:S(2)}) collective-permute-start(bf16[3,3,16,128]{3,2,1,0:T(8,128)(2,1)S(1)} %get-tuple-element.91), channel_id=1, source_target_pairs={{0,28},{4,0},{8,4},{12,8},{16,12},{20,16},{24,20},{28,24},{1,29},{... | collective-permute-start | bytes 110600 | tf_op jit(solution)/shard_map/ppermute | solution.py:38
  6.8 2.6 %shard_map.55 = (f32[2048,128]{1,0:T(8,128)S(1)}, s32[3,3,2048]{2,1,0:T(4,128)S(1)}, bf16[3,3,16,128]{3,2,1,0:T(8,128)(2,1)S(1)}, bf16[3,3,16,128]{3,2,1,0:T(8,1...) custom-call(bf16[3,3,16,16,128]{4,3,2,1,0:T(8,128)(2,1)} %refs_0_.1,, ...), custom_call_target="tpu_custom_call" | custom-call | tf_op jit(solution)/shard_map/pallas_call | solution.py:407
  9.4 4.0 %collective-permute-done.refs_4_ = bf16[3,3,16,128]{3,2,1,0:T(8,128)(2,1)S(1)} collective-permute-done((bf16[3,3,16,128]{3,2,1,0:T(8,128)(2,1)S(1)}, bf16[3,3,16,128]{3,2,1,0:T(8,128)(2,1)S(1)}, u32[]{:S(2)}, u32[]{:S(2)}) %collective-permute-start) | collective-permute-done | bytes 36896 | tf_op jit(solution)/shard_map/ppermute | solution.py:38
  13.6 0.5 collective-permute-start.2
  14.1 1.3 %shard_map.56 = (f32[512,128]{1,0:T(8,128)S(1)}, f32[8,512]{1,0:T(8,128)S(1)}, s32[3,512]{1,0:T(4,128)S(1)}) custom-call(s32[512]{0:T(512)S(1)} %bitcast.23, f32[2048,128]{1,0:T(8,128)S(1)} %get-tuple-element.52.refs_1_.refs_5_, f32[2048,128]{1,0:T(8,128)S(1)} %get-tuple-element.53.refs_2_.refs_3_), custom_call_target="tpu_custom_call" | custom-call | tf_op jit(solution)/shard_map/pallas_call | solution.py:407
  15.5 2.3 %collective-permute-done.2.refs_6_ = bf16[3,3,18,128]{3,2,1,0:T(8,128)(2,1)S(1)} collective-permute-done((bf16[3,3,18,128]{3,2,1,0:T(8,128)(2,1)S(1)}, bf16[3,3,18,128]{3,2,1,0:T(8,128)(2,1)S(1)}, u32[]{:S(2)}, u32[]{:S(2)}) %collective-permute-start.2) | collective-permute-done | bytes 41504 | tf_op jit(solution)/shard_map/ppermute | solution.py:38
  17.8 0.7 %shard_map.57 = (bf16[384,160]{1,0:T(8,128)(2,1)S(1)}, f32[216,128]{1,0:T(8,128)S(1)}, f32[216,128]{1,0:T(8,128)S(1)}, f32[72,128]{1,0:T(8,128)S(1)}, f32[72,128]{1,0:T(8,128)S(1)}) custom-call(f32[512,128]{1,0:T(8,128)S(1)} %get-tuple-element.54.refs_0_, f32[8,512]{1,0:T(8,128)S(1)} %get-tuple-element.55.refs_1_, s32[3,512]{1,0:T(4,128)S(1)} %get-tuple-element.56.refs_2_, ...), custom_call_target="tpu_custom_call" | custom-call | tf_op jit(solution)/shard_map/pallas_call | solution.py:407
  18.5 0.8 %collective-permute-start.5 = (f16[216,128]{1,0:T(8,128)(2,1)S(1)}, f16[216,128]{1,0:T(8,128)(2,1)S(1)}, u32[]{:S(2)}, u32[]{:S(2)}) collective-permute-start(f16[216,128]{1,0:T(8,128)(2,1)S(1)} %convert_element_type.74), channel_id=1, source_target_pairs={{0,28},{4,0},{8,4},{12,8},{16,12},{20,16},{24,20},{28,24},{1,29},{... | collective-permute-start | bytes 165896 | tf_op jit(solution)/shard_map/ppermute | solution.py:38
  19.3 1.3 %collective-permute-start.4 = (f16[216,128]{1,0:T(8,128)(2,1)S(1)}, f16[216,128]{1,0:T(8,128)(2,1)S(1)}, u32[]{:S(2)}, u32[]{:S(2)}) collective-permute-start(f16[216,128]{1,0:T(8,128)(2,1)S(1)} %convert_element_type.72), channel_id=1, source_target_pairs={{0,4},{4,8},{8,12},{12,16},{16,20},{20,24},{24,28},{28,0},{1,5},{5... | collective-permute-start | bytes 165896 | tf_op jit(solution)/shard_map/ppermute | solution.py:38
  20.6 2.0 %collective-permute-done.5 = f16[216,128]{1,0:T(8,128)(2,1)S(1)} collective-permute-done((f16[216,128]{1,0:T(8,128)(2,1)S(1)}, f16[216,128]{1,0:T(8,128)(2,1)S(1)}, u32[]{:S(2)}, u32[]{:S(2)}) %collective-permute-start.5) | collective-permute-done | bytes 55328 | tf_op jit(solution)/shard_map/ppermute | solution.py:38
  22.7 3.5 %collective-permute-done.4 = f16[216,128]{1,0:T(8,128)(2,1)S(1)} collective-permute-done((f16[216,128]{1,0:T(8,128)(2,1)S(1)}, f16[216,128]{1,0:T(8,128)(2,1)S(1)}, u32[]{:S(2)}, u32[]{:S(2)}) %collective-permute-start.4) | collective-permute-done | bytes 55328 | tf_op jit(solution)/shard_map/ppermute | solution.py:38
  26.3 1.8 %collective-permute-start.7 = (f16[216,128]{1,0:T(8,128)(2,1)S(1)}, f16[216,128]{1,0:T(8,128)(2,1)S(1)}, u32[]{:S(2)}, u32[]{:S(2)}) collective-permute-start(f16[216,128]{1,0:T(8,128)(2,1)S(1)} %pad_maximum_fusion.3), channel_id=1, source_target_pairs={{0,3},{1,0},{2,1},{3,2},{4,7},{5,4},{6,5},{7,6},{8,11},{9,8},{10,9... | collective-permute-start | bytes 165896 | tf_op jit(solution)/shard_map/ppermute | solution.py:38
  28.1 1.7 %shard_map.58 = (f32[2048,128]{1,0:T(8,128)S(1)}, bf16[384,160]{1,0:T(8,128)(2,1)S(1)}, bf16[384,160]{1,0:T(8,128)(2,1)S(1)}) custom-call(s32[3,3,2048]{2,1,0:T(4,128)S(1)} %get-tuple-element.50.refs_0_.refs_3_, bf16[384,256]{1,0:T(8,128)(2,1)S(1)} %get-tuple-element.51.refs_3_.refs_1_, bf16[384,160]{1,0:T(8,128)(2,1)S(1)} %get-tuple-element.59.refs_2_, ...), custom_call_target="tpu_custom_call" | custom-call | tf_op jit(solution)/shard_map/pallas_call | solution.py:407
  29.9 1.4 %shard_map.59 = (f32[2056,128]{1,0:T(8,128)S(1)}, f32[512,128]{1,0:T(8,128)S(1)}, f32[8,512]{1,0:T(8,128)S(1)}, s32[3,512]{1,0:T(4,128)S(1)}) custom-call(s32[512]{0:T(512)S(1)} %bitcast.19, s32[512]{0:T(512)S(1)} %bitcast.22, f32[2048,128]{1,0:T(8,128)S(1)} %get-tuple-element.60.refs_2_, f32[72,128]{1,0:T(8,128)S(1)} %get-tuple-element.107.refs_3_, ...), custom_call_target="tpu_custom_call" | custom-call | tf_op jit(solution)/shard_map/pallas_call | solution.py:407
  31.4 0.9 %shard_map.60 = (f32[216,128]{1,0:T(8,128)S(1)}, f32[216,128]{1,0:T(8,128)S(1)}, f32[72,128]{1,0:T(8,128)S(1)}, f32[72,128]{1,0:T(8,128)S(1)}) custom-call(f32[512,128]{1,0:T(8,128)S(1)} %get-tuple-element.64.refs_0_, f32[8,512]{1,0:T(8,128)S(1)} %get-tuple-element.65.refs_1_, s32[3,512]{1,0:T(4,128)S(1)} %get-tuple-element.66.refs_2_, ...), custom_call_target="tpu_custom_call" | custom-call | tf_op jit(solution)/shard_map/pallas_call | solution.py:407
  32.3 0.1 collective-permute-start.9
  32.5 2.1 %collective-permute-start.8 = (f16[216,128]{1,0:T(8,128)(2,1)S(1)}, f16[216,128]{1,0:T(8,128)(2,1)S(1)}, u32[]{:S(2)}, u32[]{:S(2)}) collective-permute-start(f16[216,128]{1,0:T(8,128)(2,1)S(1)} %convert_element_type.81), channel_id=1, source_target_pairs={{0,4},{4,8},{8,12},{12,16},{16,20},{20,24},{24,28},{28,0},{1,5},{5... | collective-permute-start | bytes 165896 | tf_op jit(solution)/shard_map/ppermute | solution.py:38
  34.5 2.0 %collective-permute-done.9 = f16[216,128]{1,0:T(8,128)(2,1)S(1)} collective-permute-done((f16[216,128]{1,0:T(8,128)(2,1)S(1)}, f16[216,128]{1,0:T(8,128)(2,1)S(1)}, u32[]{:S(2)}, u32[]{:S(2)}) %collective-permute-start.9) | collective-permute-done | bytes 55328 | tf_op jit(solution)/shard_map/ppermute | solution.py:38
  36.6 2.8 %collective-permute-done.8 = f16[216,128]{1,0:T(8,128)(2,1)S(1)} collective-permute-done((f16[216,128]{1,0:T(8,128)(2,1)S(1)}, f16[216,128]{1,0:T(8,128)(2,1)S(1)}, u32[]{:S(2)}, u32[]{:S(2)}) %collective-permute-start.8) | collective-permute-done | bytes 55328 | tf_op jit(solution)/shard_map/ppermute | solution.py:38
  39.5 1.8 %collective-permute-start.11 = (f16[216,128]{1,0:T(8,128)(2,1)S(1)}, f16[216,128]{1,0:T(8,128)(2,1)S(1)}, u32[]{:S(2)}, u32[]{:S(2)}) collective-permute-start(f16[216,128]{1,0:T(8,128)(2,1)S(1)} %pad_maximum_fusion.5), channel_id=1, source_target_pairs={{0,3},{1,0},{2,1},{3,2},{4,7},{5,4},{6,5},{7,6},{8,11},{9,8},{10,9... | collective-permute-start | bytes 165896 | tf_op jit(solution)/shard_map/ppermute | solution.py:38
  41.3 2.9 %shard_map.61.refs_2_ = f32[2048,128]{1,0:T(8,128)S(1)} custom-call(s32[512]{0:T(512)S(1)} %bitcast.20, f32[216,128]{1,0:T(8,128)S(1)} %convert_element_type.77.refs_7_.refs_1_, f32[216,128]{1,0:T(8,128)S(1)} %convert_element_type.79.refs_8_.refs_2_, s32[3,3,2048]{2,1,0:T(4,128)S(1)} %get-tuple-element.50.refs_0_.refs_3_, ...), custom_call_target="tpu_custom_call" | custom-call | tf_op jit(solution)/shard_map/pallas_call | solution.py:407
  44.1 1.4 %shard_map.62 = (f32[2056,128]{1,0:T(8,128)S(1)}, f32[512,128]{1,0:T(8,128)S(1)}, f32[8,512]{1,0:T(8,128)S(1)}, s32[3,512]{1,0:T(4,128)S(1)}) custom-call(s32[512]{0:T(512)S(1)} %bitcast.17, s32[512]{0:T(512)S(1)} %bitcast.21, f32[2048,128]{1,0:T(8,128)S(1)} %shard_map.61.refs_2_, f32[72,128]{1,0:T(8,128)S(1)} %get-tuple-element.102.refs_3_, ...), custom_call_target="tpu_custom_call" | custom-call | tf_op jit(solution)/shard_map/pallas_call | solution.py:407
  45.6 0.9 %shard_map.64 = (f32[216,128]{1,0:T(8,128)S(1)}, f32[216,128]{1,0:T(8,128)S(1)}, f32[72,128]{1,0:T(8,128)S(1)}, f32[72,128]{1,0:T(8,128)S(1)}) custom-call(f32[512,128]{1,0:T(8,128)S(1)} %get-tuple-element.82.refs_0_, f32[8,512]{1,0:T(8,128)S(1)} %get-tuple-element.83.refs_1_, s32[3,512]{1,0:T(4,128)S(1)} %get-tuple-element.84.refs_2_, ...), custom_call_target="tpu_custom_call" | custom-call | tf_op jit(solution)/shard_map/pallas_call | solution.py:407
  46.7 2.1 %collective-permute-start.12 = (f16[216,128]{1,0:T(8,128)(2,1)S(1)}, f16[216,128]{1,0:T(8,128)(2,1)S(1)}, u32[]{:S(2)}, u32[]{:S(2)}) collective-permute-start(f16[216,128]{1,0:T(8,128)(2,1)S(1)} %convert_element_type.88), channel_id=1, source_target_pairs={{0,4},{4,8},{8,12},{12,16},{16,20},{20,24},{24,28},{28,0},{1,5},{5... | collective-permute-start | bytes 165896 | tf_op jit(solution)/shard_map/ppermute | solution.py:38
  48.8 2.0 %collective-permute-done.13 = f16[216,128]{1,0:T(8,128)(2,1)S(1)} collective-permute-done((f16[216,128]{1,0:T(8,128)(2,1)S(1)}, f16[216,128]{1,0:T(8,128)(2,1)S(1)}, u32[]{:S(2)}, u32[]{:S(2)}) %collective-permute-start.13) | collective-permute-done | bytes 55328 | tf_op jit(solution)/shard_map/ppermute | solution.py:38
  50.8 2.8 %collective-permute-done.12 = f16[216,128]{1,0:T(8,128)(2,1)S(1)} collective-permute-done((f16[216,128]{1,0:T(8,128)(2,1)S(1)}, f16[216,128]{1,0:T(8,128)(2,1)S(1)}, u32[]{:S(2)}, u32[]{:S(2)}) %collective-permute-start.12) | collective-permute-done | bytes 55328 | tf_op jit(solution)/shard_map/ppermute | solution.py:38
  53.8 2.0 %collective-permute-start.15 = (f16[216,128]{1,0:T(8,128)(2,1)S(1)}, f16[216,128]{1,0:T(8,128)(2,1)S(1)}, u32[]{:S(2)}, u32[]{:S(2)}) collective-permute-start(f16[216,128]{1,0:T(8,128)(2,1)S(1)} %pad_maximum_fusion.7), channel_id=1, source_target_pairs={{0,3},{1,0},{2,1},{3,2},{4,7},{5,4},{6,5},{7,6},{8,11},{9,8},{10,9... | collective-permute-start | bytes 165896 | tf_op jit(solution)/shard_map/ppermute | solution.py:38
  55.7 2.9 %shard_map.63.refs_1_ = f32[2048,128]{1,0:T(8,128)S(1)} custom-call(s32[512]{0:T(512)S(1)} %bitcast.18, f32[216,128]{1,0:T(8,128)S(1)} %convert_element_type.83.refs_1_.refs_7_, f32[216,128]{1,0:T(8,128)S(1)} %convert_element_type.85.refs_2_.refs_8_, s32[3,3,2048]{2,1,0:T(4,128)S(1)} %get-tuple-element.50.refs_0_.refs_3_, ...), custom_call_target="tpu_custom_call" | custom-call | tf_op jit(solution)/shard_map/pallas_call | solution.py:407
  58.6 0.7 %shard_map.65.refs_1_ = f32[2056,128]{1,0:T(8,128)S(1)} custom-call(s32[512]{0:T(512)S(1)} %bitcast.14, f32[2048,128]{1,0:T(8,128)S(1)} %shard_map.63.refs_1_, f32[72,128]{1,0:T(8,128)S(1)} %get-tuple-element.95.refs_2_, f32[72,128]{1,0:T(8,128)S(1)} %get-tuple-element.98.refs_3_), custom_call_target="tpu_custom_call" | custom-call | tf_op jit(solution)/shard_map/pallas_call | solution.py:407
  59.3 0.7 %shard_map.66.refs_1_ = f32[2056,128]{1,0:T(8,128)S(1)} custom-call(s32[512]{0:T(512)S(1)} %bitcast.15, f32[2056,128]{1,0:T(8,128)S(1)} %shard_map.65.refs_1_, f32[216,128]{1,0:T(8,128)S(1)} %convert_element_type.93.refs_2_), custom_call_target="tpu_custom_call" | custom-call | tf_op jit(solution)/shard_map/pallas_call | solution.py:407
  60.0 1.7 %shard_map.67 = f32[2048,128]{1,0:T(8,128)} custom-call(s32[512]{0:T(512)S(1)} %bitcast.16, f32[2056,128]{1,0:T(8,128)S(1)} %shard_map.66.refs_1_, f32[216,128]{1,0:T(8,128)S(1)} %convert_element_type.95.refs_2_), custom_call_target="tpu_custom_call" | custom-call | tf_op jit(solution)/shard_map/pallas_call | solution.py:407
  (49 shorter events, 0.8 us)
Async XLA Ops:
  0.8 8.6 %collective-permute-start.1 = (bf16[3,3,16,128]{3,2,1,0:T(8,128)(2,1)S(1)}, bf16[3,3,16,128]{3,2,1,0:T(8,128)(2,1)S(1)}, u32[]{:S(2)}, u32[]{:S(2)}) collective-permute-start(bf16[3,3,16,128]{3,2,1,0:T(8,128)(2,1)S(1)} %get-tuple-element.91), channel_id=1, source_target_pairs={{0,28},{4,0},{8,4},{12,8},{16,12},{20,16},{24,20},{28,24},{1,29},{... | collective-permute-start | bytes 110600 | tf_op jit(solution)/shard_map/ppermute | solution.py:38
  6.8 6.7 %collective-permute-start = (bf16[3,3,16,128]{3,2,1,0:T(8,128)(2,1)S(1)}, bf16[3,3,16,128]{3,2,1,0:T(8,128)(2,1)S(1)}, u32[]{:S(2)}, u32[]{:S(2)}) collective-permute-start(bf16[3,3,16,128]{3,2,1,0:T(8,128)(2,1)S(1)} %get-tuple-element.92), channel_id=1, source_target_pairs={{0,4},{4,8},{8,12},{12,16},{16,20},{20,24},{24,28},{28,0},{1,5},{5... | collective-permute-start | bytes 110600 | tf_op jit(solution)/shard_map/ppermute | solution.py:38
  13.5 2.0 %collective-permute-start.3 = (bf16[3,3,18,128]{3,2,1,0:T(8,128)(2,1)S(1)}, bf16[3,3,18,128]{3,2,1,0:T(8,128)(2,1)S(1)}, u32[]{:S(2)}, u32[]{:S(2)}) collective-permute-start(bf16[3,3,18,128]{3,2,1,0:T(8,128)(2,1)S(1)} %pad_maximum_fusion.1), channel_id=1, source_target_pairs={{0,3},{1,0},{2,1},{3,2},{4,7},{5,4},{6,5},{7,6},{8,11},{9,8},{10,9... | collective-permute-start | bytes 124424 | tf_op jit(solution)/shard_map/ppermute | solution.py:38
  13.6 4.2 %collective-permute-start.2 = (bf16[3,3,18,128]{3,2,1,0:T(8,128)(2,1)S(1)}, bf16[3,3,18,128]{3,2,1,0:T(8,128)(2,1)S(1)}, u32[]{:S(2)}, u32[]{:S(2)}) collective-permute-start(bf16[3,3,18,128]{3,2,1,0:T(8,128)(2,1)S(1)} %pad_maximum_fusion), channel_id=1, source_target_pairs={{0,1},{1,2},{2,3},{3,0},{4,5},{5,6},{6,7},{7,4},{8,9},{9,10},{10,1... | collective-permute-start | bytes 124424 | tf_op jit(solution)/shard_map/ppermute | solution.py:38
  18.5 4.2 %collective-permute-start.5 = (f16[216,128]{1,0:T(8,128)(2,1)S(1)}, f16[216,128]{1,0:T(8,128)(2,1)S(1)}, u32[]{:S(2)}, u32[]{:S(2)}) collective-permute-start(f16[216,128]{1,0:T(8,128)(2,1)S(1)} %convert_element_type.74), channel_id=1, source_target_pairs={{0,28},{4,0},{8,4},{12,8},{16,12},{20,16},{24,20},{28,24},{1,29},{... | collective-permute-start | bytes 165896 | tf_op jit(solution)/shard_map/ppermute | solution.py:38
  19.3 6.9 %collective-permute-start.4 = (f16[216,128]{1,0:T(8,128)(2,1)S(1)}, f16[216,128]{1,0:T(8,128)(2,1)S(1)}, u32[]{:S(2)}, u32[]{:S(2)}) collective-permute-start(f16[216,128]{1,0:T(8,128)(2,1)S(1)} %convert_element_type.72), channel_id=1, source_target_pairs={{0,4},{4,8},{8,12},{12,16},{16,20},{20,24},{24,28},{28,0},{1,5},{5... | collective-permute-start | bytes 165896 | tf_op jit(solution)/shard_map/ppermute | solution.py:38
  26.2 5.1 %collective-permute-start.6 = (f16[216,128]{1,0:T(8,128)(2,1)S(1)}, f16[216,128]{1,0:T(8,128)(2,1)S(1)}, u32[]{:S(2)}, u32[]{:S(2)}) collective-permute-start(f16[216,128]{1,0:T(8,128)(2,1)S(1)} %pad_maximum_fusion.2), channel_id=1, source_target_pairs={{0,1},{1,2},{2,3},{3,0},{4,5},{5,6},{6,7},{7,4},{8,9},{9,10},{10,1... | collective-permute-start | bytes 165896 | tf_op jit(solution)/shard_map/ppermute | solution.py:38
  26.3 5.0 %collective-permute-start.7 = (f16[216,128]{1,0:T(8,128)(2,1)S(1)}, f16[216,128]{1,0:T(8,128)(2,1)S(1)}, u32[]{:S(2)}, u32[]{:S(2)}) collective-permute-start(f16[216,128]{1,0:T(8,128)(2,1)S(1)} %pad_maximum_fusion.3), channel_id=1, source_target_pairs={{0,3},{1,0},{2,1},{3,2},{4,7},{5,4},{6,5},{7,6},{8,11},{9,8},{10,9... | collective-permute-start | bytes 165896 | tf_op jit(solution)/shard_map/ppermute | solution.py:38
  32.3 4.2 %collective-permute-start.9 = (f16[216,128]{1,0:T(8,128)(2,1)S(1)}, f16[216,128]{1,0:T(8,128)(2,1)S(1)}, u32[]{:S(2)}, u32[]{:S(2)}) collective-permute-start(f16[216,128]{1,0:T(8,128)(2,1)S(1)} %convert_element_type.82), channel_id=1, source_target_pairs={{0,28},{4,0},{8,4},{12,8},{16,12},{20,16},{24,20},{28,24},{1,29},{... | collective-permute-start | bytes 165896 | tf_op jit(solution)/shard_map/ppermute | solution.py:38
  32.5 6.9 %collective-permute-start.8 = (f16[216,128]{1,0:T(8,128)(2,1)S(1)}, f16[216,128]{1,0:T(8,128)(2,1)S(1)}, u32[]{:S(2)}, u32[]{:S(2)}) collective-permute-start(f16[216,128]{1,0:T(8,128)(2,1)S(1)} %convert_element_type.81), channel_id=1, source_target_pairs={{0,4},{4,8},{8,12},{12,16},{16,20},{20,24},{24,28},{28,0},{1,5},{5... | collective-permute-start | bytes 165896 | tf_op jit(solution)/shard_map/ppermute | solution.py:38
  39.4 6.2 %collective-permute-start.10 = (f16[216,128]{1,0:T(8,128)(2,1)S(1)}, f16[216,128]{1,0:T(8,128)(2,1)S(1)}, u32[]{:S(2)}, u32[]{:S(2)}) collective-permute-start(f16[216,128]{1,0:T(8,128)(2,1)S(1)} %pad_maximum_fusion.4), channel_id=1, source_target_pairs={{0,1},{1,2},{2,3},{3,0},{4,5},{5,6},{6,7},{7,4},{8,9},{9,10},{10,1... | collective-permute-start | bytes 165896 | tf_op jit(solution)/shard_map/ppermute | solution.py:38
  39.5 6.1 %collective-permute-start.11 = (f16[216,128]{1,0:T(8,128)(2,1)S(1)}, f16[216,128]{1,0:T(8,128)(2,1)S(1)}, u32[]{:S(2)}, u32[]{:S(2)}) collective-permute-start(f16[216,128]{1,0:T(8,128)(2,1)S(1)} %pad_maximum_fusion.5), channel_id=1, source_target_pairs={{0,3},{1,0},{2,1},{3,2},{4,7},{5,4},{6,5},{7,6},{8,11},{9,8},{10,9... | collective-permute-start | bytes 165896 | tf_op jit(solution)/shard_map/ppermute | solution.py:38
  46.6 4.2 %collective-permute-start.13 = (f16[216,128]{1,0:T(8,128)(2,1)S(1)}, f16[216,128]{1,0:T(8,128)(2,1)S(1)}, u32[]{:S(2)}, u32[]{:S(2)}) collective-permute-start(f16[216,128]{1,0:T(8,128)(2,1)S(1)} %convert_element_type.90), channel_id=1, source_target_pairs={{0,28},{4,0},{8,4},{12,8},{16,12},{20,16},{24,20},{28,24},{1,29},{... | collective-permute-start | bytes 165896 | tf_op jit(solution)/shard_map/ppermute | solution.py:38
  46.7 6.9 %collective-permute-start.12 = (f16[216,128]{1,0:T(8,128)(2,1)S(1)}, f16[216,128]{1,0:T(8,128)(2,1)S(1)}, u32[]{:S(2)}, u32[]{:S(2)}) collective-permute-start(f16[216,128]{1,0:T(8,128)(2,1)S(1)} %convert_element_type.88), channel_id=1, source_target_pairs={{0,4},{4,8},{8,12},{12,16},{16,20},{20,24},{24,28},{28,0},{1,5},{5... | collective-permute-start | bytes 165896 | tf_op jit(solution)/shard_map/ppermute | solution.py:38
  53.7 5.6 %collective-permute-start.14 = (f16[216,128]{1,0:T(8,128)(2,1)S(1)}, f16[216,128]{1,0:T(8,128)(2,1)S(1)}, u32[]{:S(2)}, u32[]{:S(2)}) collective-permute-start(f16[216,128]{1,0:T(8,128)(2,1)S(1)} %pad_maximum_fusion.6), channel_id=1, source_target_pairs={{0,1},{1,2},{2,3},{3,0},{4,5},{5,6},{6,7},{7,4},{8,9},{9,10},{10,1... | collective-permute-start | bytes 165896 | tf_op jit(solution)/shard_map/ppermute | solution.py:38
  53.8 6.2 %collective-permute-start.15 = (f16[216,128]{1,0:T(8,128)(2,1)S(1)}, f16[216,128]{1,0:T(8,128)(2,1)S(1)}, u32[]{:S(2)}, u32[]{:S(2)}) collective-permute-start(f16[216,128]{1,0:T(8,128)(2,1)S(1)} %pad_maximum_fusion.7), channel_id=1, source_target_pairs={{0,3},{1,0},{2,1},{3,2},{4,7},{5,4},{6,5},{7,6},{8,11},{9,8},{10,9... | collective-permute-start | bytes 165896 | tf_op jit(solution)/shard_map/ppermute | solution.py:38

commit v4 on v3

--- a/solution.py
+++ b/solution.py
@@ -27,9 +27,10 @@
 NUDGE = 0.75 * 2.0**-12
 SPARE = 8
 UNROLL = 64
-SHORT = 32
+SHORT = 64
 VMEM_BYTES = 16 * 2**20
 LANES = 256
+LATER = (0, 2, 4)
 PIECES = 1
 
 
@@ -335,23 +336,34 @@
     count = cells_ref.shape[2]
     for start in range(0, count, LANES):
         rows = state_ref[start : start + LANES, :]
+        out_ref[start : start + LANES, :] = rows
+        if start < LATER[section] * LANES:
+            continue
         cell = cells_ref[section, :, start : start + LANES]
         new = advanced(section, rows.T, cell, plane_ref[...], turned_ref[...], widths)
-        out_ref[start : start + LANES, :] = rows
         out_ref[start : start + LANES, 0:6] = new.T[:, 0:6]
     for n, next_ref in enumerate(turned_refs):
         turn_rim(section + 1 + n, halo, next_ref)
 
 
-def settle(section, more, target, *refs):
+def settle(section, widths, more, target, *refs):
     if more:
-        slot, old_ref, a_ref, b_ref, rows_ref, keep_ref = refs[:6]
-        state_ref, code_ref, columns_ref, cell_ref = refs[6:10]
-        landed_ref, left_ref, part_ref = refs[10:]
+        slot, *refs = refs
+    if LATER[section]:
+        cells_ref, plane_ref, turned_ref, *refs = refs
+    if more:
+        old_ref, a_ref, b_ref, rows_ref, keep_ref = refs[:5]
+        state_ref, code_ref, columns_ref, cell_ref = refs[5:9]
+        landed_ref, left_ref, part_ref = refs[9:]
     else:
         old_ref, a_ref, b_ref, state_ref, landed_ref = refs
     decode([(a_ref, 0), (b_ref, 0)], landed_ref)
     state_ref[0 : old_ref.shape[0], :] = old_ref[...]
+    for start in range(0, LATER[section] * LANES, LANES):
+        columns = old_ref[start : start + LANES, :].T
+        cell = cells_ref[section, :, start : start + LANES]
+        new = advanced(section, columns, cell, plane_ref[...], turned_ref[...], widths)
+        state_ref[start : start + LANES, 0:6] = new.T[:, 0:6]
     scatter_rows(state_ref, target, ((landed_ref, (FROM_XP[0], FROM_XM[0])),))
     if more:
         gather_rows(slot, (left_ref, state_ref), (part_ref, rows_ref))
@@ -499,9 +511,10 @@
         from_low_y, from_high_y = from_low_y.astype(jnp.float32), from_high_y.astype(jnp.float32)
         pick = picks[3 * section : 3 * section + 3]
         out = call(
-            functools.partial(settle, section, more),
+            functools.partial(settle, section, widths, more),
             [targets[section]]
             + ([slot[section + 1]] if more else [])
+            + ([cells, planes[section], turned[section]] if LATER[section] else [])
             + [state, from_low_x[:SEGMENT].astype(jnp.float32), from_high_x[:SEGMENT].astype(jnp.float32)]
             + ([rows, pick[2]] if more else []),
             2 if more else 1,

time: 62 us -> 62 us (level)
  no operation moved by 1% of the time
where the time goes in v4:
time: 62 us; the launch traced here: 61.8 us
  waiting for transfers between devices  21.5 us (35%)
  Pallas kernels  19.7 us (32%)
  starting transfers between devices  18.7 us (30%)
  local copies, waits for them, and re-layouts  0.82 us (1%)
    ppermute x16, waiting for transfers between devices, shifted(): return lax.ppermute(x, axis, [(i, (i + by) % size) for i in range(size)])  21.5 us
    pallas_call x13, Pallas kernels, call(): pl.pallas_call(body, out_shape=outs[0] if single else outs, in_specs=[spe...  19.7 us
    ppermute x16, starting transfers between devices, shifted(): return lax.ppermute(x, axis, [(i, (i + by) % size) for i in range(size)])  18.7 us
  transfers between devices with their start and end apart: 16, of which 8 were waited for; matrix products, arithmetic and copies ran while one was open for 0% of the time, Pallas kernels for 25%

profile of v4, /device:TPU:0, one launch (start us, length us, event | category | flops | bytes accessed | tf_op | source)
XLA Modules:
  0.0 61.8 jit_solution(485590310389082035)
XLA Ops:
  0.0 0.8 %slice_bitcast_fusion = (bf16[3,3,16,128]{3,2,1,0:T(8,128)(2,1)S(1)}, bf16[3,3,16,128]{3,2,1,0:T(8,128)(2,1)S(1)}) fusion(bf16[3,3,16,16,128]{4,3,2,1,0:T(8,128)(2,1)} %refs_0_.1), kind=kLoop, calls=%fused_computation.8 | loop fusion | bytes 147456 | tf_op jit(solution)/shard_map/squeeze | solution.py:439
  0.8 6.0 %collective-permute-start.1 = (bf16[3,3,16,128]{3,2,1,0:T(8,128)(2,1)S(1)}, bf16[3,3,16,128]{3,2,1,0:T(8,128)(2,1)S(1)}, u32[]{:S(2)}, u32[]{:S(2)}) collective-permute-start(bf16[3,3,16,128]{3,2,1,0:T(8,128)(2,1)S(1)} %get-tuple-element.91), channel_id=1, source_target_pairs={{0,28},{4,0},{8,4},{12,8},{16,12},{20,16},{24,20},{28,24},{1,29},{... | collective-permute-start | bytes 110600 | tf_op jit(solution)/shard_map/ppermute | solution.py:39
  6.8 2.6 %shard_map.55 = (f32[2048,128]{1,0:T(8,128)S(1)}, s32[3,3,2048]{2,1,0:T(4,128)S(1)}, bf16[3,3,16,128]{3,2,1,0:T(8,128)(2,1)S(1)}, bf16[3,3,16,128]{3,2,1,0:T(8,1...) custom-call(bf16[3,3,16,16,128]{4,3,2,1,0:T(8,128)(2,1)} %refs_0_.1,, ...), custom_call_target="tpu_custom_call" | custom-call | tf_op jit(solution)/shard_map/pallas_call | solution.py:419
  9.4 4.0 %collective-permute-done.refs_4_ = bf16[3,3,16,128]{3,2,1,0:T(8,128)(2,1)S(1)} collective-permute-done((bf16[3,3,16,128]{3,2,1,0:T(8,128)(2,1)S(1)}, bf16[3,3,16,128]{3,2,1,0:T(8,128)(2,1)S(1)}, u32[]{:S(2)}, u32[]{:S(2)}) %collective-permute-start) | collective-permute-done | bytes 36896 | tf_op jit(solution)/shard_map/ppermute | solution.py:39
  13.6 0.5 collective-permute-start.2
  14.1 1.3 %shard_map.56 = (f32[512,128]{1,0:T(8,128)S(1)}, f32[8,512]{1,0:T(8,128)S(1)}, s32[3,512]{1,0:T(4,128)S(1)}) custom-call(s32[512]{0:T(512)S(1)} %bitcast.22, f32[2048,128]{1,0:T(8,128)S(1)} %get-tuple-element.53.refs_1_.refs_5_.refs_8_, f32[2048,128]{1,0:T(8,128)S(1)} %get-tuple-element.54.refs_2_.refs_3_), custom_call_target="tpu_custom_call" | custom-call | tf_op jit(solution)/shard_map/pallas_call | solution.py:419
  15.5 2.3 %collective-permute-done.2.refs_6_ = bf16[3,3,18,128]{3,2,1,0:T(8,128)(2,1)S(1)} collective-permute-done((bf16[3,3,18,128]{3,2,1,0:T(8,128)(2,1)S(1)}, bf16[3,3,18,128]{3,2,1,0:T(8,128)(2,1)S(1)}, u32[]{:S(2)}, u32[]{:S(2)}) %collective-permute-start.2) | collective-permute-done | bytes 41504 | tf_op jit(solution)/shard_map/ppermute | solution.py:39
  17.8 0.7 %shard_map.57 = (bf16[384,160]{1,0:T(8,128)(2,1)S(1)}, f32[216,128]{1,0:T(8,128)S(1)}, f32[216,128]{1,0:T(8,128)S(1)}, f32[72,128]{1,0:T(8,128)S(1)}, f32[72,128]{1,0:T(8,128)S(1)}) custom-call(f32[512,128]{1,0:T(8,128)S(1)} %get-tuple-element.55.refs_0_, f32[8,512]{1,0:T(8,128)S(1)} %get-tuple-element.56.refs_1_, s32[3,512]{1,0:T(4,128)S(1)} %get-tuple-element.57.refs_2_, ...), custom_call_target="tpu_custom_call" | custom-call | tf_op jit(solution)/shard_map/pallas_call | solution.py:419
  18.5 0.8 %collective-permute-start.5 = (f16[216,128]{1,0:T(8,128)(2,1)S(1)}, f16[216,128]{1,0:T(8,128)(2,1)S(1)}, u32[]{:S(2)}, u32[]{:S(2)}) collective-permute-start(f16[216,128]{1,0:T(8,128)(2,1)S(1)} %convert_element_type.74), channel_id=1, source_target_pairs={{0,28},{4,0},{8,4},{12,8},{16,12},{20,16},{24,20},{28,24},{1,29},{... | collective-permute-start | bytes 165896 | tf_op jit(solution)/shard_map/ppermute | solution.py:39
  19.3 1.4 %collective-permute-start.4 = (f16[216,128]{1,0:T(8,128)(2,1)S(1)}, f16[216,128]{1,0:T(8,128)(2,1)S(1)}, u32[]{:S(2)}, u32[]{:S(2)}) collective-permute-start(f16[216,128]{1,0:T(8,128)(2,1)S(1)} %convert_element_type.72), channel_id=1, source_target_pairs={{0,4},{4,8},{8,12},{12,16},{16,20},{20,24},{24,28},{28,0},{1,5},{5... | collective-permute-start | bytes 165896 | tf_op jit(solution)/shard_map/ppermute | solution.py:39
  20.6 2.0 %collective-permute-done.5 = f16[216,128]{1,0:T(8,128)(2,1)S(1)} collective-permute-done((f16[216,128]{1,0:T(8,128)(2,1)S(1)}, f16[216,128]{1,0:T(8,128)(2,1)S(1)}, u32[]{:S(2)}, u32[]{:S(2)}) %collective-permute-start.5) | collective-permute-done | bytes 55328 | tf_op jit(solution)/shard_map/ppermute | solution.py:39
  22.7 3.5 %collective-permute-done.4 = f16[216,128]{1,0:T(8,128)(2,1)S(1)} collective-permute-done((f16[216,128]{1,0:T(8,128)(2,1)S(1)}, f16[216,128]{1,0:T(8,128)(2,1)S(1)}, u32[]{:S(2)}, u32[]{:S(2)}) %collective-permute-start.4) | collective-permute-done | bytes 55328 | tf_op jit(solution)/shard_map/ppermute | solution.py:39
  26.3 1.8 %collective-permute-start.7 = (f16[216,128]{1,0:T(8,128)(2,1)S(1)}, f16[216,128]{1,0:T(8,128)(2,1)S(1)}, u32[]{:S(2)}, u32[]{:S(2)}) collective-permute-start(f16[216,128]{1,0:T(8,128)(2,1)S(1)} %pad_maximum_fusion.3), channel_id=1, source_target_pairs={{0,3},{1,0},{2,1},{3,2},{4,7},{5,4},{6,5},{7,6},{8,11},{9,8},{10,9... | collective-permute-start | bytes 165896 | tf_op jit(solution)/shard_map/ppermute | solution.py:39
  28.1 1.7 %shard_map.58 = (f32[2048,128]{1,0:T(8,128)S(1)}, bf16[384,160]{1,0:T(8,128)(2,1)S(1)}, bf16[384,160]{1,0:T(8,128)(2,1)S(1)}) custom-call(s32[3,3,2048]{2,1,0:T(4,128)S(1)} %get-tuple-element.49.refs_0_.refs_3_.refs_2_.refs_1_, bf16[384,256]{1,0:T(8,128)(2,1)S(1)} %get-tuple-element.51.refs_3_.refs_1_, bf16[384,160]{1,0:T(8,128)(2,1)S(1)} %get-tuple-element.60.refs_2_, ...), custom_call_target="tpu_custom_call" | custom-call | tf_op jit(solution)/shard_map/pallas_call | solution.py:419
  29.9 1.4 %shard_map.59 = (f32[2056,128]{1,0:T(8,128)S(1)}, f32[512,128]{1,0:T(8,128)S(1)}, f32[8,512]{1,0:T(8,128)S(1)}, s32[3,512]{1,0:T(4,128)S(1)}) custom-call(s32[512]{0:T(512)S(1)} %bitcast.17, s32[512]{0:T(512)S(1)} %bitcast.21, f32[2048,128]{1,0:T(8,128)S(1)} %get-tuple-element.62.refs_2_, f32[72,128]{1,0:T(8,128)S(1)} %get-tuple-element.107.refs_3_, ...), custom_call_target="tpu_custom_call" | custom-call | tf_op jit(solution)/shard_map/pallas_call | solution.py:419
  31.4 0.9 %shard_map.60 = (f32[216,128]{1,0:T(8,128)S(1)}, f32[216,128]{1,0:T(8,128)S(1)}, f32[72,128]{1,0:T(8,128)S(1)}, f32[72,128]{1,0:T(8,128)S(1)}) custom-call(f32[512,128]{1,0:T(8,128)S(1)} %get-tuple-element.66.refs_0_, f32[8,512]{1,0:T(8,128)S(1)} %get-tuple-element.67.refs_1_, s32[3,512]{1,0:T(4,128)S(1)} %get-tuple-element.68.refs_2_, ...), custom_call_target="tpu_custom_call" | custom-call | tf_op jit(solution)/shard_map/pallas_call | solution.py:419
  32.3 0.1 collective-permute-start.9
  32.4 2.1 %collective-permute-start.8 = (f16[216,128]{1,0:T(8,128)(2,1)S(1)}, f16[216,128]{1,0:T(8,128)(2,1)S(1)}, u32[]{:S(2)}, u32[]{:S(2)}) collective-permute-start(f16[216,128]{1,0:T(8,128)(2,1)S(1)} %convert_element_type.81), channel_id=1, source_target_pairs={{0,4},{4,8},{8,12},{12,16},{16,20},{20,24},{24,28},{28,0},{1,5},{5... | collective-permute-start | bytes 165896 | tf_op jit(solution)/shard_map/ppermute | solution.py:39
  34.5 2.0 %collective-permute-done.9 = f16[216,128]{1,0:T(8,128)(2,1)S(1)} collective-permute-done((f16[216,128]{1,0:T(8,128)(2,1)S(1)}, f16[216,128]{1,0:T(8,128)(2,1)S(1)}, u32[]{:S(2)}, u32[]{:S(2)}) %collective-permute-start.9) | collective-permute-done | bytes 55328 | tf_op jit(solution)/shard_map/ppermute | solution.py:39
  36.6 2.8 %collective-permute-done.8 = f16[216,128]{1,0:T(8,128)(2,1)S(1)} collective-permute-done((f16[216,128]{1,0:T(8,128)(2,1)S(1)}, f16[216,128]{1,0:T(8,128)(2,1)S(1)}, u32[]{:S(2)}, u32[]{:S(2)}) %collective-permute-start.8) | collective-permute-done | bytes 55328 | tf_op jit(solution)/shard_map/ppermute | solution.py:39
  39.5 1.8 %collective-permute-start.11 = (f16[216,128]{1,0:T(8,128)(2,1)S(1)}, f16[216,128]{1,0:T(8,128)(2,1)S(1)}, u32[]{:S(2)}, u32[]{:S(2)}) collective-permute-start(f16[216,128]{1,0:T(8,128)(2,1)S(1)} %pad_maximum_fusion.5), channel_id=1, source_target_pairs={{0,3},{1,0},{2,1},{3,2},{4,7},{5,4},{6,5},{7,6},{8,11},{9,8},{10,9... | collective-permute-start | bytes 165896 | tf_op jit(solution)/shard_map/ppermute | solution.py:39
  41.3 2.3 %shard_map.61.refs_5_ = f32[2048,128]{1,0:T(8,128)S(1)} custom-call(s32[512]{0:T(512)S(1)} %bitcast.18, f32[216,128]{1,0:T(8,128)S(1)} %convert_element_type.77.refs_7_.refs_1_, f32[216,128]{1,0:T(8,128)S(1)} %convert_element_type.79.refs_8_.refs_2_, s32[3,3,2048]{2,1,0:T(4,128)S(1)} %get-tuple-element.49.refs_0_.refs_3_.refs_2_.refs_1_, ...), custom_call_target="tpu_custom_call" | custom-call | tf_op jit(solution)/shard_map/pallas_call | solution.py:419
  43.6 1.8 %shard_map.62 = (f32[2056,128]{1,0:T(8,128)S(1)}, f32[512,128]{1,0:T(8,128)S(1)}, f32[8,512]{1,0:T(8,128)S(1)}, s32[3,512]{1,0:T(4,128)S(1)}) custom-call(s32[512]{0:T(512)S(1)} %bitcast.19, s32[512]{0:T(512)S(1)} %bitcast.23, s32[3,3,2048]{2,1,0:T(4,128)S(1)} %get-tuple-element.49.refs_0_.refs_3_.refs_2_.refs_1_, ...), custom_call_target="tpu_custom_call" | custom-call | tf_op jit(solution)/shard_map/pallas_call | solution.py:419
  45.5 0.9 %shard_map.64 = (f32[216,128]{1,0:T(8,128)S(1)}, f32[216,128]{1,0:T(8,128)S(1)}, f32[72,128]{1,0:T(8,128)S(1)}, f32[72,128]{1,0:T(8,128)S(1)}) custom-call(f32[512,128]{1,0:T(8,128)S(1)} %get-tuple-element.82.refs_0_, f32[8,512]{1,0:T(8,128)S(1)} %get-tuple-element.83.refs_1_, s32[3,512]{1,0:T(4,128)S(1)} %get-tuple-element.84.refs_2_, ...), custom_call_target="tpu_custom_call" | custom-call | tf_op jit(solution)/shard_map/pallas_call | solution.py:419
  46.6 2.1 %collective-permute-start.12 = (f16[216,128]{1,0:T(8,128)(2,1)S(1)}, f16[216,128]{1,0:T(8,128)(2,1)S(1)}, u32[]{:S(2)}, u32[]{:S(2)}) collective-permute-start(f16[216,128]{1,0:T(8,128)(2,1)S(1)} %convert_element_type.88), channel_id=1, source_target_pairs={{0,4},{4,8},{8,12},{12,16},{16,20},{20,24},{24,28},{28,0},{1,5},{5... | collective-permute-start | bytes 165896 | tf_op jit(solution)/shard_map/ppermute | solution.py:39
  48.6 2.0 %collective-permute-done.13 = f16[216,128]{1,0:T(8,128)(2,1)S(1)} collective-permute-done((f16[216,128]{1,0:T(8,128)(2,1)S(1)}, f16[216,128]{1,0:T(8,128)(2,1)S(1)}, u32[]{:S(2)}, u32[]{:S(2)}) %collective-permute-start.13) | collective-permute-done | bytes 55328 | tf_op jit(solution)/shard_map/ppermute | solution.py:39
  50.7 2.8 %collective-permute-done.12 = f16[216,128]{1,0:T(8,128)(2,1)S(1)} collective-permute-done((f16[216,128]{1,0:T(8,128)(2,1)S(1)}, f16[216,128]{1,0:T(8,128)(2,1)S(1)}, u32[]{:S(2)}, u32[]{:S(2)}) %collective-permute-start.12) | collective-permute-done | bytes 55328 | tf_op jit(solution)/shard_map/ppermute | solution.py:39
  53.6 2.0 %collective-permute-start.15 = (f16[216,128]{1,0:T(8,128)(2,1)S(1)}, f16[216,128]{1,0:T(8,128)(2,1)S(1)}, u32[]{:S(2)}, u32[]{:S(2)}) collective-permute-start(f16[216,128]{1,0:T(8,128)(2,1)S(1)} %pad_maximum_fusion.7), channel_id=1, source_target_pairs={{0,3},{1,0},{2,1},{3,2},{4,7},{5,4},{6,5},{7,6},{8,11},{9,8},{10,9... | collective-permute-start | bytes 165896 | tf_op jit(solution)/shard_map/ppermute | solution.py:39
  55.6 2.0 %shard_map.63.refs_4_ = f32[2048,128]{1,0:T(8,128)S(1)} custom-call(s32[512]{0:T(512)S(1)} %bitcast.20, f32[216,128]{1,0:T(8,128)S(1)} %convert_element_type.83.refs_1_.refs_7_, f32[216,128]{1,0:T(8,128)S(1)} %convert_element_type.85.refs_2_.refs_8_, s32[3,3,2048]{2,1,0:T(4,128)S(1)} %get-tuple-element.49.refs_0_.refs_3_.refs_2_.refs_1_, ...), custom_call_target="tpu_custom_call" | custom-call | tf_op jit(solution)/shard_map/pallas_call | solution.py:419
  57.5 1.6 %shard_map.65.refs_1_ = f32[2056,128]{1,0:T(8,128)S(1)} custom-call(s32[512]{0:T(512)S(1)} %bitcast.14, s32[3,3,2048]{2,1,0:T(4,128)S(1)} %get-tuple-element.49.refs_0_.refs_3_.refs_2_.refs_1_, bf16[384,256]{1,0:T(8,128)(2,1)S(1)} %get-tuple-element.50.refs_4_.refs_3_.refs_2_, bf16[384,160]{1,0:T(8,128)(2,1)S(1)} %get-tuple-element.61.refs_5_.refs_4_.refs_3_, ...), custom_call_target="tpu_custom_call" | custom-call | tf_op jit(solution)/shard_map/pallas_call | solution.py:419
  59.2 0.7 %shard_map.66.refs_1_ = f32[2056,128]{1,0:T(8,128)S(1)} custom-call(s32[512]{0:T(512)S(1)} %bitcast.15, f32[2056,128]{1,0:T(8,128)S(1)} %shard_map.65.refs_1_, f32[216,128]{1,0:T(8,128)S(1)} %convert_element_type.93.refs_2_), custom_call_target="tpu_custom_call" | custom-call | tf_op jit(solution)/shard_map/pallas_call | solution.py:419
  59.9 1.7 %shard_map.67 = f32[2048,128]{1,0:T(8,128)} custom-call(s32[512]{0:T(512)S(1)} %bitcast.16, f32[2056,128]{1,0:T(8,128)S(1)} %shard_map.66.refs_1_, f32[216,128]{1,0:T(8,128)S(1)} %convert_element_type.95.refs_2_), custom_call_target="tpu_custom_call" | custom-call | tf_op jit(solution)/shard_map/pallas_call | solution.py:419
  (49 shorter events, 0.8 us)
Async XLA Ops:
  0.8 8.6 %collective-permute-start.1 = (bf16[3,3,16,128]{3,2,1,0:T(8,128)(2,1)S(1)}, bf16[3,3,16,128]{3,2,1,0:T(8,128)(2,1)S(1)}, u32[]{:S(2)}, u32[]{:S(2)}) collective-permute-start(bf16[3,3,16,128]{3,2,1,0:T(8,128)(2,1)S(1)} %get-tuple-element.91), channel_id=1, source_target_pairs={{0,28},{4,0},{8,4},{12,8},{16,12},{20,16},{24,20},{28,24},{1,29},{... | collective-permute-start | bytes 110600 | tf_op jit(solution)/shard_map/ppermute | solution.py:39
  6.8 6.7 %collective-permute-start = (bf16[3,3,16,128]{3,2,1,0:T(8,128)(2,1)S(1)}, bf16[3,3,16,128]{3,2,1,0:T(8,128)(2,1)S(1)}, u32[]{:S(2)}, u32[]{:S(2)}) collective-permute-start(bf16[3,3,16,128]{3,2,1,0:T(8,128)(2,1)S(1)} %get-tuple-element.92), channel_id=1, source_target_pairs={{0,4},{4,8},{8,12},{12,16},{16,20},{20,24},{24,28},{28,0},{1,5},{5... | collective-permute-start | bytes 110600 | tf_op jit(solution)/shard_map/ppermute | solution.py:39
  13.5 2.0 %collective-permute-start.3 = (bf16[3,3,18,128]{3,2,1,0:T(8,128)(2,1)S(1)}, bf16[3,3,18,128]{3,2,1,0:T(8,128)(2,1)S(1)}, u32[]{:S(2)}, u32[]{:S(2)}) collective-permute-start(bf16[3,3,18,128]{3,2,1,0:T(8,128)(2,1)S(1)} %pad_maximum_fusion.1), channel_id=1, source_target_pairs={{0,3},{1,0},{2,1},{3,2},{4,7},{5,4},{6,5},{7,6},{8,11},{9,8},{10,9... | collective-permute-start | bytes 124424 | tf_op jit(solution)/shard_map/ppermute | solution.py:39
  13.6 4.2 %collective-permute-start.2 = (bf16[3,3,18,128]{3,2,1,0:T(8,128)(2,1)S(1)}, bf16[3,3,18,128]{3,2,1,0:T(8,128)(2,1)S(1)}, u32[]{:S(2)}, u32[]{:S(2)}) collective-permute-start(bf16[3,3,18,128]{3,2,1,0:T(8,128)(2,1)S(1)} %pad_maximum_fusion), channel_id=1, source_target_pairs={{0,1},{1,2},{2,3},{3,0},{4,5},{5,6},{6,7},{7,4},{8,9},{9,10},{10,1... | collective-permute-start | bytes 124424 | tf_op jit(solution)/shard_map/ppermute | solution.py:39
  18.5 4.2 %collective-permute-start.5 = (f16[216,128]{1,0:T(8,128)(2,1)S(1)}, f16[216,128]{1,0:T(8,128)(2,1)S(1)}, u32[]{:S(2)}, u32[]{:S(2)}) collective-permute-start(f16[216,128]{1,0:T(8,128)(2,1)S(1)} %convert_element_type.74), channel_id=1, source_target_pairs={{0,28},{4,0},{8,4},{12,8},{16,12},{20,16},{24,20},{28,24},{1,29},{... | collective-permute-start | bytes 165896 | tf_op jit(solution)/shard_map/ppermute | solution.py:39
  19.3 6.9 %collective-permute-start.4 = (f16[216,128]{1,0:T(8,128)(2,1)S(1)}, f16[216,128]{1,0:T(8,128)(2,1)S(1)}, u32[]{:S(2)}, u32[]{:S(2)}) collective-permute-start(f16[216,128]{1,0:T(8,128)(2,1)S(1)} %convert_element_type.72), channel_id=1, source_target_pairs={{0,4},{4,8},{8,12},{12,16},{16,20},{20,24},{24,28},{28,0},{1,5},{5... | collective-permute-start | bytes 165896 | tf_op jit(solution)/shard_map/ppermute | solution.py:39
  26.2 5.1 %collective-permute-start.6 = (f16[216,128]{1,0:T(8,128)(2,1)S(1)}, f16[216,128]{1,0:T(8,128)(2,1)S(1)}, u32[]{:S(2)}, u32[]{:S(2)}) collective-permute-start(f16[216,128]{1,0:T(8,128)(2,1)S(1)} %pad_maximum_fusion.2), channel_id=1, source_target_pairs={{0,1},{1,2},{2,3},{3,0},{4,5},{5,6},{6,7},{7,4},{8,9},{9,10},{10,1... | collective-permute-start | bytes 165896 | tf_op jit(solution)/shard_map/ppermute | solution.py:39
  26.3 5.0 %collective-permute-start.7 = (f16[216,128]{1,0:T(8,128)(2,1)S(1)}, f16[216,128]{1,0:T(8,128)(2,1)S(1)}, u32[]{:S(2)}, u32[]{:S(2)}) collective-permute-start(f16[216,128]{1,0:T(8,128)(2,1)S(1)} %pad_maximum_fusion.3), channel_id=1, source_target_pairs={{0,3},{1,0},{2,1},{3,2},{4,7},{5,4},{6,5},{7,6},{8,11},{9,8},{10,9... | collective-permute-start | bytes 165896 | tf_op jit(solution)/shard_map/ppermute | solution.py:39
  32.3 4.2 %collective-permute-start.9 = (f16[216,128]{1,0:T(8,128)(2,1)S(1)}, f16[216,128]{1,0:T(8,128)(2,1)S(1)}, u32[]{:S(2)}, u32[]{:S(2)}) collective-permute-start(f16[216,128]{1,0:T(8,128)(2,1)S(1)} %convert_element_type.82), channel_id=1, source_target_pairs={{0,28},{4,0},{8,4},{12,8},{16,12},{20,16},{24,20},{28,24},{1,29},{... | collective-permute-start | bytes 165896 | tf_op jit(solution)/shard_map/ppermute | solution.py:39
  32.4 6.9 %collective-permute-start.8 = (f16[216,128]{1,0:T(8,128)(2,1)S(1)}, f16[216,128]{1,0:T(8,128)(2,1)S(1)}, u32[]{:S(2)}, u32[]{:S(2)}) collective-permute-start(f16[216,128]{1,0:T(8,128)(2,1)S(1)} %convert_element_type.81), channel_id=1, source_target_pairs={{0,4},{4,8},{8,12},{12,16},{16,20},{20,24},{24,28},{28,0},{1,5},{5... | collective-permute-start | bytes 165896 | tf_op jit(solution)/shard_map/ppermute | solution.py:39
  39.4 6.0 %collective-permute-start.10 = (f16[216,128]{1,0:T(8,128)(2,1)S(1)}, f16[216,128]{1,0:T(8,128)(2,1)S(1)}, u32[]{:S(2)}, u32[]{:S(2)}) collective-permute-start(f16[216,128]{1,0:T(8,128)(2,1)S(1)} %pad_maximum_fusion.4), channel_id=1, source_target_pairs={{0,1},{1,2},{2,3},{3,0},{4,5},{5,6},{6,7},{7,4},{8,9},{9,10},{10,1... | collective-permute-start | bytes 165896 | tf_op jit(solution)/shard_map/ppermute | solution.py:39
  39.5 6.0 %collective-permute-start.11 = (f16[216,128]{1,0:T(8,128)(2,1)S(1)}, f16[216,128]{1,0:T(8,128)(2,1)S(1)}, u32[]{:S(2)}, u32[]{:S(2)}) collective-permute-start(f16[216,128]{1,0:T(8,128)(2,1)S(1)} %pad_maximum_fusion.5), channel_id=1, source_target_pairs={{0,3},{1,0},{2,1},{3,2},{4,7},{5,4},{6,5},{7,6},{8,11},{9,8},{10,9... | collective-permute-start | bytes 165896 | tf_op jit(solution)/shard_map/ppermute | solution.py:39
  46.4 4.2 %collective-permute-start.13 = (f16[216,128]{1,0:T(8,128)(2,1)S(1)}, f16[216,128]{1,0:T(8,128)(2,1)S(1)}, u32[]{:S(2)}, u32[]{:S(2)}) collective-permute-start(f16[216,128]{1,0:T(8,128)(2,1)S(1)} %convert_element_type.90), channel_id=1, source_target_pairs={{0,28},{4,0},{8,4},{12,8},{16,12},{20,16},{24,20},{28,24},{1,29},{... | collective-permute-start | bytes 165896 | tf_op jit(solution)/shard_map/ppermute | solution.py:39
  46.6 6.9 %collective-permute-start.12 = (f16[216,128]{1,0:T(8,128)(2,1)S(1)}, f16[216,128]{1,0:T(8,128)(2,1)S(1)}, u32[]{:S(2)}, u32[]{:S(2)}) collective-permute-start(f16[216,128]{1,0:T(8,128)(2,1)S(1)} %convert_element_type.88), channel_id=1, source_target_pairs={{0,4},{4,8},{8,12},{12,16},{16,20},{20,24},{24,28},{28,0},{1,5},{5... | collective-permute-start | bytes 165896 | tf_op jit(solution)/shard_map/ppermute | solution.py:39
  53.5 5.7 %collective-permute-start.14 = (f16[216,128]{1,0:T(8,128)(2,1)S(1)}, f16[216,128]{1,0:T(8,128)(2,1)S(1)}, u32[]{:S(2)}, u32[]{:S(2)}) collective-permute-start(f16[216,128]{1,0:T(8,128)(2,1)S(1)} %pad_maximum_fusion.6), channel_id=1, source_target_pairs={{0,1},{1,2},{2,3},{3,0},{4,5},{5,6},{6,7},{7,4},{8,9},{9,10},{10,1... | collective-permute-start | bytes 165896 | tf_op jit(solution)/shard_map/ppermute | solution.py:39
  53.6 6.3 %collective-permute-start.15 = (f16[216,128]{1,0:T(8,128)(2,1)S(1)}, f16[216,128]{1,0:T(8,128)(2,1)S(1)}, u32[]{:S(2)}, u32[]{:S(2)}) collective-permute-start(f16[216,128]{1,0:T(8,128)(2,1)S(1)} %pad_maximum_fusion.7), channel_id=1, source_target_pairs={{0,3},{1,0},{2,1},{3,2},{4,7},{5,4},{6,5},{7,6},{8,11},{9,8},{10,9... | collective-permute-start | bytes 165896 | tf_op jit(solution)/shard_map/ppermute | solution.py:39
